TPU v7x, 32 devices: a whole 2x2x4 slice. The times are simulated.
32 devices in a mesh: depth: 8 (over y, x, core), rays: 4 (over z).
Axes of the slice: x: 2, y: 2, z: 4, core: 2. Of those that a mesh axis runs over, the one named last changes fastest.
Arguments:
- density: float32 [256, 65536], P('depth', 'rays'), may hold values from 0.0001953125 to 0.815625
- radiance: float32 [3, 256, 65536], P(None, 'depth', 'rays'), may hold values from 0 to 1
- target: float32 [3, 65536], P(None, 'rays'), may hold values from 0 to 1
Outputs:
- grad_density: float32 [256, 65536], P('depth', 'rays')
- loss_mean: float32 [], replicated
All inputs are finite; a program needn't handle non-finite values.
Results may differ from a plain program's by a relative error of at most 0.0003.
Values sent between devices are 32-bit elements; how exact they have to be, the bound alone decides.
No kernel may reach another device: no remote copies, remote signals or barrier semaphores. Data moves between devices by JAX's collectives and lax.ppermute only.
A program may use at most 128 MiB of HBM per device.

v0:
```python
import jax
import jax.numpy as jnp
from jax import lax
from jax.sharding import PartitionSpec as P


def shifted(value, axis, steps):
    count = lax.axis_size(axis)
    initial, last = (max(0, -steps), min(count, count - steps))
    return lax.ppermute(value, axis, [(source, source + steps) for source in range(initial, last)])


def on_device(density, radiance, target):
    ray_count = density.shape[1]
    rim_density, rim_color = shifted((density[:1], radiance[:, :1]), "depth", -1)
    sample_density = 0.5 * (density + jnp.concatenate([density[1:], rim_density], axis=0))
    sample_color = 0.5 * (radiance + jnp.concatenate([radiance[:, 1:], rim_color], axis=1))
    opacity = -jnp.expm1(-sample_density)
    zero_row = jnp.zeros((1, ray_count), jnp.float32)
    running = jnp.cumsum(sample_density, axis=0)
    optical = jnp.concatenate([zero_row, running[:-1]], axis=0)
    slab_depth = running[-1]
    local_transmit = jnp.exp(-optical)
    emitted = (local_transmit * opacity)[None] * sample_color
    color_prefix = jnp.cumsum(emitted, axis=1)
    slab_color = color_prefix[:, -1]
    stacked = jnp.concatenate([slab_depth[None], slab_color], axis=0)[None]
    all_slabs = lax.all_gather(stacked, "depth", axis=0, tiled=True)
    depths = all_slabs[:, 0]
    depth_running = jnp.cumsum(depths, axis=0)
    starts = jnp.concatenate([zero_row, depth_running[:-1]], axis=0)
    weighted = jnp.exp(-starts)[:, None, :] * all_slabs[:, 1:]
    slab_number = jnp.arange(all_slabs.shape[0], dtype=jnp.int32)
    earlier_mask = slab_number < lax.axis_index("depth")
    start_depth = jnp.sum(jnp.where(earlier_mask[:, None], depths, 0.0), axis=0)
    color_before = jnp.sum(jnp.where(earlier_mask[:, None, None], weighted, 0.0), axis=0)
    pixel_color = jnp.sum(weighted, axis=0)
    offset = jnp.exp(-start_depth)
    transmit = offset[None] * local_transmit
    remaining = (
        pixel_color[:, None, :] - color_before[:, None, :] - offset[None, None, :] * color_prefix
    )
    residual_grad = 2.0 * (pixel_color - target)
    transmit_next = transmit * jnp.exp(-sample_density)
    bracket = transmit_next[None] * sample_color - remaining
    sample_grad = jnp.sum(residual_grad[:, None, :] * bracket, axis=0)
    previous = shifted(sample_grad[-1:], "depth", 1)
    grad_density = 0.5 * (sample_grad + jnp.concatenate([previous, sample_grad[:-1]], axis=0))
    error_term = pixel_color - target
    loss_part = jnp.sum(error_term * error_term)
    total_rays = ray_count * lax.axis_size("rays")
    loss_mean = lax.psum(loss_part, "rays") / (3.0 * total_rays)
    return (grad_density, loss_mean)


def solution(mesh):
    in_specs = (P("depth", "rays"), P(None, "depth", "rays"), P(None, "rays"))
    out_specs = (P("depth", "rays"), P())
    return jax.shard_map(
        on_device, mesh=mesh, in_specs=in_specs, out_specs=out_specs, check_vma=False
    )
```

profile of v0, /device:TPU:0, one launch (start us, length us, event | category | flops | bytes accessed | tf_op | source)
XLA Modules:
  0.0 120.2 jit_solution(12348934080758877961)
XLA Ops:
  7.2 1.1 slice.37
  8.3 1.3 %collective-permute-start = (f32[1,16384]{1,0:T(1,128)S(1)}, f32[1,16384]{1,0:T(1,128)S(1)}, u32[]{:S(2)}, u32[]{:S(2)}) collective-permute-start(f32[1,16384]{1,0:T(1,128)S(1)} %slice.37), channel_id=1, source_target_pairs={{4,0},{8,4},{12,8},{16,12},{20,16},{24,20},{28,24},{5,1},{9,5},{13... | collective-permute-start | bytes 196616 | tf_op jit(solution)/shard_map/ppermute | solution.py:10
  9.6 1.5 %slice.40 = f32[3,1,16384]{2,1,0:T(1,128)S(1)} slice(f32[3,32,16384]{2,1,0:T(8,128)} %param.4), slice={[0:3], [0:1], [0:16384]} | slice | bytes 393216 | tf_op jit(solution)/shard_map/slice | solution.py:15
  11.1 1.3 %collective-permute-start.1 = (f32[3,1,16384]{2,1,0:T(1,128)S(1)}, f32[3,1,16384]{2,1,0:T(1,128)S(1)}, u32[]{:S(2)}, u32[]{:S(2)}) collective-permute-start(f32[3,1,16384]{2,1,0:T(1,128)S(1)} %slice.40), channel_id=1, source_target_pairs={{4,0},{8,4},{12,8},{16,12},{20,16},{24,20},{28,24},{5,1},{9,5},{13... | collective-permute-start | bytes 589832 | tf_op jit(solution)/shard_map/ppermute | solution.py:10
  12.4 1.7 %slice.36 = f32[31,16384]{1,0:T(8,128)S(1)} slice(f32[32,16384]{1,0:T(8,128)} %param.3), slice={[1:32], [0:16384]} | slice | bytes 4063232 | tf_op jit(solution)/shard_map/slice | solution.py:16
  14.2 6.2 %slice.39 = f32[3,31,16384]{2,1,0:T(8,128)} slice(f32[3,32,16384]{2,1,0:T(8,128)} %param.4), slice={[0:3], [1:32], [0:16384]} | slice | bytes 12189696 | tf_op jit(solution)/shard_map/slice | solution.py:17
  20.7 3.0 %reduce_window_sum.33 = f32[32,16384]{1,0:T(8,128)} reduce-window(f32[32,16384]{1,0:T(8,128)S(1)} %fusion, f32[]{:T(128)} %constant.12.clone.1), window={size=32x1 pad=31_0x0_0}, to_apply=%region_0.0 | reduce-window | flops 16252928 | bytes 4194308 | tf_op jit(solution)/shard_map/jit(cumsum)/reduce_window_sum | solution.py:20
  23.7 2.8 %multiply_multiply_fusion.1 = f32[32,16384]{1,0:T(8,128)S(1)} fusion(f32[32,16384]{1,0:T(8,128)S(1)} %fusion, f32[31,16384]{1,0:T(8,128)} %bitcast.16), kind=kLoop, calls=%fused_computation.10 | loop fusion | flops 2621440 | bytes 6225920 | tf_op jit(solution)/shard_map/mul | solution.py:24
  26.6 1.1 slice.48
  27.7 6.2 %broadcast_multiply_fusion = f32[3,32,16384]{2,1,0:T(8,128)} fusion(f32[32,16384]{1,0:T(8,128)S(1)} %multiply_multiply_fusion.1, f32[3,32,16384]{2,1,0:T(8,128)} %param.4, f32[3,1,16384]{2,1,0:T(1,128)S(1)} %collective-permute-done.1, f32[3,31,16384]{2,1,0:T(8,128)S(1)} %copy-done), kind=kLoop, calls=%fused_computation.2 | loop fusion | flops 4718592 | bytes 20971520 | tf_op jit(solution)/shard_map/mul | solution.py:24
  33.9 8.7 %reduce_window_sum.34 = f32[3,32,16384]{2,1,0:T(8,128)} reduce-window(f32[3,32,16384]{2,1,0:T(8,128)} %broadcast_multiply_fusion, f32[]{:T(128)} %constant.12.clone.1), window={size=1x32x1 pad=0_0x31_0x0_0}, to_apply=%region_1.2 | reduce-window | flops 48758784 | bytes 12582916 | tf_op jit(solution)/shard_map/jit(cumsum)/reduce_window_sum | solution.py:25
  42.6 1.6 %slice.50 = f32[3,1,16384]{2,1,0:T(1,128)S(1)} slice(f32[3,32,16384]{2,1,0:T(8,128)} %reduce_window_sum.34), slice={[0:3], [31:32], [0:16384]} | slice | bytes 393216 | tf_op jit(solution)/shard_map/slice | solution.py:26
  44.3 0.8 maximum_bitcast_fusion
  45.2 32.5 %all-gather.4.cloned.1.call-done = f32[8,4,16384]{2,1,0:T(4,128)} async-done(((f32[1,4,16384]{2,1,0:T(4,128)}), f32[8,4,16384]{2,1,0:T(4,128)}) %all-gather.4.cloned.1.call-update) | async-done | bytes 2097168 | tf_op jit(solution)/shard_map/all_gather | solution.py:28
  77.7 2.0 %slice.51 = f32[8,1,16384]{2,1,0:T(1,128)S(1)} slice(f32[8,4,16384]{2,1,0:T(4,128)} %all-gather.4.cloned.1.call-done), slice={[0:8], [0:1], [0:16384]} | slice | bytes 1048576 | tf_op jit(solution)/shard_map/slice | solution.py:29
  79.7 1.1 copy.11
  80.8 1.5 %reduce_window_sum.35 = f32[8,16384]{1,0:T(8,128)S(1)} reduce-window(f32[8,16384]{1,0:T(8,128)} %bitcast.19, f32[]{:T(128)} %constant.12.clone.1), window={size=8x1 pad=7_0x0_0}, to_apply=%region_2.3 | reduce-window | flops 917504 | bytes 1048580 | tf_op jit(solution)/shard_map/jit(cumsum)/reduce_window_sum | solution.py:30
  82.9 2.5 %multiply_multiply_fusion = f32[32,16384]{1,0:T(8,128)S(1)} fusion(f32[32,16384]{1,0:T(8,128)S(1)} %fusion, f32[31,16384]{1,0:T(8,128)} %bitcast.17, f32[16384]{0:T(1024)S(1)} %negate_exponential_fusion.2), kind=kLoop, calls=%fused_computation.9 | loop fusion | flops 2621440 | bytes 6291456 | tf_op jit(solution)/shard_map/mul | solution.py:45
  85.4 3.7 %select_reduce_fusion = (f32[3,16384]{1,0:T(4,128)S(1)}, f32[3,16384]{1,0:T(4,128)S(1)}) fusion(f32[8,4,16384]{2,1,0:T(4,128)} %all-gather.4.cloned.1.call-done, f32[8,16384]{1,0:T(8,128)S(1)} %negate_exponential_fusion.1, pred[8]{0:T(512)(128)(4,1)S(1)} %iota_compare_fusion), kind=kLoop, calls=%fused_computation.8 | loop fusion | flops 1474560 | bytes 2490376 | tf_op jit(solution)/shard_map/reduce_sum | solution.py:36
  89.1 1.7 %multiply_reduce_fusion.1 = (f32[]{:T(128)}, f32[3,16384]{1,0:T(4,128)S(1)}, f32[3,16384]{1,0:T(4,128)S(1)}) fusion(f32[3,16384]{1,0:T(4,128)S(1)} %get-tuple-element.3, f32[3,16384]{1,0:T(4,128)} %param.5, f32[3,16384]{1,0:T(4,128)S(1)} %get-tuple-element.2), kind=kLoop, calls=%fused_computation.18 | loop fusion | flops 245759 | bytes 983044 | tf_op jit(solution)/shard_map/reduce_sum | solution.py:50
  90.8 4.5 %multiply_reduce_fusion = f32[32,16384]{1,0:T(8,128)S(1)} fusion(f32[3,32,16384]{2,1,0:T(8,128)S(1)} %copy-done.1, f32[16384]{0:T(1024)S(1)} %negate_exponential_fusion.2, f32[3,16384]{1,0:T(4,128)S(1)} %get-tuple-element.6, f32[32,16384]{1,0:T(8,128)S(1)} %multiply_multiply_fusion, f32[3,16384]{1,0:T(4,128)S(1)} %get-tuple-element.5, ...), kind=kLoop, calls=%fused_computation.1 | loop fusion | flops 12058624 | bytes 23527424 | tf_op jit(solution)/shard_map/reduce_sum | solution.py:46
  95.4 2.1 %collective-permute-start.2 = (f32[1,16384]{1,0:T(1,128)S(1)}, f32[1,16384]{1,0:T(1,128)S(1)}, u32[]{:S(2)}, u32[]{:S(2)}) collective-permute-start(f32[1,16384]{1,0:T(1,128)S(1)} %slice.54), channel_id=1, source_target_pairs={{0,4},{4,8},{8,12},{12,16},{16,20},{20,24},{24,28},{1,5},{5,9},{9,... | collective-permute-start | bytes 196616 | tf_op jit(solution)/shard_map/ppermute | solution.py:10
  97.6 12.3 %psum.7 = f32[]{:T(128)} all-reduce(f32[]{:T(128)} %get-tuple-element.4), channel_id=1, replica_groups=mesh['depth'=8,'rays'=4] {'rays'}, use_global_device_ids=true, to_apply=%region_8.9 | all-reduce | flops 1 | bytes 8 | tf_op jit(solution)/shard_map/psum | solution.py:52
  110.6 1.6 %fusion.1 = f32[32,16384]{1,0:T(8,128)} fusion(f32[32,16384]{1,0:T(8,128)S(1)} %multiply_reduce_fusion, f32[31,16384]{1,0:T(8,128)S(1)} %bitcast.15, f32[1,16384]{1,0:T(1,128)S(1)} %collective-permute-done.2), kind=kLoop, calls=%fused_computation.7 | loop fusion | flops 1572864 | bytes 6291456 | tf_op jit(solution)/shard_map/mul | solution.py:48
  (23 shorter events, 1.1 us)
Async XLA Ops:
  7.2 70.5 %all-gather.4.cloned.1.call-start = ((), (), s32[]{:S(2)}) async-start(), calls=%async_computation | async-start | bytes 2359296 | tf_op jit(solution)/shard_map/all_gather | solution.py:28
  8.3 12.1 %collective-permute-start = (f32[1,16384]{1,0:T(1,128)S(1)}, f32[1,16384]{1,0:T(1,128)S(1)}, u32[]{:S(2)}, u32[]{:S(2)}) collective-permute-start(f32[1,16384]{1,0:T(1,128)S(1)} %slice.37), channel_id=1, source_target_pairs={{4,0},{8,4},{12,8},{16,12},{20,16},{24,20},{28,24},{5,1},{9,5},{13... | collective-permute-start | bytes 196616 | tf_op jit(solution)/shard_map/ppermute | solution.py:10
  11.1 16.6 %collective-permute-start.1 = (f32[3,1,16384]{2,1,0:T(1,128)S(1)}, f32[3,1,16384]{2,1,0:T(1,128)S(1)}, u32[]{:S(2)}, u32[]{:S(2)}) collective-permute-start(f32[3,1,16384]{2,1,0:T(1,128)S(1)} %slice.40), channel_id=1, source_target_pairs={{4,0},{8,4},{12,8},{16,12},{20,16},{24,20},{28,24},{5,1},{9,5},{13... | collective-permute-start | bytes 589832 | tf_op jit(solution)/shard_map/ppermute | solution.py:10
  14.2 6.2 %copy-start.2 = (f32[32,16384]{1,0:T(8,128)S(1)}, f32[32,16384]{1,0:T(8,128)}, u32[]{:S(2)}) copy-start(f32[32,16384]{1,0:T(8,128)} %param.3) | copy-start | bytes 6291460
  23.7 4.0 %copy-start = (f32[3,31,16384]{2,1,0:T(8,128)S(1)}, f32[3,31,16384]{2,1,0:T(8,128)}, u32[]{:S(2)}) copy-start(f32[3,31,16384]{2,1,0:T(8,128)} %slice.39) | copy-start | bytes 18284548
  82.3 8.5 %copy-start.1 = (f32[3,32,16384]{2,1,0:T(8,128)S(1)}, f32[3,32,16384]{2,1,0:T(8,128)}, u32[]{:S(2)}) copy-start(f32[3,32,16384]{2,1,0:T(8,128)} %reduce_window_sum.34) | copy-start | bytes 18874372
  82.4 8.4 %slice-start = ((s8[6291456]{0:T(1024)(128)(4,1)}), s8[4194304]{0:T(1024)(128)(4,1)S(1)}, s32[]{:S(2)}) async-start(s8[6291456]{0:T(1024)(128)(4,1)} %bitcast.13), calls=%async_computation.1 | async-start | bytes 8388608
  82.9 7.9 %slice-start.1 = ((s8[6291456]{0:T(1024)(128)(4,1)}), s8[2097152]{0:T(1024)(128)(4,1)S(1)}, s32[]{:S(2)}) async-start(s8[6291456]{0:T(1024)(128)(4,1)} %bitcast.13), calls=%async_computation.2 | async-start | bytes 4194304
  95.4 15.1 %collective-permute-start.2 = (f32[1,16384]{1,0:T(1,128)S(1)}, f32[1,16384]{1,0:T(1,128)S(1)}, u32[]{:S(2)}, u32[]{:S(2)}) collective-permute-start(f32[1,16384]{1,0:T(1,128)S(1)} %slice.54), channel_id=1, source_target_pairs={{0,4},{4,8},{8,12},{12,16},{16,20},{20,24},{24,28},{1,5},{5,9},{9,... | collective-permute-start | bytes 196616 | tf_op jit(solution)/shard_map/ppermute | solution.py:10
Sparse Core Ops, SparseCore 0:
  45.3 32.3 all-gather.3
where the time goes:
time: 121 us; the launch traced here: 120 us
  other arithmetic  38 us (31%)
  waiting for transfers between devices  32.5 us (27%)
  local copies, waits for them, and re-layouts  16.5 us (14%)
  between operations  16 us (13%)
  blocking collectives  12.3 us (10%)
  starting transfers between devices  4.76 us (4%)
    all_gather x1, waiting for transfers between devices, on_device(): all_slabs = lax.all_gather(stacked, 'depth', axis=0, tiled=True)  32.5 us
    psum x1, blocking collectives, on_device(): loss_mean = lax.psum(loss_part, 'rays') / (3.0 * total_rays)  12.3 us
    mul x2, other arithmetic, on_device(): emitted = (local_transmit * opacity)[None] * sample_color  9.08 us
    another operation x1, other arithmetic, on_device(): color_prefix = jnp.cumsum(emitted, axis=1)  8.66 us
    slice x1, local copies, waits for them, and re-layouts, on_device(): radiance[:, 1:]  6.22 us
    ppermute x3, starting transfers between devices, shifted(): lax.ppermute(value, axis, [(source, source + steps) for source in range(i...  4.73 us
    reduce_sum x1, other arithmetic, on_device(): sample_grad = jnp.sum(residual_grad[:, None, :] * bracket, axis=0)  4.55 us
    reduce_sum x1, other arithmetic, on_device(): jnp.sum(jnp.where(earlier_mask[:, None, None], weighted, 0.0), axis=0)  3.69 us
  transfers between devices with their start and end apart: 4, of which 1 were waited for; matrix products, arithmetic and copies ran while one was open for 14% of the time, Pallas kernels for 0%

commit v1 on v0

v1 whole, which is shorter than its diff:
```python
import jax
import jax.numpy as jnp
from jax import lax
from jax.experimental import pallas as pl
from jax.experimental.pallas import tpu as pltpu
from jax.sharding import PartitionSpec as P


SUB = 8
LANES = 128
BLOCKS = 16

OPACITY = (
    0.49999998698510023,
    -0.12499944339862339,
    0.020829460991082075,
    -0.0025942459011451765,
    0.00024876881447613667,
    -1.5181374461261048e-05,
)


def opacity_of(pair):
    value = OPACITY[-1]
    for factor in OPACITY[-2::-1]:
        value = value * pair + factor
    return value * pair


def edges_kernel(density, radiance, to_core, to_chip, sems):
    tiles = density.shape[0]

    def copies(row_in, row_out):
        first = [density.at[0, :, 0, :]] + [radiance.at[c, 0, :, 0, :] for c in range(3)]
        last = [density.at[tiles - 1, :, SUB - 1, :]]
        last += [radiance.at[c, tiles - 1, :, SUB - 1, :] for c in range(3)]
        made = []
        for at, source in enumerate(first):
            made.append(pltpu.make_async_copy(source, row_in.at[at], sems.at[at]))
        for at, source in enumerate(last):
            made.append(pltpu.make_async_copy(source, row_out.at[at], sems.at[4 + at]))
        return made

    even = lax.rem(lax.axis_index("depth"), 2) == 0

    @pl.when(even)
    def _():
        made = copies(to_chip, to_core)
        for copy in made:
            copy.start()
        for copy in made:
            copy.wait()

    @pl.when(jnp.logical_not(even))
    def _():
        made = copies(to_core, to_chip)
        for copy in made:
            copy.start()
        for copy in made:
            copy.wait()


def slab_kernel(density, radiance, out_h, out_state, out_last):
    tiles, blocks = density.shape[0], density.shape[1]
    samples = tiles * SUB
    rows = density.reshape(tiles * blocks * SUB, LANES)
    colors = radiance.reshape(3 * tiles * blocks * SUB, LANES)

    def cell(ref, plane, i):
        base = (plane * tiles + i // SUB) * blocks * SUB + i % SUB
        return ref[pl.ds(base, blocks, stride=SUB), :]

    here = cell(rows, 0, 0)
    color_here = [cell(colors, c, 0) for c in range(3)]
    transmit = None
    prefix = [None] * 3
    before = [None] * 3
    for i in range(samples - 1):
        after = cell(rows, 0, i + 1)
        opacity = opacity_of(here + after)
        here = after
        if i == 0:
            weight = opacity
            transmit = 1.0 - opacity
        else:
            weight = transmit * opacity
            transmit = transmit - weight
        for c in range(3):
            next_color = cell(colors, c, i + 1)
            color = color_here[c] + next_color
            color_here[c] = next_color
            seen = weight * color
            prefix[c] = seen if i == 0 else prefix[c] + seen
            value = transmit * color + prefix[c]
            out_h[0, c, i] = value if i == 0 else value + before[c]
            before[c] = value
    out_state[0] = transmit
    for c in range(3):
        out_state[1 + c] = prefix[c]
        out_last[c] = before[c]


def boundary_kernel(
    edge_core, edge_chip, rim_core, rim_chip, first, state, last, mine, other, h_first, h_last, full
):
    blocks = state.shape[1]
    half = blocks // 2
    parity = lax.rem(lax.axis_index("depth"), 2)
    even = parity == 0
    step = BLOCKS
    for at in range(0, blocks, step):
        part = pl.ds(at, step)
        density = jnp.where(even, edge_core[0, part], edge_chip[0, part])
        density = density + jnp.where(even, rim_core[0, part], rim_chip[0, part])
        opacity = opacity_of(density)
        transmit = state[0, part]
        weight = transmit * opacity
        transmit = transmit - weight
        full[0, part] = transmit
        for c in range(1, 4):
            own_last = jnp.where(even, edge_core[c, part], edge_chip[c, part])
            own_first = jnp.where(even, edge_chip[c, part], edge_core[c, part])
            behind = jnp.where(even, rim_core[c, part], rim_chip[c, part])
            ahead = jnp.where(even, rim_chip[c, part], rim_core[c, part])
            color = own_last + behind
            prefix = state[c, part] + weight * color
            full[c, part] = prefix
            h_last[c - 1, part] = last[c - 1, part] + transmit * color + prefix
            start = jnp.where(lax.axis_index("depth") == 0, 0.0, own_first + ahead)
            h_first[c - 1, part] = first[0, c - 1, 0, part] + start
    mine[...] = full[:, pl.ds(pl.multiple_of(parity * half, SUB), half), :]
    other[...] = full[:, pl.ds(pl.multiple_of((1 - parity) * half, SUB), half), :]


def grad_kernel(mine, other, h, h_first, h_last, out):
    tiles, blocks = out.shape[0], out.shape[1]
    samples = tiles * SUB
    half = mine.shape[1]
    at = pl.program_id(0) * blocks
    inside = pl.multiple_of(lax.rem(at, half), SUB)
    use_mine = at // half == lax.rem(lax.axis_index("depth"), 2)
    part = pl.ds(inside, blocks)
    a0, a1, a2, base = (jnp.where(use_mine, mine[c, part], other[c, part]) for c in range(4))
    base_first = jnp.where(lax.axis_index("depth") == 0, 0.5 * base, base)
    rows = out.reshape(tiles * blocks * SUB, LANES)
    for i in range(samples):
        if i == 0:
            h0, h1, h2 = h_first[0], h_first[1], h_first[2]
        elif i == samples - 1:
            h0, h1, h2 = h_last[0], h_last[1], h_last[2]
        else:
            h0, h1, h2 = h[0, 0, i], h[0, 1, i], h[0, 2, i]
        value = a0 * h0 + a1 * h1 + a2 * h2 - (base_first if i == 0 else base)
        rows[pl.ds((i // SUB) * blocks * SUB + i % SUB, blocks, stride=SUB), :] = value


def compose(front, back):
    return jnp.concatenate([front[:1] * back[:1], front[1:] + front[:1] * back[1:]], axis=0)


def stages(count):
    while count > 1:
        width = 4 if count % 4 == 0 else 2 if count % 2 == 0 else count
        yield width
        count //= width


def partner(device, stride, width, step):
    digit = device // stride % width
    source = digit ^ step if width & (width - 1) == 0 else (digit + step) % width
    return device + (source - digit) * stride


def on_device(density, radiance, target):
    samples, ray_count = density.shape
    devices = lax.axis_size("depth")
    index = lax.axis_index("depth")
    tiles, blocks = samples // SUB, ray_count // LANES
    half = blocks // 2
    even = index % 2 == 0
    f32 = jnp.float32

    def tiled(value):
        lead = value.shape[:-2]
        value = value.reshape(lead + (tiles, SUB, blocks, LANES))
        return jnp.swapaxes(value, -3, -2)

    density = tiled(density)
    radiance = tiled(radiance)
    swap = [(d, d ^ 1) for d in range(devices)]
    chain = [p for d in range(1, devices - 1, 2) for p in ((d, d + 1), (d + 1, d))]

    edge = jax.ShapeDtypeStruct((4, blocks, LANES), f32)
    whole = pl.BlockSpec(memory_space=pltpu.VMEM)
    anywhere = pl.BlockSpec(memory_space=pl.ANY)
    edge_core, edge_chip = pl.pallas_call(
        edges_kernel,
        out_shape=(edge, edge),
        in_specs=[anywhere, anywhere],
        out_specs=(whole, whole),
        scratch_shapes=[pltpu.SemaphoreType.DMA((8,))],
        name="edges",
    )(density, radiance)
    rim_chip = lax.ppermute(edge_chip, "depth", chain)
    rim_core = lax.ppermute(edge_core, "depth", swap)

    step = min(BLOCKS, half)
    grid = blocks // step
    kept = pltpu.CompilerParams(dimension_semantics=("arbitrary",))
    h, state, last = pl.pallas_call(
        slab_kernel,
        grid=(grid,),
        out_shape=(
            jax.ShapeDtypeStruct((grid, 3, samples - 1, step, LANES), f32),
            edge,
            jax.ShapeDtypeStruct((3, blocks, LANES), f32),
        ),
        in_specs=[
            pl.BlockSpec((tiles, step, SUB, LANES), lambda g: (0, g, 0, 0)),
            pl.BlockSpec((3, tiles, step, SUB, LANES), lambda g: (0, 0, g, 0, 0)),
        ],
        out_specs=(
            pl.BlockSpec((1, 3, samples - 1, step, LANES), lambda g: (g, 0, 0, 0, 0)),
            pl.BlockSpec((4, step, LANES), lambda g: (0, g, 0)),
            pl.BlockSpec((3, step, LANES), lambda g: (0, g, 0)),
        ),
        compiler_params=kept,
        cost_estimate=pl.CostEstimate(flops=40 * samples * ray_count, bytes_accessed=16 * samples * ray_count, transcendentals=0),
        name="slab",
    )(density, radiance)
    first = jnp.swapaxes(h[:, :, 0], 0, 1).reshape(1, 3, 1, blocks, LANES)

    part = jax.ShapeDtypeStruct((4, half, LANES), f32)
    row = jax.ShapeDtypeStruct((3, blocks, LANES), f32)
    mine, other, h_first, h_last = pl.pallas_call(
        boundary_kernel,
        out_shape=(part, part, row, row),
        in_specs=[whole] * 7,
        out_specs=(whole,) * 4,
        scratch_shapes=[pltpu.VMEM((4, blocks, LANES), f32)],
        name="boundary",
    )(edge_core, edge_chip, rim_core, rim_chip, first, state, last)

    theirs = lax.ppermute(other, "depth", swap)
    front = jnp.where(even, mine, theirs)
    back = jnp.where(even, theirs, mine)
    total = compose(front, back)
    before = None
    stride = 2
    for width in stages(devices // 2):
        members = [total] + [
            lax.ppermute(total, "depth", [(partner(d, stride, width, k), d) for d in range(devices)])
            for k in range(1, width)
        ]
        digit = index // stride % width
        ordered = []
        for place in range(width):
            picked = members[0]
            for k in range(1, width):
                source = digit ^ k if width & (width - 1) == 0 else (digit + k) % width
                picked = jnp.where(source == place, members[k], picked)
            ordered.append(picked)
        ahead = jnp.concatenate([jnp.ones_like(total[:1]), jnp.zeros_like(total[1:])], axis=0)
        running = ordered[0]
        for place in range(1, width):
            ahead = jnp.where(digit == place, running, ahead)
            running = compose(running, ordered[place])
        before = ahead if before is None else compose(ahead, before)
        total = running
        stride *= width

    parity = index % 2
    goal = target.reshape(3, 2, half, LANES)
    goal = jnp.where(even, goal[:, 0], goal[:, 1])
    error = 0.5 * total[1:] - goal
    loss = jnp.sum(error * error, axis=0)
    loss = jnp.sum(loss.reshape(half // SUB, SUB, LANES), axis=0)

    def scales(ahead):
        gain = 0.5 * ahead[:1] * error
        base = jnp.sum(error * (total[1:] - ahead[1:]), axis=0, keepdims=True)
        return jnp.concatenate([gain, base], axis=0)

    of_front = scales(before)
    of_back = scales(compose(before, front))
    scale_mine = jnp.where(even, of_front, of_back)
    scale_other = jnp.where(even, of_back, of_front)
    message = jnp.concatenate([scale_other.reshape(4 * half, LANES), loss], axis=0)
    received = lax.ppermute(message, "depth", swap)
    scale_theirs = received[: 4 * half].reshape(4, half, LANES)
    loss = loss + received[4 * half :]

    groups = lax.axis_size("rays")
    parts = [
        lax.ppermute(loss, "rays", [(d, (d + k) % groups) for d in range(groups)])
        for k in range(1, groups)
    ]

    grad = pl.pallas_call(
        grad_kernel,
        grid=(grid,),
        out_shape=jax.ShapeDtypeStruct((tiles, blocks, SUB, LANES), f32),
        in_specs=[
            pl.BlockSpec((4, half, LANES), lambda g: (0, 0, 0)),
            pl.BlockSpec((4, half, LANES), lambda g: (0, 0, 0)),
            pl.BlockSpec((1, 3, samples - 1, step, LANES), lambda g: (g, 0, 0, 0, 0)),
            pl.BlockSpec((3, step, LANES), lambda g: (0, g, 0)),
            pl.BlockSpec((3, step, LANES), lambda g: (0, g, 0)),
        ],
        out_specs=pl.BlockSpec((tiles, step, SUB, LANES), lambda g: (0, g, 0, 0)),
        compiler_params=kept,
        cost_estimate=pl.CostEstimate(flops=8 * samples * ray_count, bytes_accessed=16 * samples * ray_count, transcendentals=0),
        name="grad",
    )(scale_mine, scale_theirs, h, h_first, h_last)
    grad = jnp.swapaxes(grad, 1, 2).reshape(samples, ray_count)
    squares = loss
    for value in parts:
        squares = squares + value
    loss_mean = jnp.sum(squares) / (3.0 * ray_count * groups)
    return grad, loss_mean


def solution(mesh):
    in_specs = (P("depth", "rays"), P(None, "depth", "rays"), P(None, "rays"))
    out_specs = (P("depth", "rays"), P())
    return jax.shard_map(
        on_device, mesh=mesh, in_specs=in_specs, out_specs=out_specs, check_vma=False
    )
```

time: 121 us -> 52.1 us (0.43)
  other arithmetic: 38 us -> 2.5 us
  waiting for transfers between devices: 32.5 us -> 8.65 us
  Pallas kernels: 0 us -> 20.3 us
  between operations: 16 us -> 2.55 us
  local copies, waits for them, and re-layouts: 16.5 us -> 3.12 us
  blocking collectives: 12.3 us -> 0 us
  starting transfers between devices: 4.76 us -> 14.4 us
    all_gather x1 -> x0, waiting for transfers between devices: 32.5 us -> none  [on_device(): all_slabs = lax.all_gather(stacked, 'depth', axis=0, tiled=True)]
    pallas_call x0 -> x4, Pallas kernels: none -> 20.3 us  [the longest x1 9.31 us: on_device(): pl.pallas_call(slab_kernel, grid=(grid,), out_shape=(jax.ShapeDtypeStruct...]
    slice x8 -> x1, local copies, waits for them, and re-layouts: 15.2 us -> 0.66 us  [on_device(): scale_theirs = received[:4 * half].reshape(4, half, LANES)]
    mul x5 -> x4, other arithmetic: 13.5 us -> 0.1 us  [the longest x2 0.08 us: scales(): gain = 0.5 * ahead[:1] * error]
    another operation x3 -> x0, other arithmetic: 13.2 us -> none  [the longest x1 8.66 us: on_device(): color_prefix = jnp.cumsum(emitted, axis=1)]
    psum x1 -> x0, blocking collectives: 12.3 us -> none  [on_device(): loss_mean = lax.psum(loss_part, 'rays') / (3.0 * total_rays)]
    reduce_sum x4 -> x3, other arithmetic: 10.4 us -> 0.66 us  [the longest x1 0.6 us: on_device(): loss_mean = jnp.sum(squares) / (3.0 * ray_count * groups)]
    ppermute x3 -> x10, starting transfers between devices: 4.73 us -> 14.4 us  [the longest x3 5.51 us: on_device(): lax.ppermute(loss, 'rays', [(d, (d + k) % groups) for d in range(groups)])]
  transfers between devices with their start and end apart: 4 -> 10, of which waited for: 1 -> 5; matrix products, arithmetic and copies ran while one was open for 14% -> 4% of each run, Pallas kernels for 0% -> 31%
where the time goes in v1:
time: 52.1 us; the launch traced here: 51.5 us
  Pallas kernels  20.3 us (39%)
  starting transfers between devices  14.4 us (28%)
  waiting for transfers between devices  8.65 us (17%)
  local copies, waits for them, and re-layouts  3.12 us (6%)
  between operations  2.55 us (5%)
  other arithmetic  2.5 us (5%)
    pallas_call x1, Pallas kernels, on_device(): pl.pallas_call(slab_kernel, grid=(grid,), out_shape=(jax.ShapeDtypeStruct...  9.31 us
    pallas_call x1, Pallas kernels, on_device(): pl.pallas_call(grad_kernel, grid=(grid,), out_shape=jax.ShapeDtypeStruct(...  6.76 us
    ppermute x3, waiting for transfers between devices, on_device(): lax.ppermute(total, 'depth', [(partner(d, stride, width, k), d) for d in...  6.1 us
    ppermute x3, starting transfers between devices, on_device(): lax.ppermute(loss, 'rays', [(d, (d + k) % groups) for d in range(groups)])  5.51 us
    ppermute x1, starting transfers between devices, on_device(): theirs = lax.ppermute(other, 'depth', swap)  3.85 us
    ppermute x3, starting transfers between devices, on_device(): lax.ppermute(total, 'depth', [(partner(d, stride, width, k), d) for d in...  3.55 us
    pallas_call x1, Pallas kernels, on_device(): pl.pallas_call(boundary_kernel, out_shape=(part, part, row, row), in_spec...  2.34 us
    pallas_call x1, Pallas kernels, on_device(): pl.pallas_call(edges_kernel, out_shape=(edge, edge), in_specs=[anywhere,...  1.94 us
  transfers between devices with their start and end apart: 10, of which 5 were waited for; matrix products, arithmetic and copies ran while one was open for 4% of the time, Pallas kernels for 31%

profile of v1, /device:TPU:0, one launch (start us, length us, event | category | flops | bytes accessed | tf_op | source)
XLA Modules:
  0.0 51.5 jit_solution(3732962586190719924)
XLA Ops:
  0.6 1.9 %edges.1 = (f32[4,128,128]{2,1,0:T(8,128)}, f32[4,128,128]{2,1,0:T(8,128)}) custom-call(f32[4,128,8,128]{3,2,1,0:T(8,128)} %bitcast.56, f32[3,4,128,8,128]{4,3,2,1,0:T(8,128)} %bitcast.54), custom_call_target="tpu_custom_call" | custom-call | tf_op jit(solution)/shard_map/edges/pallas_call | solution.py:196
  2.6 0.6 %collective-permute-start = (f32[4,128,128]{2,1,0:T(8,128)}, f32[4,128,128]{2,1,0:T(8,128)S(1)}, u32[]{:S(2)}, u32[]{:S(2)}) collective-permute-start(f32[4,128,128]{2,1,0:T(8,128)} %get-tuple-element.11.edge_core), channel_id=1, source_target_pairs={{0,4},{4,0},{8,12},{12,8},{16,20},{20,16},{24,28},{28,24},{1,5},{5... | collective-permute-start | bytes 786440 | tf_op jit(solution)/shard_map/ppermute | solution.py:205
  3.1 0.8 %collective-permute-start.1 = (f32[4,128,128]{2,1,0:T(8,128)}, f32[4,128,128]{2,1,0:T(8,128)S(1)}, u32[]{:S(2)}, u32[]{:S(2)}) collective-permute-start(f32[4,128,128]{2,1,0:T(8,128)} %get-tuple-element.12.edge_chip), channel_id=1, source_target_pairs={{4,8},{8,4},{12,16},{16,12},{20,24},{24,20},{5,9},{9,5},{13,17},{1... | collective-permute-start | bytes 786440 | tf_op jit(solution)/shard_map/ppermute | solution.py:204
  4.0 9.3 %slab.1 = (f32[8,3,31,16,128]{4,3,2,1,0:T(8,128)}, f32[4,128,128]{2,1,0:T(8,128)}, f32[3,128,128]{2,1,0:T(8,128)}) custom-call(f32[4,128,8,128]{3,2,1,0:T(8,128)} %bitcast.57, f32[3,4,128,8,128]{4,3,2,1,0:T(8,128)} %bitcast.55), custom_call_target="tpu_custom_call" | custom-call | flops 20971520 | bytes 8388608 | tf_op jit(solution)/shard_map/slab/pallas_call | solution.py:210
  13.3 0.9 %slice_bitcast_fusion = f32[3,8,16,128]{3,2,0,1:T(8,128)S(1)} fusion(f32[8,3,31,16,128]{4,3,2,1,0:T(8,128)} %get-tuple-element.13.h), kind=kLoop, calls=%fused_computation | loop fusion | bytes 393216 | tf_op jit(solution)/shard_map/transpose | solution.py:231
  14.2 0.7 %copy.9 = f32[3,8,16,128]{3,2,1,0:T(8,128)} copy(f32[3,8,16,128]{3,2,0,1:T(8,128)S(1)} %slice_bitcast_fusion) | data formatting | bytes 393216 | tf_op jit(solution)/shard_map/transpose | solution.py:231
  14.9 0.7 %copy-done.1 = f32[4,128,128]{2,1,0:T(8,128)} copy-done((f32[4,128,128]{2,1,0:T(8,128)}, f32[4,128,128]{2,1,0:T(8,128)S(1)}, u32[]{:S(2)}) %copy-start.1) | copy-done | bytes 262168
  15.7 2.3 %boundary.1 = (f32[4,64,128]{2,1,0:T(8,128)}, f32[4,64,128]{2,1,0:T(8,128)}, f32[3,128,128]{2,1,0:T(8,128)}, f32[3,128,128]{2,1,0:T(8,128)}) custom-call(f32[4,128,128]{2,1,0:T(8,128)} %get-tuple-element.11.edge_core, f32[4,128,128]{2,1,0:T(8,128)} %get-tuple-element.12.edge_chip, f32[4,128,128]{2,1,0:T(8,128)} %copy-done.1, f32[4,128,128]{2,1,0:T(8,128)} %copy-done.2, ...), custom_call_target="tpu_custom_call" | custom-call | tf_op jit(solution)/shard_map/boundary/pallas_call | solution.py:235
  18.1 3.8 %collective-permute-start.2 = (f32[4,64,128]{2,1,0:T(8,128)}, f32[4,64,128]{2,1,0:T(8,128)S(1)}, u32[]{:S(2)}, u32[]{:S(2)}) collective-permute-start(f32[4,64,128]{2,1,0:T(8,128)} %get-tuple-element.17), channel_id=1, source_target_pairs={{0,4},{4,0},{8,12},{12,8},{16,20},{20,16},{24,28},{28,24},{1,5},{5... | collective-permute-start | bytes 393224 | tf_op jit(solution)/shard_map/ppermute | solution.py:244
  21.9 1.2 %collective-permute-done.2 = f32[4,64,128]{2,1,0:T(8,128)S(1)} collective-permute-done((f32[4,64,128]{2,1,0:T(8,128)}, f32[4,64,128]{2,1,0:T(8,128)S(1)}, u32[]{:S(2)}, u32[]{:S(2)}) %collective-permute-start.2) | collective-permute-done | bytes 131104 | tf_op jit(solution)/shard_map/ppermute | solution.py:244
  23.1 0.9 %broadcast_select_fusion.1 = (f32[4,64,128]{2,1,0:T(8,128)S(1)}, f32[4,64,128]{2,1,0:T(8,128)S(1)}) fusion(f32[4,64,128]{2,1,0:T(8,128)} %get-tuple-element.16, f32[4,64,128]{2,1,0:T(8,128)S(1)} %collective-permute-done.2, pred[]{:T(512)S(6)} %eq.51), kind=kLoop, calls=%fused_computation.35 | loop fusion | flops 65536 | bytes 524289 | tf_op jit(solution)/shard_map/jit(_where)/select_n | solution.py:245
  24.1 1.9 %collective-permute-start.3 = (f32[4,64,128]{2,1,0:T(8,128)S(1)}, f32[4,64,128]{2,1,0:T(8,128)S(1)}, u32[]{:S(2)}, u32[]{:S(2)}) collective-permute-start(f32[4,64,128]{2,1,0:T(8,128)S(1)} %pad_maximum_fusion), channel_id=1, source_target_pairs={{24,0},{28,4},{16,8},{20,12},{8,16},{12,20},{0,24},{4,28},{25,1},{... | collective-permute-start | bytes 393224 | tf_op jit(solution)/shard_map/ppermute | solution.py:252
  26.0 1.1 %collective-permute-start.4 = (f32[4,64,128]{2,1,0:T(8,128)S(1)}, f32[4,64,128]{2,1,0:T(8,128)S(1)}, u32[]{:S(2)}, u32[]{:S(2)}) collective-permute-start(f32[4,64,128]{2,1,0:T(8,128)S(1)} %pad_maximum_fusion), channel_id=1, source_target_pairs={{16,0},{20,4},{24,8},{28,12},{0,16},{4,20},{8,24},{12,28},{17,1},{... | collective-permute-start | bytes 393224 | tf_op jit(solution)/shard_map/ppermute | solution.py:252
  27.1 0.5 %collective-permute-start.5 = (f32[4,64,128]{2,1,0:T(8,128)S(1)}, f32[4,64,128]{2,1,0:T(8,128)S(1)}, u32[]{:S(2)}, u32[]{:S(2)}) collective-permute-start(f32[4,64,128]{2,1,0:T(8,128)S(1)} %pad_maximum_fusion), channel_id=1, source_target_pairs={{8,0},{12,4},{0,8},{4,12},{24,16},{28,20},{16,24},{20,28},{9,1},{1... | collective-permute-start | bytes 393224 | tf_op jit(solution)/shard_map/ppermute | solution.py:252
  27.7 3.8 %collective-permute-done.3 = f32[4,64,128]{2,1,0:T(8,128)S(1)} collective-permute-done((f32[4,64,128]{2,1,0:T(8,128)S(1)}, f32[4,64,128]{2,1,0:T(8,128)S(1)}, u32[]{:S(2)}, u32[]{:S(2)}) %collective-permute-start.3) | collective-permute-done | bytes 131104 | tf_op jit(solution)/shard_map/ppermute | solution.py:252
  31.5 2.2 %collective-permute-done.4 = f32[4,64,128]{2,1,0:T(8,128)S(1)} collective-permute-done((f32[4,64,128]{2,1,0:T(8,128)S(1)}, f32[4,64,128]{2,1,0:T(8,128)S(1)}, u32[]{:S(2)}, u32[]{:S(2)}) %collective-permute-start.4) | collective-permute-done | bytes 131104 | tf_op jit(solution)/shard_map/ppermute | solution.py:252
  34.1 0.7 %fusion = (f32[4,64,128]{2,1,0:T(8,128)S(1)}, f32[4,64,128]{2,1,0:T(8,128)}) fusion(f32[1,64,128]{2,1,0:T(8,128)S(1)} %bitcast.67, f32[3,64,128]{2,1,0:T(8,128)S(1)} %get-tuple-element.43, f32[1,64,128]{2,1,0:T(8,128)S(1)} %bitcast.66, f32[3,64,128]{2,1,0:T(8,128)S(1)} %get-tuple-element.23, pred[]{:T(512)S(6)} %eq.51), kind=kLoop, calls=%fused_computation.12 | loop fusion | flops 131072 | bytes 524289 | tf_op jit(solution)/shard_map/jit(_where)/select_n | solution.py:287
  34.8 1.3 %collective-permute-done.6 = f32[264,128]{1,0:T(8,128)S(1)} collective-permute-done((f32[264,128]{1,0:T(8,128)S(1)}, f32[264,128]{1,0:T(8,128)S(1)}, u32[]{:S(2)}, u32[]{:S(2)}) %collective-permute-start.6) | collective-permute-done | bytes 135200 | tf_op jit(solution)/shard_map/ppermute | solution.py:289
  36.2 1.6 %collective-permute-start.7 = (f32[8,128]{1,0:T(8,128)S(1)}, f32[8,128]{1,0:T(8,128)S(1)}, u32[]{:S(2)}, u32[]{:S(2)}) collective-permute-start(f32[8,128]{1,0:T(8,128)S(1)} %slice_add_fusion), channel_id=1, source_target_pairs={{0,1},{1,2},{2,3},{3,0},{4,5},{5,6},{6,7},{7,4},{8,9},{9,10},{10,1... | collective-permute-start | bytes 12296 | tf_op jit(solution)/shard_map/ppermute | solution.py:295
  37.8 2.6 %collective-permute-start.8 = (f32[8,128]{1,0:T(8,128)S(1)}, f32[8,128]{1,0:T(8,128)S(1)}, u32[]{:S(2)}, u32[]{:S(2)}) collective-permute-start(f32[8,128]{1,0:T(8,128)S(1)} %slice_add_fusion), channel_id=1, source_target_pairs={{0,2},{1,3},{2,0},{3,1},{4,6},{5,7},{6,4},{7,5},{8,10},{9,11},{10,... | collective-permute-start | bytes 12296 | tf_op jit(solution)/shard_map/ppermute | solution.py:295
  40.4 1.3 %collective-permute-start.9 = (f32[8,128]{1,0:T(8,128)S(1)}, f32[8,128]{1,0:T(8,128)S(1)}, u32[]{:S(2)}, u32[]{:S(2)}) collective-permute-start(f32[8,128]{1,0:T(8,128)S(1)} %slice_add_fusion), channel_id=1, source_target_pairs={{0,3},{1,0},{2,1},{3,2},{4,7},{5,4},{6,5},{7,6},{8,11},{9,8},{10,9... | collective-permute-start | bytes 12296 | tf_op jit(solution)/shard_map/ppermute | solution.py:295
  41.7 0.7 %slice.98 = f32[256,128]{1,0:T(8,128)} slice(f32[264,128]{1,0:T(8,128)S(1)} %collective-permute-done.6), slice={[0:256], [0:128]} | slice | bytes 262144 | tf_op jit(solution)/shard_map/slice | solution.py:290
  42.4 6.8 %grad.1 = f32[4,128,8,128]{3,2,1,0:T(8,128)} custom-call(f32[4,64,128]{2,1,0:T(8,128)} %get-tuple-element.34.mine, f32[4,64,128]{2,1,0:T(8,128)} %bitcast.61, f32[8,3,31,16,128]{4,3,2,1,0:T(8,128)} %get-tuple-element.13.h, f32[3,128,128]{2,1,0:T(8,128)} %get-tuple-element.18.h_first, f32[3,128,128]{2,1,0:T(8,128)} %get-tuple-element.19.h_last), custom_call_target="tpu_custom_call" | custom-call | flops 4194304 | bytes 8388608 | tf_op jit(solution)/shard_map/grad/pallas_call | solution.py:299
  49.1 0.6 %add_reduce_fusion = f32[]{:T(128)} fusion(f32[8,128]{1,0:T(8,128)S(1)} %collective-permute-done.9, f32[8,128]{1,0:T(8,128)S(1)} %collective-permute-done.8, f32[8,128]{1,0:T(8,128)S(1)} %slice_add_fusion, f32[8,128]{1,0:T(8,128)S(1)} %collective-permute-done.7), kind=kLoop, calls=%fused_computation.48 | loop fusion | flops 4095 | bytes 16388 | tf_op jit(solution)/shard_map/reduce_sum | solution.py:319
  (28 shorter events, 0.7 us)
Async XLA Ops:
  2.6 12.3 %collective-permute-start = (f32[4,128,128]{2,1,0:T(8,128)}, f32[4,128,128]{2,1,0:T(8,128)S(1)}, u32[]{:S(2)}, u32[]{:S(2)}) collective-permute-start(f32[4,128,128]{2,1,0:T(8,128)} %get-tuple-element.11.edge_core), channel_id=1, source_target_pairs={{0,4},{4,0},{8,12},{12,8},{16,20},{20,16},{24,28},{28,24},{1,5},{5... | collective-permute-start | bytes 786440 | tf_op jit(solution)/shard_map/ppermute | solution.py:205
  3.1 24.5 %copy-start = (f32[3,16384]{1,0:T(4,128)S(1)}, f32[3,16384]{1,0:T(4,128)}, u32[]{:S(2)}) copy-start(f32[3,16384]{1,0:T(4,128)} %param.5) | copy-start | bytes 589828
  3.1 30.7 %copy-start.3 = (f32[4,64,128]{2,1,0:T(8,128)S(1)}, f32[4,64,128]{2,1,0:T(8,128)}, u32[]{:S(2)}) copy-start(f32[4,64,128]{2,1,0:T(8,128)} %constant.49.clone.1) | copy-start | bytes 393220
  3.1 11.8 %collective-permute-start.1 = (f32[4,128,128]{2,1,0:T(8,128)}, f32[4,128,128]{2,1,0:T(8,128)S(1)}, u32[]{:S(2)}, u32[]{:S(2)}) collective-permute-start(f32[4,128,128]{2,1,0:T(8,128)} %get-tuple-element.12.edge_chip), channel_id=1, source_target_pairs={{4,8},{8,4},{12,16},{16,12},{20,24},{24,20},{5,9},{9,5},{13,17},{1... | collective-permute-start | bytes 786440 | tf_op jit(solution)/shard_map/ppermute | solution.py:204
  14.9 0.7 %copy-start.1 = (f32[4,128,128]{2,1,0:T(8,128)}, f32[4,128,128]{2,1,0:T(8,128)S(1)}, u32[]{:S(2)}) copy-start(f32[4,128,128]{2,1,0:T(8,128)S(1)} %collective-permute-done.rim_core) | copy-start | bytes 786436
  14.9 0.8 %copy-start.2 = (f32[4,128,128]{2,1,0:T(8,128)}, f32[4,128,128]{2,1,0:T(8,128)S(1)}, u32[]{:S(2)}) copy-start(f32[4,128,128]{2,1,0:T(8,128)S(1)} %collective-permute-done.1.rim_chip) | copy-start | bytes 786436
  18.1 5.0 %collective-permute-start.2 = (f32[4,64,128]{2,1,0:T(8,128)}, f32[4,64,128]{2,1,0:T(8,128)S(1)}, u32[]{:S(2)}, u32[]{:S(2)}) collective-permute-start(f32[4,64,128]{2,1,0:T(8,128)} %get-tuple-element.17), channel_id=1, source_target_pairs={{0,4},{4,0},{8,12},{12,8},{16,20},{20,16},{24,28},{28,24},{1,5},{5... | collective-permute-start | bytes 393224 | tf_op jit(solution)/shard_map/ppermute | solution.py:244
  24.1 7.4 %collective-permute-start.3 = (f32[4,64,128]{2,1,0:T(8,128)S(1)}, f32[4,64,128]{2,1,0:T(8,128)S(1)}, u32[]{:S(2)}, u32[]{:S(2)}) collective-permute-start(f32[4,64,128]{2,1,0:T(8,128)S(1)} %pad_maximum_fusion), channel_id=1, source_target_pairs={{24,0},{28,4},{16,8},{20,12},{8,16},{12,20},{0,24},{4,28},{25,1},{... | collective-permute-start | bytes 393224 | tf_op jit(solution)/shard_map/ppermute | solution.py:252
  26.0 7.7 %collective-permute-start.4 = (f32[4,64,128]{2,1,0:T(8,128)S(1)}, f32[4,64,128]{2,1,0:T(8,128)S(1)}, u32[]{:S(2)}, u32[]{:S(2)}) collective-permute-start(f32[4,64,128]{2,1,0:T(8,128)S(1)} %pad_maximum_fusion), channel_id=1, source_target_pairs={{16,0},{20,4},{24,8},{28,12},{0,16},{4,20},{8,24},{12,28},{17,1},{... | collective-permute-start | bytes 393224 | tf_op jit(solution)/shard_map/ppermute | solution.py:252
  27.1 6.7 %collective-permute-start.5 = (f32[4,64,128]{2,1,0:T(8,128)S(1)}, f32[4,64,128]{2,1,0:T(8,128)S(1)}, u32[]{:S(2)}, u32[]{:S(2)}) collective-permute-start(f32[4,64,128]{2,1,0:T(8,128)S(1)} %pad_maximum_fusion), channel_id=1, source_target_pairs={{8,0},{12,4},{0,8},{4,12},{24,16},{28,20},{16,24},{20,28},{9,1},{1... | collective-permute-start | bytes 393224 | tf_op jit(solution)/shard_map/ppermute | solution.py:252
  34.8 1.4 %collective-permute-start.6 = (f32[264,128]{1,0:T(8,128)S(1)}, f32[264,128]{1,0:T(8,128)S(1)}, u32[]{:S(2)}, u32[]{:S(2)}) collective-permute-start(f32[264,128]{1,0:T(8,128)S(1)} %pad_maximum_fusion.1), channel_id=1, source_target_pairs={{0,4},{4,0},{8,12},{12,8},{16,20},{20,16},{24,28},{28,24},{1,5},{5... | collective-permute-start | bytes 405512 | tf_op jit(solution)/shard_map/ppermute | solution.py:289
  36.2 12.9 %collective-permute-start.7 = (f32[8,128]{1,0:T(8,128)S(1)}, f32[8,128]{1,0:T(8,128)S(1)}, u32[]{:S(2)}, u32[]{:S(2)}) collective-permute-start(f32[8,128]{1,0:T(8,128)S(1)} %slice_add_fusion), channel_id=1, source_target_pairs={{0,1},{1,2},{2,3},{3,0},{4,5},{5,6},{6,7},{7,4},{8,9},{9,10},{10,1... | collective-permute-start | bytes 12296 | tf_op jit(solution)/shard_map/ppermute | solution.py:295
  37.8 11.4 %collective-permute-start.8 = (f32[8,128]{1,0:T(8,128)S(1)}, f32[8,128]{1,0:T(8,128)S(1)}, u32[]{:S(2)}, u32[]{:S(2)}) collective-permute-start(f32[8,128]{1,0:T(8,128)S(1)} %slice_add_fusion), channel_id=1, source_target_pairs={{0,2},{1,3},{2,0},{3,1},{4,6},{5,7},{6,4},{7,5},{8,10},{9,11},{10,... | collective-permute-start | bytes 12296 | tf_op jit(solution)/shard_map/ppermute | solution.py:295
  40.4 8.8 %collective-permute-start.9 = (f32[8,128]{1,0:T(8,128)S(1)}, f32[8,128]{1,0:T(8,128)S(1)}, u32[]{:S(2)}, u32[]{:S(2)}) collective-permute-start(f32[8,128]{1,0:T(8,128)S(1)} %slice_add_fusion), channel_id=1, source_target_pairs={{0,3},{1,0},{2,1},{3,2},{4,7},{5,4},{6,5},{7,6},{8,11},{9,8},{10,9... | collective-permute-start | bytes 12296 | tf_op jit(solution)/shard_map/ppermute | solution.py:295

commit v2 on v1

v2 whole, which is shorter than its diff:
```python
import functools

import jax
import jax.numpy as jnp
from jax import lax
from jax.experimental import pallas as pl
from jax.experimental.pallas import tpu as pltpu
from jax.sharding import PartitionSpec as P


SUB = 8
LANES = 128
BLOCKS = 16
EDGES = 52 << 20
KEPT = 20 << 20
SMALL = 8 << 20

OPACITY = (
    0.49999998698510023,
    -0.12499944339862339,
    0.020829460991082075,
    -0.0025942459011451765,
    0.00024876881447613667,
    -1.5181374461261048e-05,
)


def opacity_of(pair):
    value = OPACITY[-1]
    for factor in OPACITY[-2::-1]:
        value = value * pair + factor
    return value * pair


def edges_kernel(density, radiance, to_core, to_chip, sems):
    tiles = density.shape[0]

    def copies(row_in, row_out):
        first = [density.at[0, :, 0, :]] + [radiance.at[c, 0, :, 0, :] for c in range(3)]
        last = [density.at[tiles - 1, :, SUB - 1, :]]
        last += [radiance.at[c, tiles - 1, :, SUB - 1, :] for c in range(3)]
        made = []
        for at, source in enumerate(first):
            made.append(pltpu.make_async_copy(source, row_in.at[at], sems.at[at]))
        for at, source in enumerate(last):
            made.append(pltpu.make_async_copy(source, row_out.at[at], sems.at[4 + at]))
        return made

    even = lax.rem(lax.axis_index("depth"), 2) == 0

    @pl.when(even)
    def _():
        made = copies(to_chip, to_core)
        for copy in made:
            copy.start()
        for copy in made:
            copy.wait()

    @pl.when(jnp.logical_not(even))
    def _():
        made = copies(to_core, to_chip)
        for copy in made:
            copy.start()
        for copy in made:
            copy.wait()


def slab_kernel(density, radiance, out_h, out_state, out_first, out_last):
    tiles, blocks = density.shape[0], density.shape[1]
    samples = tiles * SUB
    step = BLOCKS
    rows = density.reshape(tiles * blocks * SUB, LANES)
    planes = radiance.reshape(3 * tiles * blocks * SUB, LANES)

    @pl.loop(0, blocks // step)
    def _(g):
        part = pl.ds(pl.multiple_of(g * step, step), step)

        def cell(ref, plane, i):
            base = (plane * tiles + i // SUB) * blocks * SUB + i % SUB
            base = pl.multiple_of(g * (step * SUB), SUB) + base
            return ref[pl.ds(base, step, stride=SUB), :]

        here = cell(rows, 0, 0)
        color_here = [cell(planes, c, 0) for c in range(3)]
        transmit = None
        prefix = [None] * 3
        before = [None] * 3
        for i in range(samples - 1):
            after = cell(rows, 0, i + 1)
            opacity = opacity_of(here + after)
            here = after
            if i == 0:
                weight = opacity
                transmit = 1.0 - opacity
            else:
                weight = transmit * opacity
                transmit = transmit - weight
            for c in range(3):
                next_color = cell(planes, c, i + 1)
                color = color_here[c] + next_color
                color_here[c] = next_color
                seen = weight * color
                prefix[c] = seen if i == 0 else prefix[c] + seen
                value = transmit * color + prefix[c]
                if i == 0:
                    out_first[c, part] = value
                else:
                    out_h[g, c, i - 1] = value + before[c]
                before[c] = value
        out_state[0, part] = transmit
        for c in range(3):
            out_state[1 + c, part] = prefix[c]
            out_last[c, part] = before[c]


def boundary_kernel(
    edge_core, edge_chip, rim_core, rim_chip, first, state, last, mine, other, h_first, h_last, full
):
    blocks = state.shape[1]
    half = blocks // 2
    parity = lax.rem(lax.axis_index("depth"), 2)
    even = parity == 0
    step = BLOCKS
    for at in range(0, blocks, step):
        part = pl.ds(at, step)
        density = jnp.where(even, edge_core[0, part], edge_chip[0, part])
        density = density + jnp.where(even, rim_core[0, part], rim_chip[0, part])
        opacity = opacity_of(density)
        transmit = state[0, part]
        weight = transmit * opacity
        transmit = transmit - weight
        full[0, part] = transmit
        for c in range(1, 4):
            own_last = jnp.where(even, edge_core[c, part], edge_chip[c, part])
            own_first = jnp.where(even, edge_chip[c, part], edge_core[c, part])
            behind = jnp.where(even, rim_core[c, part], rim_chip[c, part])
            ahead = jnp.where(even, rim_chip[c, part], rim_core[c, part])
            color = own_last + behind
            prefix = state[c, part] + weight * color
            full[c, part] = prefix
            h_last[c - 1, part] = last[c - 1, part] + transmit * color + prefix
            start = jnp.where(lax.axis_index("depth") == 0, 0.0, own_first + ahead)
            h_first[c - 1, part] = first[c - 1, part] + start
    mine[...] = full[:, pl.ds(pl.multiple_of(parity * half, SUB), half), :]
    other[...] = full[:, pl.ds(pl.multiple_of((1 - parity) * half, SUB), half), :]


def grad_kernel(mine, other, h, h_first, h_last, out):
    tiles, blocks = out.shape[0], out.shape[1]
    samples = tiles * SUB
    half = mine.shape[1]
    at = pl.program_id(0) * blocks
    inside = pl.multiple_of(lax.rem(at, half), SUB)
    use_mine = at // half == lax.rem(lax.axis_index("depth"), 2)
    part = pl.ds(inside, blocks)
    outer = pl.ds(pl.multiple_of(at, SUB), blocks)
    a0, a1, a2, base = (jnp.where(use_mine, mine[c, part], other[pl.ds(c * half + inside, blocks), :]) for c in range(4))
    base_first = jnp.where(lax.axis_index("depth") == 0, 0.5 * base, base)
    rows = out.reshape(tiles * blocks * SUB, LANES)
    for i in range(samples):
        if i == 0:
            h0, h1, h2 = (h_first[c, outer] for c in range(3))
        elif i == samples - 1:
            h0, h1, h2 = (h_last[c, outer] for c in range(3))
        else:
            h0, h1, h2 = (h[pl.program_id(0), c, i - 1] for c in range(3))
        value = a0 * h0 + a1 * h1 + a2 * h2 - (base_first if i == 0 else base)
        rows[pl.ds((i // SUB) * blocks * SUB + i % SUB, blocks, stride=SUB), :] = value


def compose(front, back):
    return [front[0] * back[0]] + [front[c] + front[0] * back[c] for c in range(1, 4)]


def chosen(flag, yes, no):
    return [jnp.where(flag, a, b) for a, b in zip(yes, no, strict=True)]


def chip_kernel(mine, theirs, out):
    even = lax.rem(lax.axis_index("depth"), 2) == 0
    for at in range(0, out.shape[1], BLOCKS):
        part = pl.ds(at, BLOCKS)
        own = [mine[c, part] for c in range(4)]
        far = [theirs[c, part] for c in range(4)]
        total = compose(chosen(even, own, far), chosen(even, far, own))
        for c in range(4):
            out[c, part] = total[c]


def gathered(members, earlier, part, stride):
    width = len(members)
    digit = lax.rem(lax.div(lax.axis_index("depth"), stride), width)
    values = [[member[c, part] for c in range(4)] for member in members]
    ordered = []
    for place in range(width):
        picked = values[0]
        for k in range(1, width):
            source = digit ^ k if width & (width - 1) == 0 else lax.rem(digit + k, width)
            picked = chosen(source == place, values[k], picked)
        ordered.append(picked)
    one = jnp.ones_like(values[0][0])
    ahead = [one] + [jnp.zeros_like(one)] * 3
    total = ordered[0]
    for place in range(1, width):
        ahead = chosen(digit == place, total, ahead)
        total = compose(total, ordered[place])
    if earlier is not None:
        ahead = compose(ahead, [earlier[c, part] for c in range(4)])
    return ahead, total


def stage_kernel(stride, width, started, *refs):
    members = refs[:width]
    earlier = refs[width] if started else None
    out_ahead, out_total = refs[-2:]
    for at in range(0, out_total.shape[1], BLOCKS):
        part = pl.ds(at, BLOCKS)
        ahead, total = gathered(members, earlier, part, stride)
        for c in range(4):
            out_ahead[c, part] = ahead[c]
            out_total[c, part] = total[c]


def scale_kernel(stride, width, started, mine, theirs, target, *refs):
    members = refs[:width]
    earlier = refs[width] if started else None
    out_mine, out_message, out_loss = refs[-3:]
    half = out_mine.shape[1]
    parity = lax.rem(lax.axis_index("depth"), 2)
    even = parity == 0
    loss = None
    for at in range(0, half, BLOCKS):
        part = pl.ds(at, BLOCKS)
        before, total = gathered(members, earlier, part, stride)
        own = [mine[c, part] for c in range(4)]
        far = [theirs[c, part] for c in range(4)]
        behind = compose(before, chosen(even, own, far))
        goal = pl.ds(pl.multiple_of(parity * half + at, SUB), BLOCKS)
        error = [0.5 * total[c] - target[c - 1, goal] for c in range(1, 4)]
        squares = error[0] * error[0] + error[1] * error[1] + error[2] * error[2]
        loss = squares if loss is None else loss + squares
        for ahead, is_own in ((before, even), (behind, jnp.logical_not(even))):
            gain = 0.5 * ahead[0]
            values = [gain * error[c] for c in range(3)]
            base = error[0] * (total[1] - ahead[1])
            for c in (1, 2):
                base = base + error[c] * (total[1 + c] - ahead[1 + c])
            values.append(base)

            @pl.when(is_own)
            def _():
                for c in range(4):
                    out_mine[c, part] = values[c]

            @pl.when(jnp.logical_not(is_own))
            def _():
                for c in range(4):
                    out_message[pl.ds(c * half + at, BLOCKS), :] = values[c]

    folded = sum(loss[at : at + SUB] for at in range(0, BLOCKS, SUB))
    folded = jnp.full((SUB, LANES), jnp.sum(folded), jnp.float32)
    out_message[pl.ds(4 * half, SUB), :] = folded
    out_loss[...] = folded


def stages(count):
    while count > 1:
        width = 4 if count % 4 == 0 else 2 if count % 2 == 0 else count
        yield width
        count //= width


def partner(device, stride, width, step):
    digit = device // stride % width
    source = digit ^ step if width & (width - 1) == 0 else (digit + step) % width
    return device + (source - digit) * stride


def on_device(density, radiance, target):
    samples, ray_count = density.shape
    devices = lax.axis_size("depth")
    tiles, blocks = samples // SUB, ray_count // LANES
    half = blocks // 2
    f32 = jnp.float32

    def tiled(value):
        lead = value.shape[:-2]
        value = value.reshape(lead + (tiles, SUB, blocks, LANES))
        return jnp.swapaxes(value, -3, -2)

    density = tiled(density)
    radiance = tiled(radiance)
    swap = [(d, d ^ 1) for d in range(devices)]
    chain = [p for d in range(1, devices - 1, 2) for p in ((d, d + 1), (d + 1, d))]

    edge = jax.ShapeDtypeStruct((4, blocks, LANES), f32)
    row = jax.ShapeDtypeStruct((3, blocks, LANES), f32)
    whole = pl.BlockSpec(memory_space=pltpu.VMEM)
    stays = pl.BlockSpec(memory_space=pltpu.HBM)
    edge_core, edge_chip = pl.pallas_call(
        edges_kernel,
        out_shape=(edge, edge),
        in_specs=[stays, stays],
        out_specs=(whole, whole),
        scratch_shapes=[pltpu.SemaphoreType.DMA((8,))],
        compiler_params=pltpu.CompilerParams(vmem_limit_bytes=EDGES),
        name="edges",
    )(density, radiance)
    rim_chip = lax.ppermute(edge_chip, "depth", chain)
    rim_core = lax.ppermute(edge_core, "depth", swap)

    step = BLOCKS
    grid = blocks // step
    h, state, first, last = pl.pallas_call(
        slab_kernel,
        out_shape=(
            jax.ShapeDtypeStruct((grid, 3, samples - 2, step, LANES), f32),
            edge,
            row,
            row,
        ),
        in_specs=[whole, whole],
        out_specs=(whole,) * 4,
        compiler_params=pltpu.CompilerParams(vmem_limit_bytes=KEPT),
        cost_estimate=pl.CostEstimate(
            flops=40 * samples * ray_count,
            bytes_accessed=16 * samples * ray_count,
            transcendentals=0,
        ),
        name="slab",
    )(density, radiance)

    part = jax.ShapeDtypeStruct((4, half, LANES), f32)
    mine, other, h_first, h_last = pl.pallas_call(
        boundary_kernel,
        out_shape=(part, part, row, row),
        in_specs=[whole] * 7,
        out_specs=(whole,) * 4,
        scratch_shapes=[pltpu.VMEM((4, blocks, LANES), f32)],
        compiler_params=pltpu.CompilerParams(vmem_limit_bytes=KEPT),
        name="boundary",
    )(edge_core, edge_chip, rim_core, rim_chip, first, state, last)

    small = pltpu.CompilerParams(vmem_limit_bytes=SMALL)
    theirs = lax.ppermute(other, "depth", swap)
    total = pl.pallas_call(
        chip_kernel,
        out_shape=part,
        in_specs=[whole, whole],
        out_specs=whole,
        compiler_params=small,
        name="chip",
    )(mine, theirs)
    goal = target.reshape(3, blocks, LANES)
    earlier = ()
    stride = 2
    widths = list(stages(devices // 2)) or [1]
    for at, width in enumerate(widths):
        members = [total] + [
            lax.ppermute(total, "depth", [(partner(d, stride, width, k), d) for d in range(devices)])
            for k in range(1, width)
        ]
        last_stage = at == len(widths) - 1
        if last_stage:
            body = functools.partial(scale_kernel, stride, width, bool(earlier))
            given = (mine, theirs, goal, *members, *earlier)
            made = (
                part,
                jax.ShapeDtypeStruct((4 * half + SUB, LANES), f32),
                jax.ShapeDtypeStruct((SUB, LANES), f32),
            )
        else:
            body = functools.partial(stage_kernel, stride, width, bool(earlier))
            given = (*members, *earlier)
            made = (part, part)
        results = pl.pallas_call(
            body,
            out_shape=made,
            in_specs=[whole] * len(given),
            out_specs=(whole,) * len(made),
            compiler_params=small,
            name="scale" if last_stage else "stage",
        )(*given)
        if not last_stage:
            earlier, total = (results[0],), results[1]
        stride *= width
    scale_mine, message, loss = results

    received = lax.ppermute(message, "depth", swap)
    loss = loss + received[4 * half :]

    groups = lax.axis_size("rays")
    parts = [
        lax.ppermute(loss, "rays", [(d, (d + k) % groups) for d in range(groups)])
        for k in range(1, groups)
    ]

    grad = pl.pallas_call(
        grad_kernel,
        grid=(grid,),
        out_shape=jax.ShapeDtypeStruct((tiles, blocks, SUB, LANES), f32),
        in_specs=[
            whole,
            whole,
            whole,
            whole,
            whole,
        ],
        out_specs=pl.BlockSpec((tiles, step, SUB, LANES), lambda g: (0, g, 0, 0)),
        compiler_params=pltpu.CompilerParams(vmem_limit_bytes=KEPT),
        cost_estimate=pl.CostEstimate(
            flops=8 * samples * ray_count,
            bytes_accessed=16 * samples * ray_count,
            transcendentals=0,
        ),
        name="grad",
    )(scale_mine, received, h, h_first, h_last)
    grad = jnp.swapaxes(grad, 1, 2).reshape(samples, ray_count)
    squares = loss
    for value in parts:
        squares = squares + value
    loss_mean = squares[0, 0] / (3.0 * ray_count * groups)
    return grad, loss_mean


def solution(mesh):
    in_specs = (P("depth", "rays"), P(None, "depth", "rays"), P(None, "rays"))
    out_specs = (P("depth", "rays"), P())
    return jax.shard_map(
        on_device, mesh=mesh, in_specs=in_specs, out_specs=out_specs, check_vma=False
    )
```

time: 52.1 us -> 39.1 us (0.75)
  Pallas kernels: 20.3 us -> 7.51 us
  starting transfers between devices: 14.4 us -> 18.3 us
  other arithmetic: 2.5 us -> 0.01 us
  local copies, waits for them, and re-layouts: 3.12 us -> 1.5 us
    pallas_call x2 -> x4, Pallas kernels: 11.2 us -> 4.17 us  [the longest x1 2.54 us: on_device(): pl.pallas_call(slab_kernel, out_shape=(jax.ShapeDtypeStruct((grid, 3, sam...]
    pallas_call x1, Pallas kernels: 6.76 us -> 3.19 us  [on_device(): pl.pallas_call(grad_kernel, grid=(grid,), out_shape=jax.ShapeDtypeStruct(...]
    ppermute x1, starting transfers between devices: 3.85 us -> 6.43 us  [on_device(): theirs = lax.ppermute(other, 'depth', swap)]
    pallas_call x1, Pallas kernels: 2.34 us -> 0.15 us  [on_device(): pl.pallas_call(boundary_kernel, out_shape=(part, part, row, row), in_spec...]
    select_n x4 -> x0, other arithmetic: 1.68 us -> none  [the longest x1 0.92 us: on_device(): front = jnp.where(even, mine, theirs)]
    transpose x2 -> x0, local copies, waits for them, and re-layouts: 1.64 us -> none  [on_device(): first = jnp.swapaxes(h[:, :, 0], 0, 1).reshape(1, 3, 1, blocks, LANES)]
    ppermute x3, starting transfers between devices: 3.55 us -> 4.91 us  [on_device(): lax.ppermute(total, 'depth', [(partner(d, stride, width, k), d) for d in...]
    reduce_sum x3 -> x0, other arithmetic: 0.66 us -> none  [the longest x1 0.6 us: on_device(): loss_mean = jnp.sum(squares) / (3.0 * ray_count * groups)]
  transfers between devices with their start and end apart: 10 -> 10, of which waited for: 5 -> 4; matrix products, arithmetic and copies ran while one was open for 4% -> 0% of each run, Pallas kernels for 31% -> 15%
where the time goes in v2:
time: 39.1 us; the launch traced here: 38.9 us
  starting transfers between devices  18.3 us (47%)
  waiting for transfers between devices  9.07 us (23%)
  Pallas kernels  7.51 us (19%)
  between operations  2.53 us (6%)
  local copies, waits for them, and re-layouts  1.5 us (4%)
    ppermute x3, waiting for transfers between devices, on_device(): lax.ppermute(total, 'depth', [(partner(d, stride, width, k), d) for d in...  6.73 us
    ppermute x1, starting transfers between devices, on_device(): theirs = lax.ppermute(other, 'depth', swap)  6.43 us
    ppermute x3, starting transfers between devices, on_device(): lax.ppermute(loss, 'rays', [(d, (d + k) % groups) for d in range(groups)])  5.51 us
    ppermute x3, starting transfers between devices, on_device(): lax.ppermute(total, 'depth', [(partner(d, stride, width, k), d) for d in...  4.91 us
    pallas_call x1, Pallas kernels, on_device(): pl.pallas_call(grad_kernel, grid=(grid,), out_shape=jax.ShapeDtypeStruct(...  3.19 us
    pallas_call x1, Pallas kernels, on_device(): pl.pallas_call(slab_kernel, out_shape=(jax.ShapeDtypeStruct((grid, 3, sam...  2.54 us
    ppermute x1, waiting for transfers between devices, on_device(): received = lax.ppermute(message, 'depth', swap)  1.34 us
    pallas_call x1, Pallas kernels, on_device(): pl.pallas_call(edges_kernel, out_shape=(edge, edge), in_specs=[stays, sta...  1.29 us
  transfers between devices with their start and end apart: 10, of which 4 were waited for; matrix products, arithmetic and copies ran while one was open for 0% of the time, Pallas kernels for 15%

profile of v2, /device:TPU:0, one launch (start us, length us, event | category | flops | bytes accessed | tf_op | source)
XLA Modules:
  0.0 38.9 jit_solution(13160974486234628551)
XLA Ops:
  0.6 1.3 %edges.1 = (f32[4,128,128]{2,1,0:T(8,128)S(1)}, f32[4,128,128]{2,1,0:T(8,128)S(1)}) custom-call(f32[4,128,8,128]{3,2,1,0:T(8,128)} %bitcast.16, f32[3,4,128,8,128]{4,3,2,1,0:T(8,128)} %bitcast.14), custom_call_target="tpu_custom_call" | custom-call | tf_op jit(solution)/shard_map/edges/pallas_call | solution.py:301
  1.9 0.0 copy-start.2
  2.0 0.6 %collective-permute-start = (f32[4,128,128]{2,1,0:T(8,128)S(1)}, f32[4,128,128]{2,1,0:T(8,128)S(1)}, u32[]{:S(2)}, u32[]{:S(2)}) collective-permute-start(f32[4,128,128]{2,1,0:T(8,128)S(1)} %get-tuple-element.15.edge_core), channel_id=1, source_target_pairs={{0,4},{4,0},{8,12},{12,8},{16,20},{20,16},{24,28},{28,24},{1,5},{5... | collective-permute-start | bytes 786440 | tf_op jit(solution)/shard_map/ppermute | solution.py:311
  2.5 0.8 %collective-permute-start.1 = (f32[4,128,128]{2,1,0:T(8,128)S(1)}, f32[4,128,128]{2,1,0:T(8,128)S(1)}, u32[]{:S(2)}, u32[]{:S(2)}) collective-permute-start(f32[4,128,128]{2,1,0:T(8,128)S(1)} %get-tuple-element.16.edge_chip), channel_id=1, source_target_pairs={{4,8},{8,4},{12,16},{16,12},{20,24},{24,20},{5,9},{9,5},{13,17},{1... | collective-permute-start | bytes 786440 | tf_op jit(solution)/shard_map/ppermute | solution.py:310
  3.3 1.0 %copy-done = f32[3,32,16384]{2,1,0:T(8,128)S(1)} copy-done((f32[3,32,16384]{2,1,0:T(8,128)S(1)}, f32[3,32,16384]{2,1,0:T(8,128)}, u32[]{:S(2)}) %copy-start) | copy-done | bytes 6291480
  4.3 2.5 %slab.1 = (f32[8,3,30,16,128]{4,3,2,1,0:T(8,128)S(1)}, f32[4,128,128]{2,1,0:T(8,128)S(1)}, f32[3,128,128]{2,1,0:T(8,128)S(1)}, f32[3,128,128]{2,1,0:T(8,128)S(1)}) custom-call(f32[4,128,8,128]{3,2,1,0:T(8,128)S(1)} %bitcast.17, f32[3,4,128,8,128]{4,3,2,1,0:T(8,128)S(1)} %bitcast.15), custom_call_target="tpu_custom_call" | custom-call | flops 20971520 | bytes 8388608 | tf_op jit(solution)/shard_map/slab/pallas_call | solution.py:315
  6.9 0.0 collective-permute-done.1.rim_chip
  6.9 0.2 boundary.1
  7.0 6.4 %collective-permute-start.2 = (f32[4,64,128]{2,1,0:T(8,128)S(1)}, f32[4,64,128]{2,1,0:T(8,128)S(1)}, u32[]{:S(2)}, u32[]{:S(2)}) collective-permute-start(f32[4,64,128]{2,1,0:T(8,128)S(1)} %get-tuple-element.21), channel_id=1, source_target_pairs={{0,4},{4,0},{8,12},{12,8},{16,20},{20,16},{24,28},{28,24},{1,5},{5... | collective-permute-start | bytes 393224 | tf_op jit(solution)/shard_map/ppermute | solution.py:346
  13.5 1.0 %collective-permute-done.2.theirs = f32[4,64,128]{2,1,0:T(8,128)S(1)} collective-permute-done((f32[4,64,128]{2,1,0:T(8,128)S(1)}, f32[4,64,128]{2,1,0:T(8,128)S(1)}, u32[]{:S(2)}, u32[]{:S(2)}) %collective-permute-start.2) | collective-permute-done | bytes 131104 | tf_op jit(solution)/shard_map/ppermute | solution.py:346
  14.5 3.4 %collective-permute-start.3 = (f32[4,64,128]{2,1,0:T(8,128)S(1)}, f32[4,64,128]{2,1,0:T(8,128)S(1)}, u32[]{:S(2)}, u32[]{:S(2)}) collective-permute-start(f32[4,64,128]{2,1,0:T(8,128)S(1)} %chip.1.refs_0_), channel_id=1, source_target_pairs={{8,0},{12,4},{0,8},{4,12},{24,16},{28,20},{16,24},{20,28},{9,1},{1... | collective-permute-start | bytes 393224 | tf_op jit(solution)/shard_map/ppermute | solution.py:361
  17.8 0.6 %collective-permute-start.4 = (f32[4,64,128]{2,1,0:T(8,128)S(1)}, f32[4,64,128]{2,1,0:T(8,128)S(1)}, u32[]{:S(2)}, u32[]{:S(2)}) collective-permute-start(f32[4,64,128]{2,1,0:T(8,128)S(1)} %chip.1.refs_0_), channel_id=1, source_target_pairs={{16,0},{20,4},{24,8},{28,12},{0,16},{4,20},{8,24},{12,28},{17,1},{... | collective-permute-start | bytes 393224 | tf_op jit(solution)/shard_map/ppermute | solution.py:361
  18.5 0.9 %collective-permute-start.5 = (f32[4,64,128]{2,1,0:T(8,128)S(1)}, f32[4,64,128]{2,1,0:T(8,128)S(1)}, u32[]{:S(2)}, u32[]{:S(2)}) collective-permute-start(f32[4,64,128]{2,1,0:T(8,128)S(1)} %chip.1.refs_0_), channel_id=1, source_target_pairs={{24,0},{28,4},{16,8},{20,12},{8,16},{12,20},{0,24},{4,28},{25,1},{... | collective-permute-start | bytes 393224 | tf_op jit(solution)/shard_map/ppermute | solution.py:361
  19.4 2.6 %collective-permute-done.3.refs_1_ = f32[4,64,128]{2,1,0:T(8,128)S(1)} collective-permute-done((f32[4,64,128]{2,1,0:T(8,128)S(1)}, f32[4,64,128]{2,1,0:T(8,128)S(1)}, u32[]{:S(2)}, u32[]{:S(2)}) %collective-permute-start.3) | collective-permute-done | bytes 131104 | tf_op jit(solution)/shard_map/ppermute | solution.py:361
  22.0 4.1 %collective-permute-done.4.refs_2_ = f32[4,64,128]{2,1,0:T(8,128)S(1)} collective-permute-done((f32[4,64,128]{2,1,0:T(8,128)S(1)}, f32[4,64,128]{2,1,0:T(8,128)S(1)}, u32[]{:S(2)}, u32[]{:S(2)}) %collective-permute-start.4) | collective-permute-done | bytes 131104 | tf_op jit(solution)/shard_map/ppermute | solution.py:361
  26.1 0.3 scale.1
  26.5 0.1 collective-permute-start.6
  26.5 1.3 %collective-permute-done.6.other = f32[264,128]{1,0:T(8,128)S(1)} collective-permute-done((f32[264,128]{1,0:T(8,128)S(1)}, f32[264,128]{1,0:T(8,128)S(1)}, u32[]{:S(2)}, u32[]{:S(2)}) %collective-permute-start.6) | collective-permute-done | bytes 135200 | tf_op jit(solution)/shard_map/ppermute | solution.py:390
  27.9 1.6 %collective-permute-start.7 = (f32[8,128]{1,0:T(8,128)S(1)}, f32[8,128]{1,0:T(8,128)S(1)}, u32[]{:S(2)}, u32[]{:S(2)}) collective-permute-start(f32[8,128]{1,0:T(8,128)S(1)} %slice_add_fusion), channel_id=1, source_target_pairs={{0,1},{1,2},{2,3},{3,0},{4,5},{5,6},{6,7},{7,4},{8,9},{9,10},{10,1... | collective-permute-start | bytes 12296 | tf_op jit(solution)/shard_map/ppermute | solution.py:395
  29.5 2.6 %collective-permute-start.8 = (f32[8,128]{1,0:T(8,128)S(1)}, f32[8,128]{1,0:T(8,128)S(1)}, u32[]{:S(2)}, u32[]{:S(2)}) collective-permute-start(f32[8,128]{1,0:T(8,128)S(1)} %slice_add_fusion), channel_id=1, source_target_pairs={{0,2},{1,3},{2,0},{3,1},{4,6},{5,7},{6,4},{7,5},{8,10},{9,11},{10,... | collective-permute-start | bytes 12296 | tf_op jit(solution)/shard_map/ppermute | solution.py:395
  32.1 1.3 %collective-permute-start.9 = (f32[8,128]{1,0:T(8,128)S(1)}, f32[8,128]{1,0:T(8,128)S(1)}, u32[]{:S(2)}, u32[]{:S(2)}) collective-permute-start(f32[8,128]{1,0:T(8,128)S(1)} %slice_add_fusion), channel_id=1, source_target_pairs={{0,3},{1,0},{2,1},{3,2},{4,7},{5,4},{6,5},{7,6},{8,11},{9,8},{10,9... | collective-permute-start | bytes 12296 | tf_op jit(solution)/shard_map/ppermute | solution.py:395
  33.4 3.2 %grad.1 = f32[4,128,8,128]{3,2,1,0:T(8,128)} custom-call(f32[4,64,128]{2,1,0:T(8,128)S(1)} %get-tuple-element.22.mine, f32[264,128]{1,0:T(8,128)S(1)} %collective-permute-done.6.other, f32[8,3,30,16,128]{4,3,2,1,0:T(8,128)S(1)} %get-tuple-element.24.h, f32[3,128,128]{2,1,0:T(8,128)S(1)} %get-tuple-element.25.h_first, f32[3,128,128]{2,1,0:T(8,128)S(1)} %get-tuple-element.26.h_last), custom_call_target="tpu_custom_call" | custom-call | flops 4194304 | bytes 8388608 | tf_op jit(solution)/shard_map/grad/pallas_call | solution.py:399
  36.6 0.0 collective-permute-done.7
  36.6 0.5 %slice.7 = f32[1,1]{1,0:T(1,128)} slice(f32[8,128]{1,0:T(8,128)S(1)} %add_add_fusion), slice={[0:1], [0:1]} | slice | bytes 8 | tf_op jit(solution)/shard_map/slice | solution.py:423
  (12 shorter events, 0.1 us)
Async XLA Ops:
  0.6 2.7 %copy-start.1 = (f32[32,16384]{1,0:T(8,128)S(1)}, f32[32,16384]{1,0:T(8,128)}, u32[]{:S(2)}) copy-start(f32[32,16384]{1,0:T(8,128)} %param.3) | copy-start | bytes 6291460
  0.6 3.7 %copy-start = (f32[3,32,16384]{2,1,0:T(8,128)S(1)}, f32[3,32,16384]{2,1,0:T(8,128)}, u32[]{:S(2)}) copy-start(f32[3,32,16384]{2,1,0:T(8,128)} %param.4) | copy-start | bytes 18874372
  1.9 17.4 %copy-start.2 = (f32[3,16384]{1,0:T(4,128)S(1)}, f32[3,16384]{1,0:T(4,128)}, u32[]{:S(2)}) copy-start(f32[3,16384]{1,0:T(4,128)} %param.5) | copy-start | bytes 589828
  2.0 4.9 %collective-permute-start = (f32[4,128,128]{2,1,0:T(8,128)S(1)}, f32[4,128,128]{2,1,0:T(8,128)S(1)}, u32[]{:S(2)}, u32[]{:S(2)}) collective-permute-start(f32[4,128,128]{2,1,0:T(8,128)S(1)} %get-tuple-element.15.edge_core), channel_id=1, source_target_pairs={{0,4},{4,0},{8,12},{12,8},{16,20},{20,16},{24,28},{28,24},{1,5},{5... | collective-permute-start | bytes 786440 | tf_op jit(solution)/shard_map/ppermute | solution.py:311
  2.5 4.3 %collective-permute-start.1 = (f32[4,128,128]{2,1,0:T(8,128)S(1)}, f32[4,128,128]{2,1,0:T(8,128)S(1)}, u32[]{:S(2)}, u32[]{:S(2)}) collective-permute-start(f32[4,128,128]{2,1,0:T(8,128)S(1)} %get-tuple-element.16.edge_chip), channel_id=1, source_target_pairs={{4,8},{8,4},{12,16},{16,12},{20,24},{24,20},{5,9},{9,5},{13,17},{1... | collective-permute-start | bytes 786440 | tf_op jit(solution)/shard_map/ppermute | solution.py:310
  7.0 7.4 %collective-permute-start.2 = (f32[4,64,128]{2,1,0:T(8,128)S(1)}, f32[4,64,128]{2,1,0:T(8,128)S(1)}, u32[]{:S(2)}, u32[]{:S(2)}) collective-permute-start(f32[4,64,128]{2,1,0:T(8,128)S(1)} %get-tuple-element.21), channel_id=1, source_target_pairs={{0,4},{4,0},{8,12},{12,8},{16,20},{20,16},{24,28},{28,24},{1,5},{5... | collective-permute-start | bytes 393224 | tf_op jit(solution)/shard_map/ppermute | solution.py:346
  14.5 7.6 %collective-permute-start.3 = (f32[4,64,128]{2,1,0:T(8,128)S(1)}, f32[4,64,128]{2,1,0:T(8,128)S(1)}, u32[]{:S(2)}, u32[]{:S(2)}) collective-permute-start(f32[4,64,128]{2,1,0:T(8,128)S(1)} %chip.1.refs_0_), channel_id=1, source_target_pairs={{8,0},{12,4},{0,8},{4,12},{24,16},{28,20},{16,24},{20,28},{9,1},{1... | collective-permute-start | bytes 393224 | tf_op jit(solution)/shard_map/ppermute | solution.py:361
  17.8 8.3 %collective-permute-start.4 = (f32[4,64,128]{2,1,0:T(8,128)S(1)}, f32[4,64,128]{2,1,0:T(8,128)S(1)}, u32[]{:S(2)}, u32[]{:S(2)}) collective-permute-start(f32[4,64,128]{2,1,0:T(8,128)S(1)} %chip.1.refs_0_), channel_id=1, source_target_pairs={{16,0},{20,4},{24,8},{28,12},{0,16},{4,20},{8,24},{12,28},{17,1},{... | collective-permute-start | bytes 393224 | tf_op jit(solution)/shard_map/ppermute | solution.py:361
  18.5 7.7 %collective-permute-start.5 = (f32[4,64,128]{2,1,0:T(8,128)S(1)}, f32[4,64,128]{2,1,0:T(8,128)S(1)}, u32[]{:S(2)}, u32[]{:S(2)}) collective-permute-start(f32[4,64,128]{2,1,0:T(8,128)S(1)} %chip.1.refs_0_), channel_id=1, source_target_pairs={{24,0},{28,4},{16,8},{20,12},{8,16},{12,20},{0,24},{4,28},{25,1},{... | collective-permute-start | bytes 393224 | tf_op jit(solution)/shard_map/ppermute | solution.py:361
  26.5 1.4 %collective-permute-start.6 = (f32[264,128]{1,0:T(8,128)S(1)}, f32[264,128]{1,0:T(8,128)S(1)}, u32[]{:S(2)}, u32[]{:S(2)}) collective-permute-start(f32[264,128]{1,0:T(8,128)S(1)} %get-tuple-element.23), channel_id=1, source_target_pairs={{0,4},{4,0},{8,12},{12,8},{16,20},{20,16},{24,28},{28,24},{1,5},{5... | collective-permute-start | bytes 405512 | tf_op jit(solution)/shard_map/ppermute | solution.py:390
  27.9 8.7 %collective-permute-start.7 = (f32[8,128]{1,0:T(8,128)S(1)}, f32[8,128]{1,0:T(8,128)S(1)}, u32[]{:S(2)}, u32[]{:S(2)}) collective-permute-start(f32[8,128]{1,0:T(8,128)S(1)} %slice_add_fusion), channel_id=1, source_target_pairs={{0,1},{1,2},{2,3},{3,0},{4,5},{5,6},{6,7},{7,4},{8,9},{9,10},{10,1... | collective-permute-start | bytes 12296 | tf_op jit(solution)/shard_map/ppermute | solution.py:395
  29.5 7.1 %collective-permute-start.8 = (f32[8,128]{1,0:T(8,128)S(1)}, f32[8,128]{1,0:T(8,128)S(1)}, u32[]{:S(2)}, u32[]{:S(2)}) collective-permute-start(f32[8,128]{1,0:T(8,128)S(1)} %slice_add_fusion), channel_id=1, source_target_pairs={{0,2},{1,3},{2,0},{3,1},{4,6},{5,7},{6,4},{7,5},{8,10},{9,11},{10,... | collective-permute-start | bytes 12296 | tf_op jit(solution)/shard_map/ppermute | solution.py:395
  32.1 4.5 %collective-permute-start.9 = (f32[8,128]{1,0:T(8,128)S(1)}, f32[8,128]{1,0:T(8,128)S(1)}, u32[]{:S(2)}, u32[]{:S(2)}) collective-permute-start(f32[8,128]{1,0:T(8,128)S(1)} %slice_add_fusion), channel_id=1, source_target_pairs={{0,3},{1,0},{2,1},{3,2},{4,7},{5,4},{6,5},{7,6},{8,11},{9,8},{10,9... | collective-permute-start | bytes 12296 | tf_op jit(solution)/shard_map/ppermute | solution.py:395

commit v3 on v2

--- a/solution.py
+++ b/solution.py
@@ -32,40 +32,16 @@
     return value * pair
 
 
-def edges_kernel(density, radiance, to_core, to_chip, sems):
-    tiles = density.shape[0]
-
-    def copies(row_in, row_out):
-        first = [density.at[0, :, 0, :]] + [radiance.at[c, 0, :, 0, :] for c in range(3)]
-        last = [density.at[tiles - 1, :, SUB - 1, :]]
-        last += [radiance.at[c, tiles - 1, :, SUB - 1, :] for c in range(3)]
-        made = []
-        for at, source in enumerate(first):
-            made.append(pltpu.make_async_copy(source, row_in.at[at], sems.at[at]))
-        for at, source in enumerate(last):
-            made.append(pltpu.make_async_copy(source, row_out.at[at], sems.at[4 + at]))
-        return made
-
-    even = lax.rem(lax.axis_index("depth"), 2) == 0
-
-    @pl.when(even)
-    def _():
-        made = copies(to_chip, to_core)
-        for copy in made:
-            copy.start()
-        for copy in made:
-            copy.wait()
-
-    @pl.when(jnp.logical_not(even))
-    def _():
-        made = copies(to_core, to_chip)
-        for copy in made:
-            copy.start()
-        for copy in made:
-            copy.wait()
-
-
-def slab_kernel(density, radiance, out_h, out_state, out_first, out_last):
+def edge_kernel(density, radiance, out, sems):
+    rows = [density.at[0, :, 0, :]] + [radiance.at[c, 0, :, 0, :] for c in range(3)]
+    copies = [pltpu.make_async_copy(row, out.at[at], sems.at[at]) for at, row in enumerate(rows)]
+    for copy in copies:
+        copy.start()
+    for copy in copies:
+        copy.wait()
+
+
+def slab_kernel(density, radiance, out_h, out_state, out_first, out_last, out_cell, out_colors):
     tiles, blocks = density.shape[0], density.shape[1]
     samples = tiles * SUB
     step = BLOCKS
@@ -108,65 +84,80 @@
                 else:
                     out_h[g, c, i - 1] = value + before[c]
                 before[c] = value
+        out_cell[0, part] = here
         out_state[0, part] = transmit
         for c in range(3):
             out_state[1 + c, part] = prefix[c]
             out_last[c, part] = before[c]
-
-
-def boundary_kernel(
-    edge_core, edge_chip, rim_core, rim_chip, first, state, last, mine, other, h_first, h_last, full
-):
+            out_colors[c, part] = color_here[c]
+
+
+def boundary_kernel(cell, colors, behind, state, last, mine, other, h_last, full):
     blocks = state.shape[1]
     half = blocks // 2
     parity = lax.rem(lax.axis_index("depth"), 2)
-    even = parity == 0
-    step = BLOCKS
-    for at in range(0, blocks, step):
-        part = pl.ds(at, step)
-        density = jnp.where(even, edge_core[0, part], edge_chip[0, part])
-        density = density + jnp.where(even, rim_core[0, part], rim_chip[0, part])
-        opacity = opacity_of(density)
+    for at in range(0, blocks, BLOCKS):
+        part = pl.ds(at, BLOCKS)
+        opacity = opacity_of(cell[0, part] + behind[0, part])
         transmit = state[0, part]
         weight = transmit * opacity
         transmit = transmit - weight
         full[0, part] = transmit
-        for c in range(1, 4):
-            own_last = jnp.where(even, edge_core[c, part], edge_chip[c, part])
-            own_first = jnp.where(even, edge_chip[c, part], edge_core[c, part])
-            behind = jnp.where(even, rim_core[c, part], rim_chip[c, part])
-            ahead = jnp.where(even, rim_chip[c, part], rim_core[c, part])
-            color = own_last + behind
-            prefix = state[c, part] + weight * color
-            full[c, part] = prefix
-            h_last[c - 1, part] = last[c - 1, part] + transmit * color + prefix
-            start = jnp.where(lax.axis_index("depth") == 0, 0.0, own_first + ahead)
-            h_first[c - 1, part] = first[c - 1, part] + start
+        for c in range(3):
+            color = colors[c, part] + behind[1 + c, part]
+            prefix = state[1 + c, part] + weight * color
+            full[1 + c, part] = prefix
+            h_last[c, part] = last[c, part] + transmit * color + prefix
     mine[...] = full[:, pl.ds(pl.multiple_of(parity * half, SUB), half), :]
     other[...] = full[:, pl.ds(pl.multiple_of((1 - parity) * half, SUB), half), :]
 
 
-def grad_kernel(mine, other, h, h_first, h_last, out):
+def grad_kernel(own, scales, h, first, edge, ahead, h_last, *refs):
+    out, buffers, sems = refs[-3:]
     tiles, blocks = out.shape[0], out.shape[1]
     samples = tiles * SUB
-    half = mine.shape[1]
-    at = pl.program_id(0) * blocks
-    inside = pl.multiple_of(lax.rem(at, half), SUB)
-    use_mine = at // half == lax.rem(lax.axis_index("depth"), 2)
-    part = pl.ds(inside, blocks)
-    outer = pl.ds(pl.multiple_of(at, SUB), blocks)
-    a0, a1, a2, base = (jnp.where(use_mine, mine[c, part], other[pl.ds(c * half + inside, blocks), :]) for c in range(4))
-    base_first = jnp.where(lax.axis_index("depth") == 0, 0.5 * base, base)
-    rows = out.reshape(tiles * blocks * SUB, LANES)
-    for i in range(samples):
-        if i == 0:
-            h0, h1, h2 = (h_first[c, outer] for c in range(3))
-        elif i == samples - 1:
-            h0, h1, h2 = (h_last[c, outer] for c in range(3))
-        else:
-            h0, h1, h2 = (h[pl.program_id(0), c, i - 1] for c in range(3))
-        value = a0 * h0 + a1 * h1 + a2 * h2 - (base_first if i == 0 else base)
-        rows[pl.ds((i // SUB) * blocks * SUB + i % SUB, blocks, stride=SUB), :] = value
+    half = blocks // 2
+    step = BLOCKS
+    index = lax.axis_index("depth")
+    parity = lax.rem(index, 2)
+    start = pl.multiple_of((parity if own else 1 - parity) * half, step)
+    count = half // step
+
+    def copy(k):
+        part = pl.ds(pl.multiple_of(start + k * step, step), step)
+        return pltpu.make_async_copy(buffers.at[k], out.at[:, part], sems.at[k])
+
+    @pl.loop(0, count)
+    def _(k):
+        inside = pl.ds(pl.multiple_of(k * step, step), step)
+        part = pl.ds(pl.multiple_of(start + k * step, step), step)
+        group = lax.div(start, step) + k
+        a0, a1, a2, base = (scales[c, inside] for c in range(4))
+        rows = buffers.at[k].reshape(tiles * step * SUB, LANES)
+        for i in range(samples):
+            away = base
+            if i == 0:
+                h0, h1, h2 = (
+                    first[c, part]
+                    + jnp.where(index == 0, 0.0, edge[1 + c, part] + ahead[c, part])
+                    for c in range(3)
+                )
+                away = jnp.where(index == 0, 0.5 * base, base)
+            elif i == samples - 1:
+                h0, h1, h2 = (h_last[c, part] for c in range(3))
+            else:
+                h0, h1, h2 = (h[group, c, i - 1] for c in range(3))
+            value = a0 * h0 + a1 * h1 + a2 * h2 - away
+            rows[pl.ds((i // SUB) * step * SUB + i % SUB, step, stride=SUB), :] = value
+        copy(k).start()
+
+    @pl.loop(0, count)
+    def _(k):
+        copy(k).wait()
+
+
+def sent(value, axis, pairs):
+    return lax.ppermute(value, axis, pairs)
 
 
 def compose(front, back):
@@ -225,7 +216,7 @@
 def scale_kernel(stride, width, started, mine, theirs, target, *refs):
     members = refs[:width]
     earlier = refs[width] if started else None
-    out_mine, out_message, out_loss = refs[-3:]
+    out_mine, out_other, out_loss = refs[-3:]
     half = out_mine.shape[1]
     parity = lax.rem(lax.axis_index("depth"), 2)
     even = parity == 0
@@ -256,12 +247,9 @@
             @pl.when(jnp.logical_not(is_own))
             def _():
                 for c in range(4):
-                    out_message[pl.ds(c * half + at, BLOCKS), :] = values[c]
-
-    folded = sum(loss[at : at + SUB] for at in range(0, BLOCKS, SUB))
-    folded = jnp.full((SUB, LANES), jnp.sum(folded), jnp.float32)
-    out_message[pl.ds(4 * half, SUB), :] = folded
-    out_loss[...] = folded
+                    out_other[c, part] = values[c]
+
+    out_loss[...] = jnp.full(out_loss.shape, jnp.sum(loss), jnp.float32)
 
 
 def stages(count):
@@ -269,6 +257,15 @@
         width = 4 if count % 4 == 0 else 2 if count % 2 == 0 else count
         yield width
         count //= width
+
+
+def ring_sum(count):
+    if count == 4:
+        return [[[(0, 1), (1, 0), (2, 3), (3, 2)]], [[(1, 2), (2, 1), (3, 0), (0, 3)]]]
+    if count & (count - 1) == 0 and count > 1:
+        steps = [1 << bit for bit in range(count.bit_length() - 1)]
+        return [[[(d, d ^ step) for d in range(count)]] for step in steps]
+    return [[[(d, (d + k) % count) for d in range(count)] for k in range(1, count)]]
 
 
 def partner(device, stride, width, step):
@@ -292,36 +289,37 @@
     density = tiled(density)
     radiance = tiled(radiance)
     swap = [(d, d ^ 1) for d in range(devices)]
-    chain = [p for d in range(1, devices - 1, 2) for p in ((d, d + 1), (d + 1, d))]
-
+
+    row = jax.ShapeDtypeStruct((1, blocks, LANES), f32)
+    colors = jax.ShapeDtypeStruct((3, blocks, LANES), f32)
     edge = jax.ShapeDtypeStruct((4, blocks, LANES), f32)
-    row = jax.ShapeDtypeStruct((3, blocks, LANES), f32)
     whole = pl.BlockSpec(memory_space=pltpu.VMEM)
-    stays = pl.BlockSpec(memory_space=pltpu.HBM)
-    edge_core, edge_chip = pl.pallas_call(
-        edges_kernel,
-        out_shape=(edge, edge),
+    stays = pl.BlockSpec(memory_space=pl.ANY)
+    first_row = pl.pallas_call(
+        edge_kernel,
+        out_shape=edge,
         in_specs=[stays, stays],
-        out_specs=(whole, whole),
-        scratch_shapes=[pltpu.SemaphoreType.DMA((8,))],
+        out_specs=whole,
+        scratch_shapes=[pltpu.SemaphoreType.DMA((4,))],
         compiler_params=pltpu.CompilerParams(vmem_limit_bytes=EDGES),
-        name="edges",
+        name="edge",
     )(density, radiance)
-    rim_chip = lax.ppermute(edge_chip, "depth", chain)
-    rim_core = lax.ppermute(edge_core, "depth", swap)
+    behind = sent(first_row, "depth", [(d + 1, d) for d in range(devices - 1)])
 
     step = BLOCKS
     grid = blocks // step
-    h, state, first, last = pl.pallas_call(
+    h, state, first, last, last_cell, last_colors = pl.pallas_call(
         slab_kernel,
         out_shape=(
             jax.ShapeDtypeStruct((grid, 3, samples - 2, step, LANES), f32),
             edge,
+            colors,
+            colors,
             row,
-            row,
+            colors,
         ),
         in_specs=[whole, whole],
-        out_specs=(whole,) * 4,
+        out_specs=(whole,) * 6,
         compiler_params=pltpu.CompilerParams(vmem_limit_bytes=KEPT),
         cost_estimate=pl.CostEstimate(
             flops=40 * samples * ray_count,
@@ -332,18 +330,19 @@
     )(density, radiance)
 
     part = jax.ShapeDtypeStruct((4, half, LANES), f32)
-    mine, other, h_first, h_last = pl.pallas_call(
+    ahead = sent(last_colors, "depth", [(d, d + 1) for d in range(devices - 1)])
+    mine, other, h_last = pl.pallas_call(
         boundary_kernel,
-        out_shape=(part, part, row, row),
-        in_specs=[whole] * 7,
-        out_specs=(whole,) * 4,
+        out_shape=(part, part, colors),
+        in_specs=[whole] * 5,
+        out_specs=(whole,) * 3,
         scratch_shapes=[pltpu.VMEM((4, blocks, LANES), f32)],
         compiler_params=pltpu.CompilerParams(vmem_limit_bytes=KEPT),
         name="boundary",
-    )(edge_core, edge_chip, rim_core, rim_chip, first, state, last)
+    )(last_cell, last_colors, behind, state, last)
 
     small = pltpu.CompilerParams(vmem_limit_bytes=SMALL)
-    theirs = lax.ppermute(other, "depth", swap)
+    theirs = sent(other, "depth", swap)
     total = pl.pallas_call(
         chip_kernel,
         out_shape=part,
@@ -358,7 +357,7 @@
     widths = list(stages(devices // 2)) or [1]
     for at, width in enumerate(widths):
         members = [total] + [
-            lax.ppermute(total, "depth", [(partner(d, stride, width, k), d) for d in range(devices)])
+            sent(total, "depth", [(partner(d, stride, width, k), d) for d in range(devices)])
             for k in range(1, width)
         ]
         last_stage = at == len(widths) - 1
@@ -367,7 +366,7 @@
             given = (mine, theirs, goal, *members, *earlier)
             made = (
                 part,
-                jax.ShapeDtypeStruct((4 * half + SUB, LANES), f32),
+                part,
                 jax.ShapeDtypeStruct((SUB, LANES), f32),
             )
         else:
@@ -385,43 +384,41 @@
         if not last_stage:
             earlier, total = (results[0],), results[1]
         stride *= width
-    scale_mine, message, loss = results
-
-    received = lax.ppermute(message, "depth", swap)
-    loss = loss + received[4 * half :]
-
+    scale_mine, scale_other, loss = results
+
+    def grad_half(own, scales, *before):
+        return pl.pallas_call(
+            functools.partial(grad_kernel, own),
+            out_shape=jax.ShapeDtypeStruct((tiles, blocks, SUB, LANES), f32),
+            in_specs=[whole] * 6 + [stays] * len(before),
+            out_specs=stays,
+            input_output_aliases={6: 0} if before else {},
+            scratch_shapes=[
+                pltpu.VMEM((grid // 2, tiles, step, SUB, LANES), f32),
+                pltpu.SemaphoreType.DMA((grid // 2,)),
+            ],
+            compiler_params=pltpu.CompilerParams(vmem_limit_bytes=KEPT),
+            cost_estimate=pl.CostEstimate(
+                flops=4 * samples * ray_count,
+                bytes_accessed=8 * samples * ray_count,
+                transcendentals=0,
+            ),
+            name="grad",
+        )(scales, h, first, first_row, ahead, h_last, *before)
+
+    scale_theirs = sent(scale_other, "depth", swap)
     groups = lax.axis_size("rays")
-    parts = [
-        lax.ppermute(loss, "rays", [(d, (d + k) % groups) for d in range(groups)])
-        for k in range(1, groups)
-    ]
-
-    grad = pl.pallas_call(
-        grad_kernel,
-        grid=(grid,),
-        out_shape=jax.ShapeDtypeStruct((tiles, blocks, SUB, LANES), f32),
-        in_specs=[
-            whole,
-            whole,
-            whole,
-            whole,
-            whole,
-        ],
-        out_specs=pl.BlockSpec((tiles, step, SUB, LANES), lambda g: (0, g, 0, 0)),
-        compiler_params=pltpu.CompilerParams(vmem_limit_bytes=KEPT),
-        cost_estimate=pl.CostEstimate(
-            flops=8 * samples * ray_count,
-            bytes_accessed=16 * samples * ray_count,
-            transcendentals=0,
-        ),
-        name="grad",
-    )(scale_mine, received, h, h_first, h_last)
+    rounds = ring_sum(groups)
+    for at, pairs in enumerate(rounds):
+        others = [sent(loss, "rays", pair) for pair in pairs]
+        if at == 0:
+            grad = grad_half(True, scale_mine)
+        loss = sum(others, loss)
+        if at == 0:
+            loss = loss + sent(loss, "depth", swap)
+            grad = grad_half(False, scale_theirs, grad)
     grad = jnp.swapaxes(grad, 1, 2).reshape(samples, ray_count)
-    squares = loss
-    for value in parts:
-        squares = squares + value
-    loss_mean = squares[0, 0] / (3.0 * ray_count * groups)
-    return grad, loss_mean
+    return grad, loss[0, 0] / (3.0 * ray_count * groups)
 
 
 def solution(mesh):

time: 39.1 us -> 36.3 us (0.928)
  starting transfers between devices: 18.3 us -> 16.9 us
  Pallas kernels: 7.51 us -> 6.24 us
    ppermute x10, starting transfers between devices: 18.3 us -> 16.9 us  [sent(): return lax.ppermute(value, axis, pairs)]
    pallas_call x3 -> x4, Pallas kernels: 4.63 us -> 3.36 us  [the longest x2 2.14 us: grad_half(): pl.pallas_call(functools.partial(grad_kernel, own), out_shape=jax.ShapeDt...]
  transfers between devices with their start and end apart: 10 -> 10, of which waited for: 4 -> 7; matrix products, arithmetic and copies ran while one was open for 0% -> 1% of each run, Pallas kernels for 15% -> 11%
where the time goes in v3:
time: 36.3 us; the launch traced here: 36.1 us
  starting transfers between devices  16.9 us (47%)
  waiting for transfers between devices  9.09 us (25%)
  Pallas kernels  6.24 us (17%)
  between operations  2.55 us (7%)
  local copies, waits for them, and re-layouts  1.36 us (4%)
    ppermute x10, starting transfers between devices, sent(): return lax.ppermute(value, axis, pairs)  16.9 us
    ppermute x10, waiting for transfers between devices, sent(): return lax.ppermute(value, axis, pairs)  9.09 us
    pallas_call x1, Pallas kernels, on_device(): pl.pallas_call(slab_kernel, out_shape=(jax.ShapeDtypeStruct((grid, 3, sam...  2.54 us
    pallas_call x2, Pallas kernels, grad_half(): pl.pallas_call(functools.partial(grad_kernel, own), out_shape=jax.ShapeDt...  2.14 us
    pallas_call x1, Pallas kernels, on_device(): pl.pallas_call(edge_kernel, out_shape=edge, in_specs=[stays, stays], out_...  1.12 us
    unnamed x7, local copies, waits for them, and re-layouts  0.84 us
  transfers between devices with their start and end apart: 10, of which 7 were waited for; matrix products, arithmetic and copies ran while one was open for 1% of the time, Pallas kernels for 11%

profile of v3, /device:TPU:0, one launch (start us, length us, event | category | flops | bytes accessed | tf_op | source)
XLA Modules:
  0.0 36.1 jit_solution(17773308865712563768)
XLA Ops:
  0.6 1.1 %edge.1 = f32[4,128,128]{2,1,0:T(8,128)S(1)} custom-call(f32[4,128,8,128]{3,2,1,0:T(8,128)} %bitcast.16, f32[3,4,128,8,128]{4,3,2,1,0:T(8,128)} %bitcast.14), custom_call_target="tpu_custom_call" | custom-call | tf_op jit(solution)/shard_map/edge/pallas_call | solution.py:298
  1.8 1.6 %collective-permute-start = (f32[4,128,128]{2,1,0:T(8,128)S(1)}, f32[4,128,128]{2,1,0:T(8,128)S(1)}, u32[]{:S(2)}, u32[]{:S(2)}) collective-permute-start(f32[4,128,128]{2,1,0:T(8,128)S(1)} %edge.1), channel_id=1, source_target_pairs={{4,0},{8,4},{12,8},{16,12},{20,16},{24,20},{28,24},{5,1},{9,5},{13... | collective-permute-start | bytes 786440 | tf_op jit(solution)/shard_map/ppermute | solution.py:160
  3.4 0.2 copy-done
  3.5 0.6 %copy-done.1 = f32[32,16384]{1,0:T(8,128)S(1)} copy-done((f32[32,16384]{1,0:T(8,128)S(1)}, f32[32,16384]{1,0:T(8,128)}, u32[]{:S(2)}) %copy-start.1) | copy-done | bytes 2097176
  4.2 2.5 %slab.1 = (f32[8,3,30,16,128]{4,3,2,1,0:T(8,128)S(1)}, f32[4,128,128]{2,1,0:T(8,128)S(1)}, f32[3,128,128]{2,1,0:T(8,128)S(1)}, f32[3,128,128]{2,1,0:T(8,128)S(1)...) custom-call(f32[4,128,8,128]{3,2,1,0:T(8,128)S(1)} %bitcast.17, f32[3,4,128,8,128]{4,3,2,1,0:T(8,128)S(1)} %bitcast.15), custom_call_target="tpu_custom_call" | custom-call | flops 20971520 | bytes 8388608 | tf_op jit(solution)/shard_map/slab/pallas_call | solution.py:311
  6.7 0.1 boundary.1
  6.8 4.4 %collective-permute-start.1 = (f32[4,64,128]{2,1,0:T(8,128)S(1)}, f32[4,64,128]{2,1,0:T(8,128)S(1)}, u32[]{:S(2)}, u32[]{:S(2)}) collective-permute-start(f32[4,64,128]{2,1,0:T(8,128)S(1)} %get-tuple-element.19), channel_id=1, source_target_pairs={{0,4},{4,0},{8,12},{12,8},{16,20},{20,16},{24,28},{28,24},{1,5},{5... | collective-permute-start | bytes 393224 | tf_op jit(solution)/shard_map/ppermute | solution.py:160
  11.3 1.0 %collective-permute-done.1.theirs = f32[4,64,128]{2,1,0:T(8,128)S(1)} collective-permute-done((f32[4,64,128]{2,1,0:T(8,128)S(1)}, f32[4,64,128]{2,1,0:T(8,128)S(1)}, u32[]{:S(2)}, u32[]{:S(2)}) %collective-permute-start.1) | collective-permute-done | bytes 131104 | tf_op jit(solution)/shard_map/ppermute | solution.py:160
  12.3 1.1 %collective-permute-start.4 = (f32[4,64,128]{2,1,0:T(8,128)S(1)}, f32[4,64,128]{2,1,0:T(8,128)S(1)}, u32[]{:S(2)}, u32[]{:S(2)}) collective-permute-start(f32[4,64,128]{2,1,0:T(8,128)S(1)} %chip.1.refs_0_), channel_id=1, source_target_pairs={{24,0},{28,4},{16,8},{20,12},{8,16},{12,20},{0,24},{4,28},{25,1},{... | collective-permute-start | bytes 393224 | tf_op jit(solution)/shard_map/ppermute | solution.py:160
  13.4 2.8 %collective-permute-start.3 = (f32[4,64,128]{2,1,0:T(8,128)S(1)}, f32[4,64,128]{2,1,0:T(8,128)S(1)}, u32[]{:S(2)}, u32[]{:S(2)}) collective-permute-start(f32[4,64,128]{2,1,0:T(8,128)S(1)} %chip.1.refs_0_), channel_id=1, source_target_pairs={{16,0},{20,4},{24,8},{28,12},{0,16},{4,20},{8,24},{12,28},{17,1},{... | collective-permute-start | bytes 393224 | tf_op jit(solution)/shard_map/ppermute | solution.py:160
  16.2 1.7 %collective-permute-start.6 = (f32[3,128,128]{2,1,0:T(8,128)S(1)}, f32[3,128,128]{2,1,0:T(8,128)S(1)}, u32[]{:S(2)}, u32[]{:S(2)}) collective-permute-start(f32[3,128,128]{2,1,0:T(8,128)S(1)} %get-tuple-element.15.colors), channel_id=1, source_target_pairs={{0,4},{4,8},{8,12},{12,16},{16,20},{20,24},{24,28},{1,5},{5,9},{9,... | collective-permute-start | bytes 589832 | tf_op jit(solution)/shard_map/ppermute | solution.py:160
  17.9 1.7 %collective-permute-done.4.refs_3_ = f32[4,64,128]{2,1,0:T(8,128)S(1)} collective-permute-done((f32[4,64,128]{2,1,0:T(8,128)S(1)}, f32[4,64,128]{2,1,0:T(8,128)S(1)}, u32[]{:S(2)}, u32[]{:S(2)}) %collective-permute-start.4) | collective-permute-done | bytes 131104 | tf_op jit(solution)/shard_map/ppermute | solution.py:160
  19.6 2.2 %collective-permute-done.3.refs_2_ = f32[4,64,128]{2,1,0:T(8,128)S(1)} collective-permute-done((f32[4,64,128]{2,1,0:T(8,128)S(1)}, f32[4,64,128]{2,1,0:T(8,128)S(1)}, u32[]{:S(2)}, u32[]{:S(2)}) %collective-permute-start.3) | collective-permute-done | bytes 131104 | tf_op jit(solution)/shard_map/ppermute | solution.py:160
  21.8 0.3 collective-permute-done.2.refs_1_
  22.1 0.3 scale.1
  22.4 0.1 collective-permute-start.5
  22.5 1.6 %collective-permute-start.7 = (f32[8,128]{1,0:T(8,128)S(1)}, f32[8,128]{1,0:T(8,128)S(1)}, u32[]{:S(2)}, u32[]{:S(2)}) collective-permute-start(f32[8,128]{1,0:T(8,128)S(1)} %get-tuple-element.25), channel_id=1, source_target_pairs={{0,1},{1,0},{2,3},{3,2},{4,5},{5,4},{6,7},{7,6},{8,9},{9,8},{10,11... | collective-permute-start | bytes 12296 | tf_op jit(solution)/shard_map/ppermute | solution.py:160
  24.1 2.0 %collective-permute-done.7 = f32[8,128]{1,0:T(8,128)S(1)} collective-permute-done((f32[8,128]{1,0:T(8,128)S(1)}, f32[8,128]{1,0:T(8,128)S(1)}, u32[]{:S(2)}, u32[]{:S(2)}) %collective-permute-start.7) | collective-permute-done | bytes 4128 | tf_op jit(solution)/shard_map/ppermute | solution.py:160
  26.2 1.2 %collective-permute-done.8 = f32[8,128]{1,0:T(8,128)S(1)} collective-permute-done((f32[8,128]{1,0:T(8,128)S(1)}, f32[8,128]{1,0:T(8,128)S(1)}, u32[]{:S(2)}, u32[]{:S(2)}) %collective-permute-start.8) | collective-permute-done | bytes 4128 | tf_op jit(solution)/shard_map/ppermute | solution.py:160
  27.3 3.6 %collective-permute-start.9 = (f32[8,128]{1,0:T(8,128)S(1)}, f32[8,128]{1,0:T(8,128)S(1)}, u32[]{:S(2)}, u32[]{:S(2)}) collective-permute-start(f32[8,128]{1,0:T(8,128)S(1)} %add.10), channel_id=1, source_target_pairs={{1,2},{2,1},{3,0},{0,3},{5,6},{6,5},{7,4},{4,7},{9,10},{10,9},{11,... | collective-permute-start | bytes 12296 | tf_op jit(solution)/shard_map/ppermute | solution.py:160
  30.9 1.1 %grad.2.refs_0_ = f32[4,128,8,128]{3,2,1,0:T(8,128)} custom-call(f32[4,64,128]{2,1,0:T(8,128)S(1)} %get-tuple-element.24.scales, f32[8,3,30,16,128]{4,3,2,1,0:T(8,128)S(1)} %get-tuple-element.21.h, f32[3,128,128]{2,1,0:T(8,128)S(1)} %get-tuple-element.22.first, f32[4,128,128]{2,1,0:T(8,128)S(1)} %edge.1, f32[3,128,128]{2,1,0:T(8,128)S(1)} %collective-permute-done.6.ahead, ...), custom_call_target="tpu_custom_call" | custom-call | flops 2097152 | bytes 4194304 | tf_op jit(solution)/shard_map/grad/pallas_call | solution.py:390
  32.0 0.7 %collective-permute-done.9 = f32[8,128]{1,0:T(8,128)S(1)} collective-permute-done((f32[8,128]{1,0:T(8,128)S(1)}, f32[8,128]{1,0:T(8,128)S(1)}, u32[]{:S(2)}, u32[]{:S(2)}) %collective-permute-start.9) | collective-permute-done | bytes 4128 | tf_op jit(solution)/shard_map/ppermute | solution.py:160
  32.7 0.5 %slice.3 = f32[1,1]{1,0:T(1,128)} slice(f32[8,128]{1,0:T(8,128)S(1)} %add.11), slice={[0:1], [0:1]} | slice | bytes 8 | tf_op jit(solution)/shard_map/slice | solution.py:421
  33.9 1.1 %grad.3 = f32[4,128,8,128]{3,2,1,0:T(8,128)} custom-call(f32[4,64,128]{2,1,0:T(8,128)S(1)} %collective-permute-done.5.scales, f32[8,3,30,16,128]{4,3,2,1,0:T(8,128)S(1)} %get-tuple-element.21.h, f32[3,128,128]{2,1,0:T(8,128)S(1)} %get-tuple-element.22.first, f32[4,128,128]{2,1,0:T(8,128)S(1)} %edge.1, ...), custom_call_target="tpu_custom_call", output_to_operand_aliasing={{}: (6, {})} | custom-call | flops 2097152 | bytes 4194304 | tf_op jit(solution)/shard_map/grad/pallas_call | solution.py:390
  (14 shorter events, 0.1 us)
Async XLA Ops:
  0.6 2.9 %copy-start = (f32[3,32,16384]{2,1,0:T(8,128)S(1)}, f32[3,32,16384]{2,1,0:T(8,128)}, u32[]{:S(2)}) copy-start(f32[3,32,16384]{2,1,0:T(8,128)} %param.4) | copy-start | bytes 18874372
  0.6 3.5 %copy-start.1 = (f32[32,16384]{1,0:T(8,128)S(1)}, f32[32,16384]{1,0:T(8,128)}, u32[]{:S(2)}) copy-start(f32[32,16384]{1,0:T(8,128)} %param.3) | copy-start | bytes 6291460
  1.8 16.1 %copy-start.2 = (f32[3,16384]{1,0:T(4,128)S(1)}, f32[3,16384]{1,0:T(4,128)}, u32[]{:S(2)}) copy-start(f32[3,16384]{1,0:T(4,128)} %param.5) | copy-start | bytes 589828
  1.8 4.9 %collective-permute-start = (f32[4,128,128]{2,1,0:T(8,128)S(1)}, f32[4,128,128]{2,1,0:T(8,128)S(1)}, u32[]{:S(2)}, u32[]{:S(2)}) collective-permute-start(f32[4,128,128]{2,1,0:T(8,128)S(1)} %edge.1), channel_id=1, source_target_pairs={{4,0},{8,4},{12,8},{16,12},{20,16},{24,20},{28,24},{5,1},{9,5},{13... | collective-permute-start | bytes 786440 | tf_op jit(solution)/shard_map/ppermute | solution.py:160
  6.8 5.4 %collective-permute-start.1 = (f32[4,64,128]{2,1,0:T(8,128)S(1)}, f32[4,64,128]{2,1,0:T(8,128)S(1)}, u32[]{:S(2)}, u32[]{:S(2)}) collective-permute-start(f32[4,64,128]{2,1,0:T(8,128)S(1)} %get-tuple-element.19), channel_id=1, source_target_pairs={{0,4},{4,0},{8,12},{12,8},{16,20},{20,16},{24,28},{28,24},{1,5},{5... | collective-permute-start | bytes 393224 | tf_op jit(solution)/shard_map/ppermute | solution.py:160
  12.3 7.3 %collective-permute-start.4 = (f32[4,64,128]{2,1,0:T(8,128)S(1)}, f32[4,64,128]{2,1,0:T(8,128)S(1)}, u32[]{:S(2)}, u32[]{:S(2)}) collective-permute-start(f32[4,64,128]{2,1,0:T(8,128)S(1)} %chip.1.refs_0_), channel_id=1, source_target_pairs={{24,0},{28,4},{16,8},{20,12},{8,16},{12,20},{0,24},{4,28},{25,1},{... | collective-permute-start | bytes 393224 | tf_op jit(solution)/shard_map/ppermute | solution.py:160
  13.4 8.4 %collective-permute-start.3 = (f32[4,64,128]{2,1,0:T(8,128)S(1)}, f32[4,64,128]{2,1,0:T(8,128)S(1)}, u32[]{:S(2)}, u32[]{:S(2)}) collective-permute-start(f32[4,64,128]{2,1,0:T(8,128)S(1)} %chip.1.refs_0_), channel_id=1, source_target_pairs={{16,0},{20,4},{24,8},{28,12},{0,16},{4,20},{8,24},{12,28},{17,1},{... | collective-permute-start | bytes 393224 | tf_op jit(solution)/shard_map/ppermute | solution.py:160
  16.2 5.9 %collective-permute-start.2 = (f32[4,64,128]{2,1,0:T(8,128)S(1)}, f32[4,64,128]{2,1,0:T(8,128)S(1)}, u32[]{:S(2)}, u32[]{:S(2)}) collective-permute-start(f32[4,64,128]{2,1,0:T(8,128)S(1)} %chip.1.refs_0_), channel_id=1, source_target_pairs={{8,0},{12,4},{0,8},{4,12},{24,16},{28,20},{16,24},{20,28},{9,1},{1... | collective-permute-start | bytes 393224 | tf_op jit(solution)/shard_map/ppermute | solution.py:160
  16.2 14.8 %collective-permute-start.6 = (f32[3,128,128]{2,1,0:T(8,128)S(1)}, f32[3,128,128]{2,1,0:T(8,128)S(1)}, u32[]{:S(2)}, u32[]{:S(2)}) collective-permute-start(f32[3,128,128]{2,1,0:T(8,128)S(1)} %get-tuple-element.15.colors), channel_id=1, source_target_pairs={{0,4},{4,8},{8,12},{12,16},{16,20},{20,24},{24,28},{1,5},{5,9},{9,... | collective-permute-start | bytes 589832 | tf_op jit(solution)/shard_map/ppermute | solution.py:160
  22.4 11.5 %collective-permute-start.5 = (f32[4,64,128]{2,1,0:T(8,128)S(1)}, f32[4,64,128]{2,1,0:T(8,128)S(1)}, u32[]{:S(2)}, u32[]{:S(2)}) collective-permute-start(f32[4,64,128]{2,1,0:T(8,128)S(1)} %get-tuple-element.20), channel_id=1, source_target_pairs={{0,4},{4,0},{8,12},{12,8},{16,20},{20,16},{24,28},{28,24},{1,5},{5... | collective-permute-start | bytes 393224 | tf_op jit(solution)/shard_map/ppermute | solution.py:160
  22.5 3.7 %collective-permute-start.7 = (f32[8,128]{1,0:T(8,128)S(1)}, f32[8,128]{1,0:T(8,128)S(1)}, u32[]{:S(2)}, u32[]{:S(2)}) collective-permute-start(f32[8,128]{1,0:T(8,128)S(1)} %get-tuple-element.25), channel_id=1, source_target_pairs={{0,1},{1,0},{2,3},{3,2},{4,5},{5,4},{6,7},{7,6},{8,9},{9,8},{10,11... | collective-permute-start | bytes 12296 | tf_op jit(solution)/shard_map/ppermute | solution.py:160
  26.2 1.2 %collective-permute-start.8 = (f32[8,128]{1,0:T(8,128)S(1)}, f32[8,128]{1,0:T(8,128)S(1)}, u32[]{:S(2)}, u32[]{:S(2)}) collective-permute-start(f32[8,128]{1,0:T(8,128)S(1)} %add.9), channel_id=1, source_target_pairs={{0,4},{4,0},{8,12},{12,8},{16,20},{20,16},{24,28},{28,24},{1,5},{5... | collective-permute-start | bytes 12296 | tf_op jit(solution)/shard_map/ppermute | solution.py:160
  27.3 5.4 %collective-permute-start.9 = (f32[8,128]{1,0:T(8,128)S(1)}, f32[8,128]{1,0:T(8,128)S(1)}, u32[]{:S(2)}, u32[]{:S(2)}) collective-permute-start(f32[8,128]{1,0:T(8,128)S(1)} %add.10), channel_id=1, source_target_pairs={{1,2},{2,1},{3,0},{0,3},{5,6},{6,5},{7,4},{4,7},{9,10},{10,9},{11,... | collective-permute-start | bytes 12296 | tf_op jit(solution)/shard_map/ppermute | solution.py:160

commit v4 on v3

--- a/solution.py
+++ b/solution.py
@@ -1,4 +1,5 @@
 import functools
+import math
 
 import jax
 import jax.numpy as jnp
@@ -32,16 +33,24 @@
     return value * pair
 
 
-def edge_kernel(density, radiance, out, sems):
-    rows = [density.at[0, :, 0, :]] + [radiance.at[c, 0, :, 0, :] for c in range(3)]
-    copies = [pltpu.make_async_copy(row, out.at[at], sems.at[at]) for at, row in enumerate(rows)]
-    for copy in copies:
-        copy.start()
-    for copy in copies:
-        copy.wait()
-
-
-def slab_kernel(density, radiance, out_h, out_state, out_first, out_last, out_cell, out_colors):
+def is_even():
+    return lax.rem(lax.axis_index("depth"), 2) == 0
+
+
+def edge_kernel(density, unused, to_core, to_chip, rows, sems):
+    tiles = density.shape[0]
+    first = pltpu.make_async_copy(density.at[0, :, 0, :], rows.at[0], sems.at[0])
+    last = pltpu.make_async_copy(density.at[tiles - 1, :, SUB - 1, :], rows.at[1], sems.at[1])
+    first.start()
+    last.start()
+    first.wait()
+    last.wait()
+    even = is_even()
+    to_core[0] = jnp.where(even, rows[1], rows[0])
+    to_chip[0] = jnp.where(even, rows[0], rows[1])
+
+
+def slab_kernel(density, radiance, out_h, out_state, out_first, out_last, to_core, to_chip):
     tiles, blocks = density.shape[0], density.shape[1]
     samples = tiles * SUB
     step = BLOCKS
@@ -59,6 +68,8 @@
 
         here = cell(rows, 0, 0)
         color_here = [cell(planes, c, 0) for c in range(3)]
+        even = is_even()
+        color_first = list(color_here)
         transmit = None
         prefix = [None] * 3
         before = [None] * 3
@@ -84,76 +95,123 @@
                 else:
                     out_h[g, c, i - 1] = value + before[c]
                 before[c] = value
-        out_cell[0, part] = here
         out_state[0, part] = transmit
         for c in range(3):
             out_state[1 + c, part] = prefix[c]
             out_last[c, part] = before[c]
-            out_colors[c, part] = color_here[c]
-
-
-def boundary_kernel(cell, colors, behind, state, last, mine, other, h_last, full):
+            to_core[c, part] = jnp.where(even, color_here[c], color_first[c])
+            to_chip[c, part] = jnp.where(even, color_first[c], color_here[c])
+
+
+def boundary_kernel(
+    own_core, own_chip, rim_core, rim_chip, core_colors, chip_colors, state, mine, other, out_opacity, full
+):
     blocks = state.shape[1]
     half = blocks // 2
-    parity = lax.rem(lax.axis_index("depth"), 2)
+    index = lax.axis_index("depth")
+    parity = lax.rem(index, 2)
+    even = parity == 0
     for at in range(0, blocks, BLOCKS):
         part = pl.ds(at, BLOCKS)
-        opacity = opacity_of(cell[0, part] + behind[0, part])
-        transmit = state[0, part]
-        weight = transmit * opacity
-        transmit = transmit - weight
+        of_core = opacity_of(own_core[0, part] + rim_core[0, part])
+        ends = index == lax.axis_size("depth") - 1
+        of_chip = opacity_of(own_chip[0, part] + jnp.where(ends, 0.0, rim_chip[0, part]))
+        ahead = jnp.where(index == 0, 0.0, jnp.where(even, of_chip, of_core))
+        behind = jnp.where(even, of_core, of_chip)
+        out_opacity[0, part] = ahead
+        through = 1.0 - ahead
+        transmit = through * state[0, part]
         full[0, part] = transmit
+        closing = transmit * behind
         for c in range(3):
-            color = colors[c, part] + behind[1 + c, part]
-            prefix = state[1 + c, part] + weight * color
-            full[1 + c, part] = prefix
-            h_last[c, part] = last[c, part] + transmit * color + prefix
+            first = jnp.where(even, chip_colors[c, part], core_colors[c, part])
+            last = jnp.where(even, core_colors[c, part], chip_colors[c, part])
+            full[1 + c, part] = ahead * first + through * state[1 + c, part] + closing * last
     mine[...] = full[:, pl.ds(pl.multiple_of(parity * half, SUB), half), :]
     other[...] = full[:, pl.ds(pl.multiple_of((1 - parity) * half, SUB), half), :]
 
 
-def grad_kernel(own, scales, h, first, edge, ahead, h_last, *refs):
+def grad_kernel(
+    halves, groups, mine, theirs, h, first, last, state, opacity, own_core, own_chip, *refs
+):
     out, buffers, sems = refs[-3:]
+    edges = 0 in groups
+    if edges:
+        rim_core, rim_chip = refs[:2]
     tiles, blocks = out.shape[0], out.shape[1]
     samples = tiles * SUB
     half = blocks // 2
     step = BLOCKS
     index = lax.axis_index("depth")
     parity = lax.rem(index, 2)
-    start = pl.multiple_of((parity if own else 1 - parity) * half, step)
+    even = parity == 0
     count = half // step
 
-    def copy(k):
+    def copies(which, k):
+        start = pl.multiple_of((parity if which == 0 else 1 - parity) * half, step)
         part = pl.ds(pl.multiple_of(start + k * step, step), step)
-        return pltpu.make_async_copy(buffers.at[k], out.at[:, part], sems.at[k])
+        return [
+            pltpu.make_async_copy(
+                buffers.at[at, k, place], out.at[group, part], sems.at[at, k, place]
+            )
+            for at, whose in enumerate(halves)
+            if whose == which
+            for place, group in enumerate(groups)
+        ]
+
+    def piece(which, k):
+        start = pl.multiple_of((parity if which == 0 else 1 - parity) * half, step)
+        inside = pl.multiple_of(k * step, step)
+        part = pl.ds(pl.multiple_of(start + k * step, step), step)
+        slot = lax.div(start, step) + k
+        if which == 0:
+            a0, a1, a2, base = (mine[c, pl.ds(inside, step)] for c in range(4))
+        else:
+            a0, a1, a2, base = (theirs[pl.ds(c * half + inside, step), :] for c in range(4))
+        ahead = opacity[0, part]
+        core = [own_core[c, part] for c in range(3)]
+        chip = [own_chip[c, part] for c in range(3)]
+        opening = [jnp.where(even, chip[c], core[c]) for c in range(3)]
+        base = base - 2.0 * ahead * (a0 * opening[0] + a1 * opening[1] + a2 * opening[2])
+        through = 1.0 - ahead
+        a0, a1, a2 = through * a0, through * a1, through * a2
+        if edges:
+            of_core = [core[c] + rim_core[c, part] for c in range(3)]
+            ends = index == lax.axis_size("depth") - 1
+            of_chip = [chip[c] + jnp.where(ends, 0.0, rim_chip[c, part]) for c in range(3)]
+        for place, group in enumerate(groups):
+            rows = buffers.at[halves.index(which), k, place].reshape(step * SUB, LANES)
+            for i in range(group * SUB, (group + 1) * SUB):
+                away = base
+                if i == 0:
+                    h0, h1, h2 = (
+                        first[c, part]
+                        + jnp.where(index == 0, 0.0, jnp.where(even, of_chip[c], of_core[c]))
+                        for c in range(3)
+                    )
+                    away = jnp.where(index == 0, 0.5 * base, base)
+                elif i == samples - 1:
+                    h0, h1, h2 = (
+                        last[c, part]
+                        + state[1 + c, part]
+                        + state[0, part] * jnp.where(even, of_core[c], of_chip[c])
+                        for c in range(3)
+                    )
+                else:
+                    h0, h1, h2 = (h[slot, c, i - 1] for c in range(3))
+                value = a0 * h0 + a1 * h1 + a2 * h2 - away
+                rows[pl.ds(i % SUB, step, stride=SUB), :] = value
+        for copy in copies(which, k):
+            copy.start()
+
+    for which in halves:
+        pl.loop(0, count)(functools.partial(piece, which))
 
     @pl.loop(0, count)
     def _(k):
-        inside = pl.ds(pl.multiple_of(k * step, step), step)
-        part = pl.ds(pl.multiple_of(start + k * step, step), step)
-        group = lax.div(start, step) + k
-        a0, a1, a2, base = (scales[c, inside] for c in range(4))
-        rows = buffers.at[k].reshape(tiles * step * SUB, LANES)
-        for i in range(samples):
-            away = base
-            if i == 0:
-                h0, h1, h2 = (
-                    first[c, part]
-                    + jnp.where(index == 0, 0.0, edge[1 + c, part] + ahead[c, part])
-                    for c in range(3)
-                )
-                away = jnp.where(index == 0, 0.5 * base, base)
-            elif i == samples - 1:
-                h0, h1, h2 = (h_last[c, part] for c in range(3))
-            else:
-                h0, h1, h2 = (h[group, c, i - 1] for c in range(3))
-            value = a0 * h0 + a1 * h1 + a2 * h2 - away
-            rows[pl.ds((i // SUB) * step * SUB + i % SUB, step, stride=SUB), :] = value
-        copy(k).start()
-
-    @pl.loop(0, count)
-    def _(k):
-        copy(k).wait()
+        for which in halves:
+            for copy in copies(which, k):
+                copy.wait()
 
 
 def sent(value, axis, pairs):
@@ -247,9 +305,11 @@
             @pl.when(jnp.logical_not(is_own))
             def _():
                 for c in range(4):
-                    out_other[c, part] = values[c]
-
-    out_loss[...] = jnp.full(out_loss.shape, jnp.sum(loss), jnp.float32)
+                    out_other[pl.ds(c * half + at, BLOCKS), :] = values[c]
+
+    loss = jnp.full((SUB, LANES), jnp.sum(loss), jnp.float32)
+    out_other[pl.ds(4 * half, SUB), :] = loss
+    out_loss[...] = loss
 
 
 def stages(count):
@@ -260,8 +320,6 @@
 
 
 def ring_sum(count):
-    if count == 4:
-        return [[[(0, 1), (1, 0), (2, 3), (3, 2)]], [[(1, 2), (2, 1), (3, 0), (0, 3)]]]
     if count & (count - 1) == 0 and count > 1:
         steps = [1 << bit for bit in range(count.bit_length() - 1)]
         return [[[(d, d ^ step) for d in range(count)]] for step in steps]
@@ -292,30 +350,33 @@
 
     row = jax.ShapeDtypeStruct((1, blocks, LANES), f32)
     colors = jax.ShapeDtypeStruct((3, blocks, LANES), f32)
-    edge = jax.ShapeDtypeStruct((4, blocks, LANES), f32)
+    states = jax.ShapeDtypeStruct((4, blocks, LANES), f32)
     whole = pl.BlockSpec(memory_space=pltpu.VMEM)
     stays = pl.BlockSpec(memory_space=pl.ANY)
-    first_row = pl.pallas_call(
+    chain = [p for d in range(1, devices - 1, 2) for p in ((d, d + 1), (d + 1, d))]
+    chain += [(0, devices - 1), (devices - 1, 0)]
+    core_cell, chip_cell = pl.pallas_call(
         edge_kernel,
-        out_shape=edge,
+        out_shape=(row, row),
         in_specs=[stays, stays],
-        out_specs=whole,
-        scratch_shapes=[pltpu.SemaphoreType.DMA((4,))],
+        out_specs=(whole, whole),
+        scratch_shapes=[pltpu.VMEM((2, blocks, LANES), f32), pltpu.SemaphoreType.DMA((2,))],
         compiler_params=pltpu.CompilerParams(vmem_limit_bytes=EDGES),
         name="edge",
     )(density, radiance)
-    behind = sent(first_row, "depth", [(d + 1, d) for d in range(devices - 1)])
+    rim_chip = sent(chip_cell, "depth", chain)
+    rim_core = sent(core_cell, "depth", swap)
 
     step = BLOCKS
     grid = blocks // step
-    h, state, first, last, last_cell, last_colors = pl.pallas_call(
+    h, state, first, last, core_colors, chip_colors = pl.pallas_call(
         slab_kernel,
         out_shape=(
             jax.ShapeDtypeStruct((grid, 3, samples - 2, step, LANES), f32),
-            edge,
+            states,
             colors,
             colors,
-            row,
+            colors,
             colors,
         ),
         in_specs=[whole, whole],
@@ -330,16 +391,17 @@
     )(density, radiance)
 
     part = jax.ShapeDtypeStruct((4, half, LANES), f32)
-    ahead = sent(last_colors, "depth", [(d, d + 1) for d in range(devices - 1)])
-    mine, other, h_last = pl.pallas_call(
+    edge_core = sent(core_colors, "depth", swap)
+    edge_chip = sent(chip_colors, "depth", chain)
+    mine, other, opacity = pl.pallas_call(
         boundary_kernel,
-        out_shape=(part, part, colors),
-        in_specs=[whole] * 5,
+        out_shape=(part, part, row),
+        in_specs=[whole] * 7,
         out_specs=(whole,) * 3,
         scratch_shapes=[pltpu.VMEM((4, blocks, LANES), f32)],
         compiler_params=pltpu.CompilerParams(vmem_limit_bytes=KEPT),
         name="boundary",
-    )(last_cell, last_colors, behind, state, last)
+    )(core_cell, chip_cell, rim_core, rim_chip, core_colors, chip_colors, state)
 
     small = pltpu.CompilerParams(vmem_limit_bytes=SMALL)
     theirs = sent(other, "depth", swap)
@@ -366,7 +428,7 @@
             given = (mine, theirs, goal, *members, *earlier)
             made = (
                 part,
-                part,
+                jax.ShapeDtypeStruct((4 * half + SUB, LANES), f32),
                 jax.ShapeDtypeStruct((SUB, LANES), f32),
             )
         else:
@@ -386,37 +448,44 @@
         stride *= width
     scale_mine, scale_other, loss = results
 
-    def grad_half(own, scales, *before):
+    def grad_part(halves, chosen_tiles, *extra):
+        given = (scale_mine, theirs, h, first, last, state, opacity, core_colors, chip_colors)
+        if 0 in chosen_tiles:
+            given += (edge_core, edge_chip)
+        shape = (len(halves), grid // 2, len(chosen_tiles))
+        share = math.prod(shape)
         return pl.pallas_call(
-            functools.partial(grad_kernel, own),
+            functools.partial(grad_kernel, halves, chosen_tiles),
             out_shape=jax.ShapeDtypeStruct((tiles, blocks, SUB, LANES), f32),
-            in_specs=[whole] * 6 + [stays] * len(before),
+            in_specs=[whole] * len(given) + [stays] * len(extra),
             out_specs=stays,
-            input_output_aliases={6: 0} if before else {},
+            input_output_aliases={len(given): 0} if extra else {},
             scratch_shapes=[
-                pltpu.VMEM((grid // 2, tiles, step, SUB, LANES), f32),
-                pltpu.SemaphoreType.DMA((grid // 2,)),
+                pltpu.VMEM(shape + (step, SUB, LANES), f32),
+                pltpu.SemaphoreType.DMA(shape),
             ],
             compiler_params=pltpu.CompilerParams(vmem_limit_bytes=KEPT),
             cost_estimate=pl.CostEstimate(
-                flops=4 * samples * ray_count,
-                bytes_accessed=8 * samples * ray_count,
+                flops=8 * share * step * SUB * LANES,
+                bytes_accessed=16 * share * step * SUB * LANES,
                 transcendentals=0,
             ),
             name="grad",
-        )(scales, h, first, first_row, ahead, h_last, *before)
-
-    scale_theirs = sent(scale_other, "depth", swap)
+        )(*given, *extra)
+
+    theirs = sent(scale_other, "depth", swap)
     groups = lax.axis_size("rays")
     rounds = ring_sum(groups)
-    for at, pairs in enumerate(rounds):
+    outer_tiles = tuple(sorted({0, tiles - 1}))
+    inner_tiles = tuple(range(1, tiles - 1))
+    grad = ()
+    loss = loss + theirs[4 * half :]
+    for pairs in rounds:
         others = [sent(loss, "rays", pair) for pair in pairs]
-        if at == 0:
-            grad = grad_half(True, scale_mine)
         loss = sum(others, loss)
-        if at == 0:
-            loss = loss + sent(loss, "depth", swap)
-            grad = grad_half(False, scale_theirs, grad)
+    if inner_tiles:
+        grad = (grad_part((0, 1), inner_tiles),)
+    grad = grad_part((0, 1), outer_tiles, *grad)
     grad = jnp.swapaxes(grad, 1, 2).reshape(samples, ray_count)
     return grad, loss[0, 0] / (3.0 * ray_count * groups)
 

time: 36.3 us -> 32.7 us (0.901)
  starting transfers between devices: 16.9 us -> 13.9 us
  local copies, waits for them, and re-layouts: 1.36 us -> 0.54 us
    ppermute x10 -> x11, starting transfers between devices: 16.9 us -> 13.9 us  [sent(): return lax.ppermute(value, axis, pairs)]
    unnamed x7, local copies, waits for them, and re-layouts: 0.84 us -> 0.03 us
    ppermute x10 -> x11, waiting for transfers between devices: 9.09 us -> 9.13 us  [sent(): return lax.ppermute(value, axis, pairs)]
  transfers between devices with their start and end apart: 10 -> 11, of which waited for: 7 -> 4; matrix products, arithmetic and copies ran while one was open for 1% -> 0% of each run, Pallas kernels for 11% -> 15%
where the time goes in v4:
time: 32.7 us; the launch traced here: 32.6 us
  starting transfers between devices  13.9 us (43%)
  waiting for transfers between devices  9.13 us (28%)
  Pallas kernels  6.46 us (20%)
  between operations  2.54 us (8%)
  local copies, waits for them, and re-layouts  0.54 us (2%)
    ppermute x11, starting transfers between devices, sent(): return lax.ppermute(value, axis, pairs)  13.9 us
    ppermute x11, waiting for transfers between devices, sent(): return lax.ppermute(value, axis, pairs)  9.13 us
    pallas_call x1, Pallas kernels, on_device(): pl.pallas_call(slab_kernel, out_shape=(jax.ShapeDtypeStruct((grid, 3, sam...  2.56 us
    pallas_call x2, Pallas kernels, grad_part(): pl.pallas_call(functools.partial(grad_kernel, halves, chosen_tiles), out_...  2.36 us
    pallas_call x1, Pallas kernels, on_device(): pl.pallas_call(edge_kernel, out_shape=(row, row), in_specs=[stays, stays]...  1.06 us
  transfers between devices with their start and end apart: 11, of which 4 were waited for; matrix products, arithmetic and copies ran while one was open for 0% of the time, Pallas kernels for 15%

profile of v4, /device:TPU:0, one launch (start us, length us, event | category | flops | bytes accessed | tf_op | source)
XLA Modules:
  0.0 32.6 jit_solution(11976309658692528683)
XLA Ops:
  0.6 1.1 %edge.1 = (f32[1,128,128]{2,1,0:T(8,128)S(1)}, f32[1,128,128]{2,1,0:T(8,128)S(1)}) custom-call(f32[4,128,8,128]{3,2,1,0:T(8,128)} %bitcast.16, f32[3,4,128,8,128]{4,3,2,1,0:T(8,128)} %bitcast.14), custom_call_target="tpu_custom_call" | custom-call | tf_op jit(solution)/shard_map/edge/pallas_call | solution.py:358
  1.7 0.6 %collective-permute-start = (f32[1,128,128]{2,1,0:T(8,128)S(1)}, f32[1,128,128]{2,1,0:T(8,128)S(1)}, u32[]{:S(2)}, u32[]{:S(2)}) collective-permute-start(f32[1,128,128]{2,1,0:T(8,128)S(1)} %get-tuple-element.16.own_core), channel_id=1, source_target_pairs={{0,4},{4,0},{8,12},{12,8},{16,20},{20,16},{24,28},{28,24},{1,5},{5... | collective-permute-start | bytes 196616 | tf_op jit(solution)/shard_map/ppermute | solution.py:218
  2.3 3.5 %collective-permute-start.1 = (f32[1,128,128]{2,1,0:T(8,128)S(1)}, f32[1,128,128]{2,1,0:T(8,128)S(1)}, u32[]{:S(2)}, u32[]{:S(2)}) collective-permute-start(f32[1,128,128]{2,1,0:T(8,128)S(1)} %get-tuple-element.17.own_chip), channel_id=1, source_target_pairs={{4,8},{8,4},{12,16},{16,12},{20,24},{24,20},{0,28},{28,0},{5,9},{9... | collective-permute-start | bytes 196616 | tf_op jit(solution)/shard_map/ppermute | solution.py:218
  5.8 2.6 %slab.1 = (f32[8,3,30,16,128]{4,3,2,1,0:T(8,128)S(1)}, f32[4,128,128]{2,1,0:T(8,128)S(1)}, f32[3,128,128]{2,1,0:T(8,128)S(1)}, f32[3,128,128]{2,1,0:T(8,128)S(1)...) custom-call(f32[4,128,8,128]{3,2,1,0:T(8,128)S(1)} %bitcast.17, f32[3,4,128,8,128]{4,3,2,1,0:T(8,128)S(1)} %bitcast.15), custom_call_target="tpu_custom_call" | custom-call | flops 20971520 | bytes 8388608 | tf_op jit(solution)/shard_map/slab/pallas_call | solution.py:372
  8.4 0.0 collective-permute-done.rim_core
  8.4 0.0 collective-permute-done.1.rim_chip
  8.4 0.1 boundary.1
  8.6 0.1 collective-permute-start.2
  8.6 1.3 %collective-permute-done.2.theirs = f32[4,64,128]{2,1,0:T(8,128)S(1)} collective-permute-done((f32[4,64,128]{2,1,0:T(8,128)S(1)}, f32[4,64,128]{2,1,0:T(8,128)S(1)}, u32[]{:S(2)}, u32[]{:S(2)}) %collective-permute-start.2) | collective-permute-done | bytes 131104 | tf_op jit(solution)/shard_map/ppermute | solution.py:218
  10.0 2.3 %collective-permute-start.5 = (f32[4,64,128]{2,1,0:T(8,128)S(1)}, f32[4,64,128]{2,1,0:T(8,128)S(1)}, u32[]{:S(2)}, u32[]{:S(2)}) collective-permute-start(f32[4,64,128]{2,1,0:T(8,128)S(1)} %chip.1.refs_0_), channel_id=1, source_target_pairs={{24,0},{28,4},{16,8},{20,12},{8,16},{12,20},{0,24},{4,28},{25,1},{... | collective-permute-start | bytes 393224 | tf_op jit(solution)/shard_map/ppermute | solution.py:218
  12.3 0.5 %collective-permute-start.4 = (f32[4,64,128]{2,1,0:T(8,128)S(1)}, f32[4,64,128]{2,1,0:T(8,128)S(1)}, u32[]{:S(2)}, u32[]{:S(2)}) collective-permute-start(f32[4,64,128]{2,1,0:T(8,128)S(1)} %chip.1.refs_0_), channel_id=1, source_target_pairs={{16,0},{20,4},{24,8},{28,12},{0,16},{4,20},{8,24},{12,28},{17,1},{... | collective-permute-start | bytes 393224 | tf_op jit(solution)/shard_map/ppermute | solution.py:218
  12.8 0.8 %collective-permute-start.3 = (f32[4,64,128]{2,1,0:T(8,128)S(1)}, f32[4,64,128]{2,1,0:T(8,128)S(1)}, u32[]{:S(2)}, u32[]{:S(2)}) collective-permute-start(f32[4,64,128]{2,1,0:T(8,128)S(1)} %chip.1.refs_0_), channel_id=1, source_target_pairs={{8,0},{12,4},{0,8},{4,12},{24,16},{28,20},{16,24},{20,28},{9,1},{1... | collective-permute-start | bytes 393224 | tf_op jit(solution)/shard_map/ppermute | solution.py:218
  13.6 3.5 %collective-permute-done.5.refs_3_ = f32[4,64,128]{2,1,0:T(8,128)S(1)} collective-permute-done((f32[4,64,128]{2,1,0:T(8,128)S(1)}, f32[4,64,128]{2,1,0:T(8,128)S(1)}, u32[]{:S(2)}, u32[]{:S(2)}) %collective-permute-start.5) | collective-permute-done | bytes 131104 | tf_op jit(solution)/shard_map/ppermute | solution.py:218
  17.1 2.2 %collective-permute-done.4.refs_2_ = f32[4,64,128]{2,1,0:T(8,128)S(1)} collective-permute-done((f32[4,64,128]{2,1,0:T(8,128)S(1)}, f32[4,64,128]{2,1,0:T(8,128)S(1)}, u32[]{:S(2)}, u32[]{:S(2)}) %collective-permute-start.4) | collective-permute-done | bytes 131104 | tf_op jit(solution)/shard_map/ppermute | solution.py:218
  19.3 0.3 scale.1
  19.7 0.1 collective-permute-start.6
  19.7 0.5 %collective-permute-start.7 = (f32[3,128,128]{2,1,0:T(8,128)S(1)}, f32[3,128,128]{2,1,0:T(8,128)S(1)}, u32[]{:S(2)}, u32[]{:S(2)}) collective-permute-start(f32[3,128,128]{2,1,0:T(8,128)S(1)} %get-tuple-element.18.core_colors.own_core), channel_id=1, source_target_pairs={{0,4},{4,0},{8,12},{12,8},{16,20},{20,16},{24,28},{28,24},{1,5},{5... | collective-permute-start | bytes 589832 | tf_op jit(solution)/shard_map/ppermute | solution.py:218
  20.2 1.4 %collective-permute-start.8 = (f32[3,128,128]{2,1,0:T(8,128)S(1)}, f32[3,128,128]{2,1,0:T(8,128)S(1)}, u32[]{:S(2)}, u32[]{:S(2)}) collective-permute-start(f32[3,128,128]{2,1,0:T(8,128)S(1)} %get-tuple-element.19.chip_colors.own_chip), channel_id=1, source_target_pairs={{4,8},{8,4},{12,16},{16,12},{20,24},{24,20},{0,28},{28,0},{5,9},{9... | collective-permute-start | bytes 589832 | tf_op jit(solution)/shard_map/ppermute | solution.py:218
  21.7 1.6 %collective-permute-start.9 = (f32[8,128]{1,0:T(8,128)S(1)}, f32[8,128]{1,0:T(8,128)S(1)}, u32[]{:S(2)}, u32[]{:S(2)}) collective-permute-start(f32[8,128]{1,0:T(8,128)S(1)} %slice_add_fusion), channel_id=1, source_target_pairs={{0,1},{1,0},{2,3},{3,2},{4,5},{5,4},{6,7},{7,6},{8,9},{9,8},{10,11... | collective-permute-start | bytes 12296 | tf_op jit(solution)/shard_map/ppermute | solution.py:218
  23.2 2.0 %collective-permute-done.9 = f32[8,128]{1,0:T(8,128)S(1)} collective-permute-done((f32[8,128]{1,0:T(8,128)S(1)}, f32[8,128]{1,0:T(8,128)S(1)}, u32[]{:S(2)}, u32[]{:S(2)}) %collective-permute-start.9) | collective-permute-done | bytes 4128 | tf_op jit(solution)/shard_map/ppermute | solution.py:218
  25.3 2.6 %collective-permute-start.10 = (f32[8,128]{1,0:T(8,128)S(1)}, f32[8,128]{1,0:T(8,128)S(1)}, u32[]{:S(2)}, u32[]{:S(2)}) collective-permute-start(f32[8,128]{1,0:T(8,128)S(1)} %add.10), channel_id=1, source_target_pairs={{0,2},{1,3},{2,0},{3,1},{4,6},{5,7},{6,4},{7,5},{8,10},{9,11},{10,... | collective-permute-start | bytes 12296 | tf_op jit(solution)/shard_map/ppermute | solution.py:218
  27.9 1.1 %grad.2.refs_2_ = f32[4,128,8,128]{3,2,1,0:T(8,128)} custom-call(f32[4,64,128]{2,1,0:T(8,128)S(1)} %get-tuple-element.23.mine, f32[264,128]{1,0:T(8,128)S(1)} %collective-permute-done.6.theirs, f32[8,3,30,16,128]{4,3,2,1,0:T(8,128)S(1)} %get-tuple-element.25.h, f32[3,128,128]{2,1,0:T(8,128)S(1)} %get-tuple-element.26.first, ...), custom_call_target="tpu_custom_call" | custom-call | flops 2097152 | bytes 4194304 | tf_op jit(solution)/shard_map/grad/pallas_call | solution.py:457
  29.0 1.2 %grad.3 = f32[4,128,8,128]{3,2,1,0:T(8,128)} custom-call(f32[4,64,128]{2,1,0:T(8,128)S(1)} %get-tuple-element.23.mine, f32[264,128]{1,0:T(8,128)S(1)} %collective-permute-done.6.theirs, f32[8,3,30,16,128]{4,3,2,1,0:T(8,128)S(1)} %get-tuple-element.25.h, f32[3,128,128]{2,1,0:T(8,128)S(1)} %get-tuple-element.26.first, ...), custom_call_target="tpu_custom_call", output_to_operand_aliasing={{}: (11, {})} | custom-call | flops 2097152 | bytes 4194304 | tf_op jit(solution)/shard_map/grad/pallas_call | solution.py:457
  30.3 0.5 %slice.7 = f32[1,1]{1,0:T(1,128)} slice(f32[8,128]{1,0:T(8,128)S(1)} %add.11), slice={[0:1], [0:1]} | slice | bytes 8 | tf_op jit(solution)/shard_map/slice | solution.py:490
  (16 shorter events, 0.1 us)
Async XLA Ops:
  0.6 5.2 %copy-start = (f32[3,32,16384]{2,1,0:T(8,128)S(1)}, f32[3,32,16384]{2,1,0:T(8,128)}, u32[]{:S(2)}) copy-start(f32[3,32,16384]{2,1,0:T(8,128)} %param.4) | copy-start | bytes 18874372
  0.6 5.2 %copy-start.1 = (f32[32,16384]{1,0:T(8,128)S(1)}, f32[32,16384]{1,0:T(8,128)}, u32[]{:S(2)}) copy-start(f32[32,16384]{1,0:T(8,128)} %param.3) | copy-start | bytes 6291460
  1.7 6.7 %collective-permute-start = (f32[1,128,128]{2,1,0:T(8,128)S(1)}, f32[1,128,128]{2,1,0:T(8,128)S(1)}, u32[]{:S(2)}, u32[]{:S(2)}) collective-permute-start(f32[1,128,128]{2,1,0:T(8,128)S(1)} %get-tuple-element.16.own_core), channel_id=1, source_target_pairs={{0,4},{4,0},{8,12},{12,8},{16,20},{20,16},{24,28},{28,24},{1,5},{5... | collective-permute-start | bytes 196616 | tf_op jit(solution)/shard_map/ppermute | solution.py:218
  2.3 11.3 %copy-start.2 = (f32[3,16384]{1,0:T(4,128)S(1)}, f32[3,16384]{1,0:T(4,128)}, u32[]{:S(2)}) copy-start(f32[3,16384]{1,0:T(4,128)} %param.5) | copy-start | bytes 589828
  2.3 6.1 %collective-permute-start.1 = (f32[1,128,128]{2,1,0:T(8,128)S(1)}, f32[1,128,128]{2,1,0:T(8,128)S(1)}, u32[]{:S(2)}, u32[]{:S(2)}) collective-permute-start(f32[1,128,128]{2,1,0:T(8,128)S(1)} %get-tuple-element.17.own_chip), channel_id=1, source_target_pairs={{4,8},{8,4},{12,16},{16,12},{20,24},{24,20},{0,28},{28,0},{5,9},{9... | collective-permute-start | bytes 196616 | tf_op jit(solution)/shard_map/ppermute | solution.py:218
  8.6 1.4 %collective-permute-start.2 = (f32[4,64,128]{2,1,0:T(8,128)S(1)}, f32[4,64,128]{2,1,0:T(8,128)S(1)}, u32[]{:S(2)}, u32[]{:S(2)}) collective-permute-start(f32[4,64,128]{2,1,0:T(8,128)S(1)} %get-tuple-element.22), channel_id=1, source_target_pairs={{0,4},{4,0},{8,12},{12,8},{16,20},{20,16},{24,28},{28,24},{1,5},{5... | collective-permute-start | bytes 393224 | tf_op jit(solution)/shard_map/ppermute | solution.py:218
  10.0 7.1 %collective-permute-start.5 = (f32[4,64,128]{2,1,0:T(8,128)S(1)}, f32[4,64,128]{2,1,0:T(8,128)S(1)}, u32[]{:S(2)}, u32[]{:S(2)}) collective-permute-start(f32[4,64,128]{2,1,0:T(8,128)S(1)} %chip.1.refs_0_), channel_id=1, source_target_pairs={{24,0},{28,4},{16,8},{20,12},{8,16},{12,20},{0,24},{4,28},{25,1},{... | collective-permute-start | bytes 393224 | tf_op jit(solution)/shard_map/ppermute | solution.py:218
  12.3 7.1 %collective-permute-start.4 = (f32[4,64,128]{2,1,0:T(8,128)S(1)}, f32[4,64,128]{2,1,0:T(8,128)S(1)}, u32[]{:S(2)}, u32[]{:S(2)}) collective-permute-start(f32[4,64,128]{2,1,0:T(8,128)S(1)} %chip.1.refs_0_), channel_id=1, source_target_pairs={{16,0},{20,4},{24,8},{28,12},{0,16},{4,20},{8,24},{12,28},{17,1},{... | collective-permute-start | bytes 393224 | tf_op jit(solution)/shard_map/ppermute | solution.py:218
  12.8 6.5 %collective-permute-start.3 = (f32[4,64,128]{2,1,0:T(8,128)S(1)}, f32[4,64,128]{2,1,0:T(8,128)S(1)}, u32[]{:S(2)}, u32[]{:S(2)}) collective-permute-start(f32[4,64,128]{2,1,0:T(8,128)S(1)} %chip.1.refs_0_), channel_id=1, source_target_pairs={{8,0},{12,4},{0,8},{4,12},{24,16},{28,20},{16,24},{20,28},{9,1},{1... | collective-permute-start | bytes 393224 | tf_op jit(solution)/shard_map/ppermute | solution.py:218
  19.7 2.0 %collective-permute-start.6 = (f32[264,128]{1,0:T(8,128)S(1)}, f32[264,128]{1,0:T(8,128)S(1)}, u32[]{:S(2)}, u32[]{:S(2)}) collective-permute-start(f32[264,128]{1,0:T(8,128)S(1)} %get-tuple-element.24), channel_id=1, source_target_pairs={{0,4},{4,0},{8,12},{12,8},{16,20},{20,16},{24,28},{28,24},{1,5},{5... | collective-permute-start | bytes 405512 | tf_op jit(solution)/shard_map/ppermute | solution.py:218
  19.7 9.3 %collective-permute-start.7 = (f32[3,128,128]{2,1,0:T(8,128)S(1)}, f32[3,128,128]{2,1,0:T(8,128)S(1)}, u32[]{:S(2)}, u32[]{:S(2)}) collective-permute-start(f32[3,128,128]{2,1,0:T(8,128)S(1)} %get-tuple-element.18.core_colors.own_core), channel_id=1, source_target_pairs={{0,4},{4,0},{8,12},{12,8},{16,20},{20,16},{24,28},{28,24},{1,5},{5... | collective-permute-start | bytes 589832 | tf_op jit(solution)/shard_map/ppermute | solution.py:218
  20.2 8.8 %collective-permute-start.8 = (f32[3,128,128]{2,1,0:T(8,128)S(1)}, f32[3,128,128]{2,1,0:T(8,128)S(1)}, u32[]{:S(2)}, u32[]{:S(2)}) collective-permute-start(f32[3,128,128]{2,1,0:T(8,128)S(1)} %get-tuple-element.19.chip_colors.own_chip), channel_id=1, source_target_pairs={{4,8},{8,4},{12,16},{16,12},{20,24},{24,20},{0,28},{28,0},{5,9},{9... | collective-permute-start | bytes 589832 | tf_op jit(solution)/shard_map/ppermute | solution.py:218
  21.7 3.6 %collective-permute-start.9 = (f32[8,128]{1,0:T(8,128)S(1)}, f32[8,128]{1,0:T(8,128)S(1)}, u32[]{:S(2)}, u32[]{:S(2)}) collective-permute-start(f32[8,128]{1,0:T(8,128)S(1)} %slice_add_fusion), channel_id=1, source_target_pairs={{0,1},{1,0},{2,3},{3,2},{4,5},{5,4},{6,7},{7,6},{8,9},{9,8},{10,11... | collective-permute-start | bytes 12296 | tf_op jit(solution)/shard_map/ppermute | solution.py:218
  25.3 5.0 %collective-permute-start.10 = (f32[8,128]{1,0:T(8,128)S(1)}, f32[8,128]{1,0:T(8,128)S(1)}, u32[]{:S(2)}, u32[]{:S(2)}) collective-permute-start(f32[8,128]{1,0:T(8,128)S(1)} %add.10), channel_id=1, source_target_pairs={{0,2},{1,3},{2,0},{3,1},{4,6},{5,7},{6,4},{7,5},{8,10},{9,11},{10,... | collective-permute-start | bytes 12296 | tf_op jit(solution)/shard_map/ppermute | solution.py:218

commit v5 on v4

--- a/solution.py
+++ b/solution.py
@@ -50,33 +50,45 @@
     to_chip[0] = jnp.where(even, rows[0], rows[1])
 
 
-def slab_kernel(density, radiance, out_h, out_state, out_first, out_last, to_core, to_chip):
+def opacity_kernel(density, out):
     tiles, blocks = density.shape[0], density.shape[1]
+    rows = density.reshape(tiles * blocks * SUB, LANES)
+
+    @pl.loop(0, blocks // BLOCKS)
+    def _(g):
+        def cell(i):
+            base = pl.multiple_of(g * (BLOCKS * SUB), SUB) + (i // SUB) * blocks * SUB + i % SUB
+            return rows[pl.ds(base, BLOCKS, stride=SUB), :]
+
+        here = cell(0)
+        for i in range(tiles * SUB - 1):
+            after = cell(i + 1)
+            out[g, i] = opacity_of(here + after)
+            here = after
+
+
+def slab_kernel(opacities, radiance, out_g, out_state, to_core, to_chip):
+    tiles, blocks = radiance.shape[1], radiance.shape[2]
     samples = tiles * SUB
     step = BLOCKS
-    rows = density.reshape(tiles * blocks * SUB, LANES)
     planes = radiance.reshape(3 * tiles * blocks * SUB, LANES)
+    even = is_even()
 
     @pl.loop(0, blocks // step)
     def _(g):
         part = pl.ds(pl.multiple_of(g * step, step), step)
 
-        def cell(ref, plane, i):
-            base = (plane * tiles + i // SUB) * blocks * SUB + i % SUB
+        def color_of(c, i):
+            base = (c * tiles + i // SUB) * blocks * SUB + i % SUB
             base = pl.multiple_of(g * (step * SUB), SUB) + base
-            return ref[pl.ds(base, step, stride=SUB), :]
-
-        here = cell(rows, 0, 0)
-        color_here = [cell(planes, c, 0) for c in range(3)]
-        even = is_even()
+            return planes[pl.ds(base, step, stride=SUB), :]
+
+        color_here = [color_of(c, 0) for c in range(3)]
         color_first = list(color_here)
         transmit = None
         prefix = [None] * 3
-        before = [None] * 3
         for i in range(samples - 1):
-            after = cell(rows, 0, i + 1)
-            opacity = opacity_of(here + after)
-            here = after
+            opacity = opacities[g, i]
             if i == 0:
                 weight = opacity
                 transmit = 1.0 - opacity
@@ -84,21 +96,15 @@
                 weight = transmit * opacity
                 transmit = transmit - weight
             for c in range(3):
-                next_color = cell(planes, c, i + 1)
+                next_color = color_of(c, i + 1)
                 color = color_here[c] + next_color
                 color_here[c] = next_color
                 seen = weight * color
                 prefix[c] = seen if i == 0 else prefix[c] + seen
-                value = transmit * color + prefix[c]
-                if i == 0:
-                    out_first[c, part] = value
-                else:
-                    out_h[g, c, i - 1] = value + before[c]
-                before[c] = value
+                out_g[g, c, i] = transmit * color + prefix[c]
         out_state[0, part] = transmit
         for c in range(3):
             out_state[1 + c, part] = prefix[c]
-            out_last[c, part] = before[c]
             to_core[c, part] = jnp.where(even, color_here[c], color_first[c])
             to_chip[c, part] = jnp.where(even, color_first[c], color_here[c])
 
@@ -131,87 +137,91 @@
     other[...] = full[:, pl.ds(pl.multiple_of((1 - parity) * half, SUB), half), :]
 
 
-def grad_kernel(
-    halves, groups, mine, theirs, h, first, last, state, opacity, own_core, own_chip, *refs
-):
+def ends_kernel(mine, theirs, state, opacity, own_core, own_chip, gains, to_core, to_chip):
+    half = mine.shape[1]
+    parity = lax.rem(lax.axis_index("depth"), 2)
+    even = parity == 0
+    for scales, place in ((mine, parity), (theirs, 1 - parity)):
+        for at in range(0, half, BLOCKS):
+            inside = pl.ds(at, BLOCKS)
+            part = pl.ds(pl.multiple_of(place * half + at, SUB), BLOCKS)
+            ahead = opacity[0, part]
+            through = 1.0 - ahead
+            first = last = 0.0
+            for c in range(3):
+                scale = scales[c, inside]
+                core, chip = own_core[c, part], own_chip[c, part]
+                first = first + scale * jnp.where(even, chip, core)
+                scale = through * scale
+                last = last + scale * jnp.where(even, core, chip)
+                gains[c, part] = scale
+            gains[3, part] = 0.5 * scales[3, inside] - ahead * first
+            last = state[0, part] * last
+            to_core[0, part] = jnp.where(even, last, first)
+            to_chip[0, part] = jnp.where(even, first, last)
+
+
+def mean_kernel(scale, *refs):
+    total = sum(ref[0, 0] for ref in refs[:-1])
+    refs[-1][0, 0] = total * scale
+
+
+def grad_kernel(groups, gains, values, *refs):
     out, buffers, sems = refs[-3:]
-    edges = 0 in groups
-    if edges:
-        rim_core, rim_chip = refs[:2]
+    if 0 in groups:
+        state, opacity, own_core, own_chip, rim_core, rim_chip = refs[:6]
     tiles, blocks = out.shape[0], out.shape[1]
     samples = tiles * SUB
-    half = blocks // 2
     step = BLOCKS
     index = lax.axis_index("depth")
-    parity = lax.rem(index, 2)
-    even = parity == 0
-    count = half // step
-
-    def copies(which, k):
-        start = pl.multiple_of((parity if which == 0 else 1 - parity) * half, step)
-        part = pl.ds(pl.multiple_of(start + k * step, step), step)
+    even = lax.rem(index, 2) == 0
+    ends = index == lax.axis_size("depth") - 1
+    count = blocks // step
+
+    def copies(k):
+        part = pl.ds(pl.multiple_of(k * step, step), step)
         return [
-            pltpu.make_async_copy(
-                buffers.at[at, k, place], out.at[group, part], sems.at[at, k, place]
-            )
-            for at, whose in enumerate(halves)
-            if whose == which
+            pltpu.make_async_copy(buffers.at[k, place], out.at[group, part], sems.at[k, place])
             for place, group in enumerate(groups)
         ]
 
-    def piece(which, k):
-        start = pl.multiple_of((parity if which == 0 else 1 - parity) * half, step)
-        inside = pl.multiple_of(k * step, step)
-        part = pl.ds(pl.multiple_of(start + k * step, step), step)
-        slot = lax.div(start, step) + k
-        if which == 0:
-            a0, a1, a2, base = (mine[c, pl.ds(inside, step)] for c in range(4))
-        else:
-            a0, a1, a2, base = (theirs[pl.ds(c * half + inside, step), :] for c in range(4))
-        ahead = opacity[0, part]
-        core = [own_core[c, part] for c in range(3)]
-        chip = [own_chip[c, part] for c in range(3)]
-        opening = [jnp.where(even, chip[c], core[c]) for c in range(3)]
-        base = base - 2.0 * ahead * (a0 * opening[0] + a1 * opening[1] + a2 * opening[2])
-        through = 1.0 - ahead
-        a0, a1, a2 = through * a0, through * a1, through * a2
-        if edges:
-            of_core = [core[c] + rim_core[c, part] for c in range(3)]
-            ends = index == lax.axis_size("depth") - 1
-            of_chip = [chip[c] + jnp.where(ends, 0.0, rim_chip[c, part]) for c in range(3)]
-        for place, group in enumerate(groups):
-            rows = buffers.at[halves.index(which), k, place].reshape(step * SUB, LANES)
-            for i in range(group * SUB, (group + 1) * SUB):
-                away = base
-                if i == 0:
-                    h0, h1, h2 = (
-                        first[c, part]
-                        + jnp.where(index == 0, 0.0, jnp.where(even, of_chip[c], of_core[c]))
-                        for c in range(3)
-                    )
-                    away = jnp.where(index == 0, 0.5 * base, base)
-                elif i == samples - 1:
-                    h0, h1, h2 = (
-                        last[c, part]
-                        + state[1 + c, part]
-                        + state[0, part] * jnp.where(even, of_core[c], of_chip[c])
-                        for c in range(3)
-                    )
-                else:
-                    h0, h1, h2 = (h[slot, c, i - 1] for c in range(3))
-                value = a0 * h0 + a1 * h1 + a2 * h2 - away
-                rows[pl.ds(i % SUB, step, stride=SUB), :] = value
-        for copy in copies(which, k):
-            copy.start()
-
-    for which in halves:
-        pl.loop(0, count)(functools.partial(piece, which))
-
     @pl.loop(0, count)
     def _(k):
-        for which in halves:
-            for copy in copies(which, k):
-                copy.wait()
+        part = pl.ds(pl.multiple_of(k * step, step), step)
+        a0, a1, a2, base = (gains[c, part] for c in range(4))
+
+        def sample(i):
+            if i < 0:
+                ahead = jnp.where(
+                    even, own_chip[0, part] + rim_chip[0, part], own_core[0, part] + rim_core[0, part]
+                )
+                return jnp.where(index == 0, 0.0, (1.0 - opacity[0, part]) * ahead - base)
+            if i < samples - 1:
+                v0, v1, v2 = (values[k, c, i] for c in range(3))
+                return a0 * v0 + a1 * v1 + a2 * v2 - base
+            behind = jnp.where(
+                even,
+                own_core[0, part] + rim_core[0, part],
+                own_chip[0, part] + jnp.where(ends, 0.0, rim_chip[0, part]),
+            )
+            v0, v1, v2 = (state[1 + c, part] for c in range(3))
+            return a0 * v0 + a1 * v1 + a2 * v2 + behind - base
+
+        for place, group in enumerate(groups):
+            rows = buffers.at[k, place].reshape(step * SUB, LANES)
+            if place == 0 or groups[place - 1] != group - 1:
+                before = sample(group * SUB - 1)
+            for i in range(group * SUB, (group + 1) * SUB):
+                here = sample(i)
+                rows[pl.ds(i % SUB, step, stride=SUB), :] = here + before
+                before = here
+        for copy in copies(k):
+            copy.start()
+
+    @pl.loop(0, count)
+    def _(k):
+        for copy in copies(k):
+            copy.wait()
 
 
 def sent(value, axis, pairs):
@@ -305,11 +315,9 @@
             @pl.when(jnp.logical_not(is_own))
             def _():
                 for c in range(4):
-                    out_other[pl.ds(c * half + at, BLOCKS), :] = values[c]
-
-    loss = jnp.full((SUB, LANES), jnp.sum(loss), jnp.float32)
-    out_other[pl.ds(4 * half, SUB), :] = loss
-    out_loss[...] = loss
+                    out_other[c, part] = values[c]
+
+    out_loss[...] = jnp.full(out_loss.shape, jnp.sum(loss), jnp.float32)
 
 
 def stages(count):
@@ -321,7 +329,7 @@
 
 def ring_sum(count):
     if count & (count - 1) == 0 and count > 1:
-        steps = [1 << bit for bit in range(count.bit_length() - 1)]
+        steps = [1 << bit for bit in reversed(range(count.bit_length() - 1))]
         return [[[(d, d ^ step) for d in range(count)]] for step in steps]
     return [[[(d, (d + k) % count) for d in range(count)] for k in range(1, count)]]
 
@@ -369,30 +377,39 @@
 
     step = BLOCKS
     grid = blocks // step
-    h, state, first, last, core_colors, chip_colors = pl.pallas_call(
+    opacities = pl.pallas_call(
+        opacity_kernel,
+        out_shape=jax.ShapeDtypeStruct((grid, samples - 1, step, LANES), f32),
+        in_specs=[whole],
+        out_specs=whole,
+        compiler_params=pltpu.CompilerParams(vmem_limit_bytes=KEPT),
+        cost_estimate=pl.CostEstimate(
+            flops=12 * samples * ray_count,
+            bytes_accessed=8 * samples * ray_count,
+            transcendentals=0,
+        ),
+        name="opacity",
+    )(density)
+    values, state, core_colors, chip_colors = pl.pallas_call(
         slab_kernel,
         out_shape=(
-            jax.ShapeDtypeStruct((grid, 3, samples - 2, step, LANES), f32),
+            jax.ShapeDtypeStruct((grid, 3, samples - 1, step, LANES), f32),
             states,
-            colors,
-            colors,
             colors,
             colors,
         ),
         in_specs=[whole, whole],
-        out_specs=(whole,) * 6,
+        out_specs=(whole,) * 4,
         compiler_params=pltpu.CompilerParams(vmem_limit_bytes=KEPT),
         cost_estimate=pl.CostEstimate(
-            flops=40 * samples * ray_count,
-            bytes_accessed=16 * samples * ray_count,
+            flops=28 * samples * ray_count,
+            bytes_accessed=28 * samples * ray_count,
             transcendentals=0,
         ),
         name="slab",
-    )(density, radiance)
+    )(opacities, radiance)
 
     part = jax.ShapeDtypeStruct((4, half, LANES), f32)
-    edge_core = sent(core_colors, "depth", swap)
-    edge_chip = sent(chip_colors, "depth", chain)
     mine, other, opacity = pl.pallas_call(
         boundary_kernel,
         out_shape=(part, part, row),
@@ -428,7 +445,7 @@
             given = (mine, theirs, goal, *members, *earlier)
             made = (
                 part,
-                jax.ShapeDtypeStruct((4 * half + SUB, LANES), f32),
+                part,
                 jax.ShapeDtypeStruct((SUB, LANES), f32),
             )
         else:
@@ -448,14 +465,33 @@
         stride *= width
     scale_mine, scale_other, loss = results
 
-    def grad_part(halves, chosen_tiles, *extra):
-        given = (scale_mine, theirs, h, first, last, state, opacity, core_colors, chip_colors)
+    groups = lax.axis_size("rays")
+    rounds = ring_sum(groups)
+
+    def rays_sum(at, value):
+        return sum((sent(value, "rays", pairs) for pairs in rounds[at]), value)
+
+    theirs = sent(scale_other, "depth", swap)
+    loss = rays_sum(0, loss)
+    gains, core_end, chip_end = pl.pallas_call(
+        ends_kernel,
+        out_shape=(states, row, row),
+        in_specs=[whole] * 6,
+        out_specs=(whole,) * 3,
+        compiler_params=small,
+        name="ends",
+    )(scale_mine, theirs, state, opacity, core_colors, chip_colors)
+    rim_end_chip = sent(chip_end, "depth", chain)
+    rim_end_core = sent(core_end, "depth", swap)
+
+    def grad_part(chosen_tiles, *extra):
+        given = (gains, values)
         if 0 in chosen_tiles:
-            given += (edge_core, edge_chip)
-        shape = (len(halves), grid // 2, len(chosen_tiles))
+            given += (state, opacity, core_end, chip_end, rim_end_core, rim_end_chip)
+        shape = (grid, len(chosen_tiles))
         share = math.prod(shape)
         return pl.pallas_call(
-            functools.partial(grad_kernel, halves, chosen_tiles),
+            functools.partial(grad_kernel, chosen_tiles),
             out_shape=jax.ShapeDtypeStruct((tiles, blocks, SUB, LANES), f32),
             in_specs=[whole] * len(given) + [stays] * len(extra),
             out_specs=stays,
@@ -473,21 +509,27 @@
             name="grad",
         )(*given, *extra)
 
-    theirs = sent(scale_other, "depth", swap)
-    groups = lax.axis_size("rays")
-    rounds = ring_sum(groups)
     outer_tiles = tuple(sorted({0, tiles - 1}))
     inner_tiles = tuple(range(1, tiles - 1))
-    grad = ()
-    loss = loss + theirs[4 * half :]
-    for pairs in rounds:
-        others = [sent(loss, "rays", pair) for pair in pairs]
-        loss = sum(others, loss)
-    if inner_tiles:
-        grad = (grad_part((0, 1), inner_tiles),)
-    grad = grad_part((0, 1), outer_tiles, *grad)
+    grad = (grad_part(inner_tiles),) if inner_tiles else ()
+    grad = grad_part(outer_tiles, *grad)
+    loss = loss + sent(loss, "depth", swap)
+    for at in range(1, len(rounds) - 1):
+        loss = rays_sum(at, loss)
+    squares = [loss]
+    if len(rounds) > 1:
+        squares += [sent(loss, "rays", pairs) for pairs in rounds[-1]]
+    scale = 1.0 / (3.0 * ray_count * groups)
+    mean = pl.pallas_call(
+        functools.partial(mean_kernel, scale),
+        out_shape=jax.ShapeDtypeStruct((1, 1), f32),
+        in_specs=[whole] * len(squares),
+        out_specs=pl.BlockSpec(memory_space=pltpu.SMEM),
+        compiler_params=small,
+        name="mean",
+    )(*squares)
     grad = jnp.swapaxes(grad, 1, 2).reshape(samples, ray_count)
-    return grad, loss[0, 0] / (3.0 * ray_count * groups)
+    return grad, mean[0, 0]
 
 
 def solution(mesh):

time: 32.7 us -> 35.4 us (1.083)
  waiting for transfers between devices: 9.13 us -> 13.5 us
  between operations: 2.54 us -> 0.8 us
  local copies, waits for them, and re-layouts: 0.54 us -> 0.03 us
  Pallas kernels: 6.46 us -> 6.96 us
    ppermute x11 -> x12, waiting for transfers between devices: 9.13 us -> 13.5 us  [sent(): return lax.ppermute(value, axis, pairs)]
    pallas_call x2 -> x5, Pallas kernels: 2.36 us -> 3.96 us  [the longest x2 2.33 us: grad_part(): pl.pallas_call(functools.partial(grad_kernel, chosen_tiles), out_shape=ja...]
    pallas_call x1, Pallas kernels: 2.56 us -> 1.45 us  [on_device(): pl.pallas_call(slab_kernel, out_shape=(jax.ShapeDtypeStruct((grid, 3, sam...]
    slice x1 -> x0, local copies, waits for them, and re-layouts: 0.51 us -> none  [on_device(): return (grad, loss[0, 0] / (3.0 * ray_count * groups))]
    ppermute x11 -> x12, starting transfers between devices: 13.9 us -> 13.9 us  [sent(): return lax.ppermute(value, axis, pairs)]
  transfers between devices with their start and end apart: 11 -> 12, of which waited for: 4 -> 7; matrix products, arithmetic and copies ran while one was open for 0% -> 0% of each run, Pallas kernels for 15% -> 12%
where the time goes in v5:
time: 35.4 us; the launch traced here: 35.2 us
  starting transfers between devices  13.9 us (39%)
  waiting for transfers between devices  13.5 us (38%)
  Pallas kernels  6.96 us (20%)
  between operations  0.8 us (2%)
    ppermute x12, starting transfers between devices, sent(): return lax.ppermute(value, axis, pairs)  13.9 us
    ppermute x12, waiting for transfers between devices, sent(): return lax.ppermute(value, axis, pairs)  13.5 us
    pallas_call x2, Pallas kernels, grad_part(): pl.pallas_call(functools.partial(grad_kernel, chosen_tiles), out_shape=ja...  2.33 us
    pallas_call x1, Pallas kernels, on_device(): pl.pallas_call(slab_kernel, out_shape=(jax.ShapeDtypeStruct((grid, 3, sam...  1.45 us
    pallas_call x1, Pallas kernels, on_device(): pl.pallas_call(edge_kernel, out_shape=(row, row), in_specs=[stays, stays]...  1.07 us
    pallas_call x1, Pallas kernels, on_device(): pl.pallas_call(opacity_kernel, out_shape=jax.ShapeDtypeStruct((grid, samp...  1.01 us
  transfers between devices with their start and end apart: 12, of which 7 were waited for; matrix products, arithmetic and copies ran while one was open for 0% of the time, Pallas kernels for 12%

profile of v5, /device:TPU:0, one launch (start us, length us, event | category | flops | bytes accessed | tf_op | source)
XLA Modules:
  0.0 35.2 jit_solution(15165053991471349833)
XLA Ops:
  0.7 1.1 %edge.1 = (f32[1,128,128]{2,1,0:T(8,128)S(1)}, f32[1,128,128]{2,1,0:T(8,128)S(1)}) custom-call(f32[4,128,8,128]{3,2,1,0:T(8,128)} %bitcast.18, f32[3,4,128,8,128]{4,3,2,1,0:T(8,128)} %bitcast.14), custom_call_target="tpu_custom_call" | custom-call | tf_op jit(solution)/shard_map/edge/pallas_call | solution.py:366
  1.7 0.6 %collective-permute-start = (f32[1,128,128]{2,1,0:T(8,128)S(1)}, f32[1,128,128]{2,1,0:T(8,128)S(1)}, u32[]{:S(2)}, u32[]{:S(2)}) collective-permute-start(f32[1,128,128]{2,1,0:T(8,128)S(1)} %get-tuple-element.17.own_core), channel_id=1, source_target_pairs={{0,4},{4,0},{8,12},{12,8},{16,20},{20,16},{24,28},{28,24},{1,5},{5... | collective-permute-start | bytes 196616 | tf_op jit(solution)/shard_map/ppermute | solution.py:228
  2.3 3.5 %collective-permute-start.1 = (f32[1,128,128]{2,1,0:T(8,128)S(1)}, f32[1,128,128]{2,1,0:T(8,128)S(1)}, u32[]{:S(2)}, u32[]{:S(2)}) collective-permute-start(f32[1,128,128]{2,1,0:T(8,128)S(1)} %get-tuple-element.18.own_chip), channel_id=1, source_target_pairs={{4,8},{8,4},{12,16},{16,12},{20,24},{24,20},{0,28},{28,0},{5,9},{9... | collective-permute-start | bytes 196616 | tf_op jit(solution)/shard_map/ppermute | solution.py:228
  5.8 1.0 %opacity.1.opacities = f32[8,31,16,128]{3,2,1,0:T(8,128)S(1)} custom-call(f32[4,128,8,128]{3,2,1,0:T(8,128)S(1)} %bitcast.19), custom_call_target="tpu_custom_call" | custom-call | flops 6291456 | bytes 4194304 | tf_op jit(solution)/shard_map/opacity/pallas_call | solution.py:380
  6.9 1.4 %slab.1 = (f32[8,3,31,16,128]{4,3,2,1,0:T(8,128)S(1)}, f32[4,128,128]{2,1,0:T(8,128)S(1)}, f32[3,128,128]{2,1,0:T(8,128)S(1)}, f32[3,128,128]{2,1,0:T(8,128)S(1)}) custom-call(f32[8,31,16,128]{3,2,1,0:T(8,128)S(1)} %opacity.1.opacities, f32[3,4,128,8,128]{4,3,2,1,0:T(8,128)S(1)} %bitcast.17), custom_call_target="tpu_custom_call" | custom-call | flops 14680064 | bytes 14680064 | tf_op jit(solution)/shard_map/slab/pallas_call | solution.py:393
  8.4 0.1 boundary.1
  8.6 1.3 %collective-permute-done.2.theirs = f32[4,64,128]{2,1,0:T(8,128)S(1)} collective-permute-done((f32[4,64,128]{2,1,0:T(8,128)S(1)}, f32[4,64,128]{2,1,0:T(8,128)S(1)}, u32[]{:S(2)}, u32[]{:S(2)}) %collective-permute-start.2) | collective-permute-done | bytes 131104 | tf_op jit(solution)/shard_map/ppermute | solution.py:228
  10.0 2.1 %collective-permute-start.5 = (f32[4,64,128]{2,1,0:T(8,128)S(1)}, f32[4,64,128]{2,1,0:T(8,128)S(1)}, u32[]{:S(2)}, u32[]{:S(2)}) collective-permute-start(f32[4,64,128]{2,1,0:T(8,128)S(1)} %chip.1.refs_0_), channel_id=1, source_target_pairs={{24,0},{28,4},{16,8},{20,12},{8,16},{12,20},{0,24},{4,28},{25,1},{... | collective-permute-start | bytes 393224 | tf_op jit(solution)/shard_map/ppermute | solution.py:228
  12.1 0.7 %collective-permute-start.4 = (f32[4,64,128]{2,1,0:T(8,128)S(1)}, f32[4,64,128]{2,1,0:T(8,128)S(1)}, u32[]{:S(2)}, u32[]{:S(2)}) collective-permute-start(f32[4,64,128]{2,1,0:T(8,128)S(1)} %chip.1.refs_0_), channel_id=1, source_target_pairs={{16,0},{20,4},{24,8},{28,12},{0,16},{4,20},{8,24},{12,28},{17,1},{... | collective-permute-start | bytes 393224 | tf_op jit(solution)/shard_map/ppermute | solution.py:228
  12.8 0.8 %collective-permute-start.3 = (f32[4,64,128]{2,1,0:T(8,128)S(1)}, f32[4,64,128]{2,1,0:T(8,128)S(1)}, u32[]{:S(2)}, u32[]{:S(2)}) collective-permute-start(f32[4,64,128]{2,1,0:T(8,128)S(1)} %chip.1.refs_0_), channel_id=1, source_target_pairs={{8,0},{12,4},{0,8},{4,12},{24,16},{28,20},{16,24},{20,28},{9,1},{1... | collective-permute-start | bytes 393224 | tf_op jit(solution)/shard_map/ppermute | solution.py:228
  13.5 3.4 %collective-permute-done.5.refs_3_ = f32[4,64,128]{2,1,0:T(8,128)S(1)} collective-permute-done((f32[4,64,128]{2,1,0:T(8,128)S(1)}, f32[4,64,128]{2,1,0:T(8,128)S(1)}, u32[]{:S(2)}, u32[]{:S(2)}) %collective-permute-start.5) | collective-permute-done | bytes 131104 | tf_op jit(solution)/shard_map/ppermute | solution.py:228
  17.0 2.3 %collective-permute-done.4.refs_2_ = f32[4,64,128]{2,1,0:T(8,128)S(1)} collective-permute-done((f32[4,64,128]{2,1,0:T(8,128)S(1)}, f32[4,64,128]{2,1,0:T(8,128)S(1)}, u32[]{:S(2)}, u32[]{:S(2)}) %collective-permute-start.4) | collective-permute-done | bytes 131104 | tf_op jit(solution)/shard_map/ppermute | solution.py:228
  19.3 0.3 scale.1
  19.7 1.3 %collective-permute-done.6.theirs = f32[4,64,128]{2,1,0:T(8,128)S(1)} collective-permute-done((f32[4,64,128]{2,1,0:T(8,128)S(1)}, f32[4,64,128]{2,1,0:T(8,128)S(1)}, u32[]{:S(2)}, u32[]{:S(2)}) %collective-permute-start.6) | collective-permute-done | bytes 131104 | tf_op jit(solution)/shard_map/ppermute | solution.py:228
  21.1 0.2 collective-permute-start.7
  21.3 1.7 %collective-permute-start.8 = (f32[1,128,128]{2,1,0:T(8,128)S(1)}, f32[1,128,128]{2,1,0:T(8,128)S(1)}, u32[]{:S(2)}, u32[]{:S(2)}) collective-permute-start(f32[1,128,128]{2,1,0:T(8,128)S(1)} %get-tuple-element.30.refs_3_), channel_id=1, source_target_pairs={{4,8},{8,4},{12,16},{16,12},{20,24},{24,20},{0,28},{28,0},{5,9},{9... | collective-permute-start | bytes 196616 | tf_op jit(solution)/shard_map/ppermute | solution.py:228
  23.0 2.6 %collective-permute-start.9 = (f32[8,128]{1,0:T(8,128)S(1)}, f32[8,128]{1,0:T(8,128)S(1)}, u32[]{:S(2)}, u32[]{:S(2)}) collective-permute-start(f32[8,128]{1,0:T(8,128)S(1)} %get-tuple-element.31), channel_id=1, source_target_pairs={{0,2},{1,3},{2,0},{3,1},{4,6},{5,7},{6,4},{7,5},{8,10},{9,11},{10,... | collective-permute-start | bytes 12296 | tf_op jit(solution)/shard_map/ppermute | solution.py:228
  25.6 1.9 %collective-permute-done.9 = f32[8,128]{1,0:T(8,128)S(1)} collective-permute-done((f32[8,128]{1,0:T(8,128)S(1)}, f32[8,128]{1,0:T(8,128)S(1)}, u32[]{:S(2)}, u32[]{:S(2)}) %collective-permute-start.9) | collective-permute-done | bytes 4128 | tf_op jit(solution)/shard_map/ppermute | solution.py:228
  27.6 1.2 %collective-permute-done.10 = f32[8,128]{1,0:T(8,128)S(1)} collective-permute-done((f32[8,128]{1,0:T(8,128)S(1)}, f32[8,128]{1,0:T(8,128)S(1)}, u32[]{:S(2)}, u32[]{:S(2)}) %collective-permute-start.10) | collective-permute-done | bytes 4128 | tf_op jit(solution)/shard_map/ppermute | solution.py:228
  28.7 1.6 %collective-permute-start.11 = (f32[8,128]{1,0:T(8,128)S(1)}, f32[8,128]{1,0:T(8,128)S(1)}, u32[]{:S(2)}, u32[]{:S(2)}) collective-permute-start(f32[8,128]{1,0:T(8,128)S(1)} %add.7.refs_0_), channel_id=1, source_target_pairs={{0,1},{1,0},{2,3},{3,2},{4,5},{5,4},{6,7},{7,6},{8,9},{9,8},{10,11... | collective-permute-start | bytes 12296 | tf_op jit(solution)/shard_map/ppermute | solution.py:228
  30.3 2.0 %collective-permute-done.11.refs_1_ = f32[8,128]{1,0:T(8,128)S(1)} collective-permute-done((f32[8,128]{1,0:T(8,128)S(1)}, f32[8,128]{1,0:T(8,128)S(1)}, u32[]{:S(2)}, u32[]{:S(2)}) %collective-permute-start.11) | collective-permute-done | bytes 4128 | tf_op jit(solution)/shard_map/ppermute | solution.py:228
  32.3 0.6 %mean.1 = f32[1,1]{1,0:T(1,128)} custom-call(f32[8,128]{1,0:T(8,128)S(1)} %add.7.refs_0_, f32[8,128]{1,0:T(8,128)S(1)} %collective-permute-done.11.refs_1_), custom_call_target="tpu_custom_call" | custom-call | tf_op jit(solution)/shard_map/mean/pallas_call | solution.py:523
  32.9 1.1 %grad.2.refs_6_ = f32[4,128,8,128]{3,2,1,0:T(8,128)} custom-call(f32[4,128,128]{2,1,0:T(8,128)S(1)} %get-tuple-element.27.gains, f32[8,3,31,16,128]{4,3,2,1,0:T(8,128)S(1)} %get-tuple-element.28.values), custom_call_target="tpu_custom_call" | custom-call | flops 2097152 | bytes 4194304 | tf_op jit(solution)/shard_map/grad/pallas_call | solution.py:493
  34.1 1.2 %grad.3 = f32[4,128,8,128]{3,2,1,0:T(8,128)} custom-call(f32[4,128,128]{2,1,0:T(8,128)S(1)} %get-tuple-element.27.gains, f32[8,3,31,16,128]{4,3,2,1,0:T(8,128)S(1)} %get-tuple-element.28.values, f32[4,128,128]{2,1,0:T(8,128)S(1)} %get-tuple-element.21.state.refs_0_, ...), custom_call_target="tpu_custom_call", output_to_operand_aliasing={{}: (8, {})} | custom-call | flops 2097152 | bytes 4194304 | tf_op jit(solution)/shard_map/grad/pallas_call | solution.py:493
  (22 shorter events, 0.3 us)
Async XLA Ops:
  0.6 6.2 %slice-start = ((s8[6291456]{0:T(1024)(128)(4,1)}), s8[4194304]{0:T(1024)(128)(4,1)S(1)}, s32[]{:S(2)}) async-start(s8[6291456]{0:T(1024)(128)(4,1)} %bitcast.15), calls=%async_computation | async-start | bytes 8388608
  0.6 5.2 %copy-start = (f32[32,16384]{1,0:T(8,128)S(1)}, f32[32,16384]{1,0:T(8,128)}, u32[]{:S(2)}) copy-start(f32[32,16384]{1,0:T(8,128)} %param.3) | copy-start | bytes 6291460
  0.6 6.2 %slice-start.1 = ((s8[6291456]{0:T(1024)(128)(4,1)}), s8[2097152]{0:T(1024)(128)(4,1)S(1)}, s32[]{:S(2)}) async-start(s8[6291456]{0:T(1024)(128)(4,1)} %bitcast.15), calls=%async_computation.1 | async-start | bytes 4194304
  1.7 6.6 %collective-permute-start = (f32[1,128,128]{2,1,0:T(8,128)S(1)}, f32[1,128,128]{2,1,0:T(8,128)S(1)}, u32[]{:S(2)}, u32[]{:S(2)}) collective-permute-start(f32[1,128,128]{2,1,0:T(8,128)S(1)} %get-tuple-element.17.own_core), channel_id=1, source_target_pairs={{0,4},{4,0},{8,12},{12,8},{16,20},{20,16},{24,28},{28,24},{1,5},{5... | collective-permute-start | bytes 196616 | tf_op jit(solution)/shard_map/ppermute | solution.py:228
  2.3 6.1 %collective-permute-start.1 = (f32[1,128,128]{2,1,0:T(8,128)S(1)}, f32[1,128,128]{2,1,0:T(8,128)S(1)}, u32[]{:S(2)}, u32[]{:S(2)}) collective-permute-start(f32[1,128,128]{2,1,0:T(8,128)S(1)} %get-tuple-element.18.own_chip), channel_id=1, source_target_pairs={{4,8},{8,4},{12,16},{16,12},{20,24},{24,20},{0,28},{28,0},{5,9},{9... | collective-permute-start | bytes 196616 | tf_op jit(solution)/shard_map/ppermute | solution.py:228
  6.9 6.6 %copy-start.1 = (f32[3,16384]{1,0:T(4,128)S(1)}, f32[3,16384]{1,0:T(4,128)}, u32[]{:S(2)}) copy-start(f32[3,16384]{1,0:T(4,128)} %param.5) | copy-start | bytes 589828
  8.5 1.4 %collective-permute-start.2 = (f32[4,64,128]{2,1,0:T(8,128)S(1)}, f32[4,64,128]{2,1,0:T(8,128)S(1)}, u32[]{:S(2)}, u32[]{:S(2)}) collective-permute-start(f32[4,64,128]{2,1,0:T(8,128)S(1)} %get-tuple-element.23), channel_id=1, source_target_pairs={{0,4},{4,0},{8,12},{12,8},{16,20},{20,16},{24,28},{28,24},{1,5},{5... | collective-permute-start | bytes 393224 | tf_op jit(solution)/shard_map/ppermute | solution.py:228
  10.0 7.0 %collective-permute-start.5 = (f32[4,64,128]{2,1,0:T(8,128)S(1)}, f32[4,64,128]{2,1,0:T(8,128)S(1)}, u32[]{:S(2)}, u32[]{:S(2)}) collective-permute-start(f32[4,64,128]{2,1,0:T(8,128)S(1)} %chip.1.refs_0_), channel_id=1, source_target_pairs={{24,0},{28,4},{16,8},{20,12},{8,16},{12,20},{0,24},{4,28},{25,1},{... | collective-permute-start | bytes 393224 | tf_op jit(solution)/shard_map/ppermute | solution.py:228
  12.1 7.2 %collective-permute-start.4 = (f32[4,64,128]{2,1,0:T(8,128)S(1)}, f32[4,64,128]{2,1,0:T(8,128)S(1)}, u32[]{:S(2)}, u32[]{:S(2)}) collective-permute-start(f32[4,64,128]{2,1,0:T(8,128)S(1)} %chip.1.refs_0_), channel_id=1, source_target_pairs={{16,0},{20,4},{24,8},{28,12},{0,16},{4,20},{8,24},{12,28},{17,1},{... | collective-permute-start | bytes 393224 | tf_op jit(solution)/shard_map/ppermute | solution.py:228
  12.8 6.5 %collective-permute-start.3 = (f32[4,64,128]{2,1,0:T(8,128)S(1)}, f32[4,64,128]{2,1,0:T(8,128)S(1)}, u32[]{:S(2)}, u32[]{:S(2)}) collective-permute-start(f32[4,64,128]{2,1,0:T(8,128)S(1)} %chip.1.refs_0_), channel_id=1, source_target_pairs={{8,0},{12,4},{0,8},{4,12},{24,16},{28,20},{16,24},{20,28},{9,1},{1... | collective-permute-start | bytes 393224 | tf_op jit(solution)/shard_map/ppermute | solution.py:228
  19.6 1.4 %collective-permute-start.6 = (f32[4,64,128]{2,1,0:T(8,128)S(1)}, f32[4,64,128]{2,1,0:T(8,128)S(1)}, u32[]{:S(2)}, u32[]{:S(2)}) collective-permute-start(f32[4,64,128]{2,1,0:T(8,128)S(1)} %get-tuple-element.25), channel_id=1, source_target_pairs={{0,4},{4,0},{8,12},{12,8},{16,20},{20,16},{24,28},{28,24},{1,5},{5... | collective-permute-start | bytes 393224 | tf_op jit(solution)/shard_map/ppermute | solution.py:228
  21.1 12.9 %collective-permute-start.7 = (f32[1,128,128]{2,1,0:T(8,128)S(1)}, f32[1,128,128]{2,1,0:T(8,128)S(1)}, u32[]{:S(2)}, u32[]{:S(2)}) collective-permute-start(f32[1,128,128]{2,1,0:T(8,128)S(1)} %get-tuple-element.29.refs_2_), channel_id=1, source_target_pairs={{0,4},{4,0},{8,12},{12,8},{16,20},{20,16},{24,28},{28,24},{1,5},{5... | collective-permute-start | bytes 196616 | tf_op jit(solution)/shard_map/ppermute | solution.py:228
  21.3 12.7 %collective-permute-start.8 = (f32[1,128,128]{2,1,0:T(8,128)S(1)}, f32[1,128,128]{2,1,0:T(8,128)S(1)}, u32[]{:S(2)}, u32[]{:S(2)}) collective-permute-start(f32[1,128,128]{2,1,0:T(8,128)S(1)} %get-tuple-element.30.refs_3_), channel_id=1, source_target_pairs={{4,8},{8,4},{12,16},{16,12},{20,24},{24,20},{0,28},{28,0},{5,9},{9... | collective-permute-start | bytes 196616 | tf_op jit(solution)/shard_map/ppermute | solution.py:228
  23.0 4.5 %collective-permute-start.9 = (f32[8,128]{1,0:T(8,128)S(1)}, f32[8,128]{1,0:T(8,128)S(1)}, u32[]{:S(2)}, u32[]{:S(2)}) collective-permute-start(f32[8,128]{1,0:T(8,128)S(1)} %get-tuple-element.31), channel_id=1, source_target_pairs={{0,2},{1,3},{2,0},{3,1},{4,6},{5,7},{6,4},{7,5},{8,10},{9,11},{10,... | collective-permute-start | bytes 12296 | tf_op jit(solution)/shard_map/ppermute | solution.py:228
  27.5 1.2 %collective-permute-start.10 = (f32[8,128]{1,0:T(8,128)S(1)}, f32[8,128]{1,0:T(8,128)S(1)}, u32[]{:S(2)}, u32[]{:S(2)}) collective-permute-start(f32[8,128]{1,0:T(8,128)S(1)} %add.6), channel_id=1, source_target_pairs={{0,4},{4,0},{8,12},{12,8},{16,20},{20,16},{24,28},{28,24},{1,5},{5... | collective-permute-start | bytes 12296 | tf_op jit(solution)/shard_map/ppermute | solution.py:228
  28.7 3.6 %collective-permute-start.11 = (f32[8,128]{1,0:T(8,128)S(1)}, f32[8,128]{1,0:T(8,128)S(1)}, u32[]{:S(2)}, u32[]{:S(2)}) collective-permute-start(f32[8,128]{1,0:T(8,128)S(1)} %add.7.refs_0_), channel_id=1, source_target_pairs={{0,1},{1,0},{2,3},{3,2},{4,5},{5,4},{6,7},{7,6},{8,9},{9,8},{10,11... | collective-permute-start | bytes 12296 | tf_op jit(solution)/shard_map/ppermute | solution.py:228

commit v6 on v5

--- a/solution.py
+++ b/solution.py
@@ -162,8 +162,8 @@
 
 
 def mean_kernel(scale, *refs):
-    total = sum(ref[0, 0] for ref in refs[:-1])
-    refs[-1][0, 0] = total * scale
+    total = sum(ref[:1, :1] for ref in refs[:-1])
+    refs[-1][...] = total * scale
 
 
 def grad_kernel(groups, gains, values, *refs):
@@ -299,23 +299,17 @@
         error = [0.5 * total[c] - target[c - 1, goal] for c in range(1, 4)]
         squares = error[0] * error[0] + error[1] * error[1] + error[2] * error[2]
         loss = squares if loss is None else loss + squares
-        for ahead, is_own in ((before, even), (behind, jnp.logical_not(even))):
+        for ahead, out in (
+            (chosen(even, before, behind), out_mine),
+            (chosen(even, behind, before), out_other),
+        ):
             gain = 0.5 * ahead[0]
-            values = [gain * error[c] for c in range(3)]
+            for c in range(3):
+                out[c, part] = gain * error[c]
             base = error[0] * (total[1] - ahead[1])
             for c in (1, 2):
                 base = base + error[c] * (total[1 + c] - ahead[1 + c])
-            values.append(base)
-
-            @pl.when(is_own)
-            def _():
-                for c in range(4):
-                    out_mine[c, part] = values[c]
-
-            @pl.when(jnp.logical_not(is_own))
-            def _():
-                for c in range(4):
-                    out_other[c, part] = values[c]
+            out[3, part] = base
 
     out_loss[...] = jnp.full(out_loss.shape, jnp.sum(loss), jnp.float32)
 
@@ -329,7 +323,7 @@
 
 def ring_sum(count):
     if count & (count - 1) == 0 and count > 1:
-        steps = [1 << bit for bit in reversed(range(count.bit_length() - 1))]
+        steps = [1 << bit for bit in range(count.bit_length() - 1)]
         return [[[(d, d ^ step) for d in range(count)]] for step in steps]
     return [[[(d, (d + k) % count) for d in range(count)] for k in range(1, count)]]
 
@@ -524,7 +518,7 @@
         functools.partial(mean_kernel, scale),
         out_shape=jax.ShapeDtypeStruct((1, 1), f32),
         in_specs=[whole] * len(squares),
-        out_specs=pl.BlockSpec(memory_space=pltpu.SMEM),
+        out_specs=whole,
         compiler_params=small,
         name="mean",
     )(*squares)

time: 35.4 us -> 35.3 us (level)
  no operation moved by 1% of the time
where the time goes in v6:
time: 35.3 us; the launch traced here: 35.1 us
  starting transfers between devices  13.9 us (39%)
  waiting for transfers between devices  13.5 us (38%)
  Pallas kernels  6.87 us (19%)
  between operations  0.79 us (2%)
    ppermute x12, starting transfers between devices, sent(): return lax.ppermute(value, axis, pairs)  13.9 us
    ppermute x12, waiting for transfers between devices, sent(): return lax.ppermute(value, axis, pairs)  13.5 us
    pallas_call x2, Pallas kernels, grad_part(): pl.pallas_call(functools.partial(grad_kernel, chosen_tiles), out_shape=ja...  2.32 us
    pallas_call x1, Pallas kernels, on_device(): pl.pallas_call(slab_kernel, out_shape=(jax.ShapeDtypeStruct((grid, 3, sam...  1.45 us
    pallas_call x1, Pallas kernels, on_device(): pl.pallas_call(edge_kernel, out_shape=(row, row), in_specs=[stays, stays]...  1.07 us
    pallas_call x1, Pallas kernels, on_device(): pl.pallas_call(opacity_kernel, out_shape=jax.ShapeDtypeStruct((grid, samp...  1.01 us
  transfers between devices with their start and end apart: 12, of which 7 were waited for; matrix products, arithmetic and copies ran while one was open for 0% of the time, Pallas kernels for 12%

profile of v6, /device:TPU:0, one launch (start us, length us, event | category | flops | bytes accessed | tf_op | source)
XLA Modules:
  0.0 35.1 jit_solution(17949197152609936519)
XLA Ops:
  0.7 1.1 %edge.1 = (f32[1,128,128]{2,1,0:T(8,128)S(1)}, f32[1,128,128]{2,1,0:T(8,128)S(1)}) custom-call(f32[4,128,8,128]{3,2,1,0:T(8,128)} %bitcast.18, f32[3,4,128,8,128]{4,3,2,1,0:T(8,128)} %bitcast.14), custom_call_target="tpu_custom_call" | custom-call | tf_op jit(solution)/shard_map/edge/pallas_call | solution.py:360
  1.7 0.6 %collective-permute-start = (f32[1,128,128]{2,1,0:T(8,128)S(1)}, f32[1,128,128]{2,1,0:T(8,128)S(1)}, u32[]{:S(2)}, u32[]{:S(2)}) collective-permute-start(f32[1,128,128]{2,1,0:T(8,128)S(1)} %get-tuple-element.17.own_core), channel_id=1, source_target_pairs={{0,4},{4,0},{8,12},{12,8},{16,20},{20,16},{24,28},{28,24},{1,5},{5... | collective-permute-start | bytes 196616 | tf_op jit(solution)/shard_map/ppermute | solution.py:228
  2.3 3.5 %collective-permute-start.1 = (f32[1,128,128]{2,1,0:T(8,128)S(1)}, f32[1,128,128]{2,1,0:T(8,128)S(1)}, u32[]{:S(2)}, u32[]{:S(2)}) collective-permute-start(f32[1,128,128]{2,1,0:T(8,128)S(1)} %get-tuple-element.18.own_chip), channel_id=1, source_target_pairs={{4,8},{8,4},{12,16},{16,12},{20,24},{24,20},{0,28},{28,0},{5,9},{9... | collective-permute-start | bytes 196616 | tf_op jit(solution)/shard_map/ppermute | solution.py:228
  5.8 1.0 %opacity.1.opacities = f32[8,31,16,128]{3,2,1,0:T(8,128)S(1)} custom-call(f32[4,128,8,128]{3,2,1,0:T(8,128)S(1)} %bitcast.19), custom_call_target="tpu_custom_call" | custom-call | flops 6291456 | bytes 4194304 | tf_op jit(solution)/shard_map/opacity/pallas_call | solution.py:374
  6.9 1.4 %slab.1 = (f32[8,3,31,16,128]{4,3,2,1,0:T(8,128)S(1)}, f32[4,128,128]{2,1,0:T(8,128)S(1)}, f32[3,128,128]{2,1,0:T(8,128)S(1)}, f32[3,128,128]{2,1,0:T(8,128)S(1)}) custom-call(f32[8,31,16,128]{3,2,1,0:T(8,128)S(1)} %opacity.1.opacities, f32[3,4,128,8,128]{4,3,2,1,0:T(8,128)S(1)} %bitcast.17), custom_call_target="tpu_custom_call" | custom-call | flops 14680064 | bytes 14680064 | tf_op jit(solution)/shard_map/slab/pallas_call | solution.py:387
  8.4 0.1 boundary.1
  8.6 1.3 %collective-permute-done.2.theirs = f32[4,64,128]{2,1,0:T(8,128)S(1)} collective-permute-done((f32[4,64,128]{2,1,0:T(8,128)S(1)}, f32[4,64,128]{2,1,0:T(8,128)S(1)}, u32[]{:S(2)}, u32[]{:S(2)}) %collective-permute-start.2) | collective-permute-done | bytes 131104 | tf_op jit(solution)/shard_map/ppermute | solution.py:228
  10.0 2.1 %collective-permute-start.5 = (f32[4,64,128]{2,1,0:T(8,128)S(1)}, f32[4,64,128]{2,1,0:T(8,128)S(1)}, u32[]{:S(2)}, u32[]{:S(2)}) collective-permute-start(f32[4,64,128]{2,1,0:T(8,128)S(1)} %chip.1.refs_0_), channel_id=1, source_target_pairs={{24,0},{28,4},{16,8},{20,12},{8,16},{12,20},{0,24},{4,28},{25,1},{... | collective-permute-start | bytes 393224 | tf_op jit(solution)/shard_map/ppermute | solution.py:228
  12.1 0.7 %collective-permute-start.4 = (f32[4,64,128]{2,1,0:T(8,128)S(1)}, f32[4,64,128]{2,1,0:T(8,128)S(1)}, u32[]{:S(2)}, u32[]{:S(2)}) collective-permute-start(f32[4,64,128]{2,1,0:T(8,128)S(1)} %chip.1.refs_0_), channel_id=1, source_target_pairs={{16,0},{20,4},{24,8},{28,12},{0,16},{4,20},{8,24},{12,28},{17,1},{... | collective-permute-start | bytes 393224 | tf_op jit(solution)/shard_map/ppermute | solution.py:228
  12.8 0.8 %collective-permute-start.3 = (f32[4,64,128]{2,1,0:T(8,128)S(1)}, f32[4,64,128]{2,1,0:T(8,128)S(1)}, u32[]{:S(2)}, u32[]{:S(2)}) collective-permute-start(f32[4,64,128]{2,1,0:T(8,128)S(1)} %chip.1.refs_0_), channel_id=1, source_target_pairs={{8,0},{12,4},{0,8},{4,12},{24,16},{28,20},{16,24},{20,28},{9,1},{1... | collective-permute-start | bytes 393224 | tf_op jit(solution)/shard_map/ppermute | solution.py:228
  13.5 3.4 %collective-permute-done.5.refs_3_ = f32[4,64,128]{2,1,0:T(8,128)S(1)} collective-permute-done((f32[4,64,128]{2,1,0:T(8,128)S(1)}, f32[4,64,128]{2,1,0:T(8,128)S(1)}, u32[]{:S(2)}, u32[]{:S(2)}) %collective-permute-start.5) | collective-permute-done | bytes 131104 | tf_op jit(solution)/shard_map/ppermute | solution.py:228
  17.0 2.3 %collective-permute-done.4.refs_2_ = f32[4,64,128]{2,1,0:T(8,128)S(1)} collective-permute-done((f32[4,64,128]{2,1,0:T(8,128)S(1)}, f32[4,64,128]{2,1,0:T(8,128)S(1)}, u32[]{:S(2)}, u32[]{:S(2)}) %collective-permute-start.4) | collective-permute-done | bytes 131104 | tf_op jit(solution)/shard_map/ppermute | solution.py:228
  19.3 0.3 scale.1
  19.7 1.3 %collective-permute-done.6.theirs = f32[4,64,128]{2,1,0:T(8,128)S(1)} collective-permute-done((f32[4,64,128]{2,1,0:T(8,128)S(1)}, f32[4,64,128]{2,1,0:T(8,128)S(1)}, u32[]{:S(2)}, u32[]{:S(2)}) %collective-permute-start.6) | collective-permute-done | bytes 131104 | tf_op jit(solution)/shard_map/ppermute | solution.py:228
  21.1 0.2 collective-permute-start.7
  21.3 1.7 %collective-permute-start.8 = (f32[1,128,128]{2,1,0:T(8,128)S(1)}, f32[1,128,128]{2,1,0:T(8,128)S(1)}, u32[]{:S(2)}, u32[]{:S(2)}) collective-permute-start(f32[1,128,128]{2,1,0:T(8,128)S(1)} %get-tuple-element.30.refs_3_), channel_id=1, source_target_pairs={{4,8},{8,4},{12,16},{16,12},{20,24},{24,20},{0,28},{28,0},{5,9},{9... | collective-permute-start | bytes 196616 | tf_op jit(solution)/shard_map/ppermute | solution.py:228
  23.0 1.6 %collective-permute-start.9 = (f32[8,128]{1,0:T(8,128)S(1)}, f32[8,128]{1,0:T(8,128)S(1)}, u32[]{:S(2)}, u32[]{:S(2)}) collective-permute-start(f32[8,128]{1,0:T(8,128)S(1)} %get-tuple-element.31), channel_id=1, source_target_pairs={{0,1},{1,0},{2,3},{3,2},{4,5},{5,4},{6,7},{7,6},{8,9},{9,8},{10,11... | collective-permute-start | bytes 12296 | tf_op jit(solution)/shard_map/ppermute | solution.py:228
  24.6 2.0 %collective-permute-done.9 = f32[8,128]{1,0:T(8,128)S(1)} collective-permute-done((f32[8,128]{1,0:T(8,128)S(1)}, f32[8,128]{1,0:T(8,128)S(1)}, u32[]{:S(2)}, u32[]{:S(2)}) %collective-permute-start.9) | collective-permute-done | bytes 4128 | tf_op jit(solution)/shard_map/ppermute | solution.py:228
  26.6 1.2 %collective-permute-done.10 = f32[8,128]{1,0:T(8,128)S(1)} collective-permute-done((f32[8,128]{1,0:T(8,128)S(1)}, f32[8,128]{1,0:T(8,128)S(1)}, u32[]{:S(2)}, u32[]{:S(2)}) %collective-permute-start.10) | collective-permute-done | bytes 4128 | tf_op jit(solution)/shard_map/ppermute | solution.py:228
  27.8 2.6 %collective-permute-start.11 = (f32[8,128]{1,0:T(8,128)S(1)}, f32[8,128]{1,0:T(8,128)S(1)}, u32[]{:S(2)}, u32[]{:S(2)}) collective-permute-start(f32[8,128]{1,0:T(8,128)S(1)} %add.7.refs_0_), channel_id=1, source_target_pairs={{0,2},{1,3},{2,0},{3,1},{4,6},{5,7},{6,4},{7,5},{8,10},{9,11},{10,... | collective-permute-start | bytes 12296 | tf_op jit(solution)/shard_map/ppermute | solution.py:228
  30.4 1.9 %collective-permute-done.11.refs_1_ = f32[8,128]{1,0:T(8,128)S(1)} collective-permute-done((f32[8,128]{1,0:T(8,128)S(1)}, f32[8,128]{1,0:T(8,128)S(1)}, u32[]{:S(2)}, u32[]{:S(2)}) %collective-permute-start.11) | collective-permute-done | bytes 4128 | tf_op jit(solution)/shard_map/ppermute | solution.py:228
  32.3 0.5 %mean.1 = f32[1,1]{1,0:T(1,128)} custom-call(f32[8,128]{1,0:T(8,128)S(1)} %add.7.refs_0_, f32[8,128]{1,0:T(8,128)S(1)} %collective-permute-done.11.refs_1_), custom_call_target="tpu_custom_call" | custom-call | tf_op jit(solution)/shard_map/mean/pallas_call | solution.py:517
  32.8 1.1 %grad.2.refs_6_ = f32[4,128,8,128]{3,2,1,0:T(8,128)} custom-call(f32[4,128,128]{2,1,0:T(8,128)S(1)} %get-tuple-element.27.gains, f32[8,3,31,16,128]{4,3,2,1,0:T(8,128)S(1)} %get-tuple-element.28.values), custom_call_target="tpu_custom_call" | custom-call | flops 2097152 | bytes 4194304 | tf_op jit(solution)/shard_map/grad/pallas_call | solution.py:487
  34.0 1.2 %grad.3 = f32[4,128,8,128]{3,2,1,0:T(8,128)} custom-call(f32[4,128,128]{2,1,0:T(8,128)S(1)} %get-tuple-element.27.gains, f32[8,3,31,16,128]{4,3,2,1,0:T(8,128)S(1)} %get-tuple-element.28.values, f32[4,128,128]{2,1,0:T(8,128)S(1)} %get-tuple-element.21.state.refs_0_, ...), custom_call_target="tpu_custom_call", output_to_operand_aliasing={{}: (8, {})} | custom-call | flops 2097152 | bytes 4194304 | tf_op jit(solution)/shard_map/grad/pallas_call | solution.py:487
  (22 shorter events, 0.3 us)
Async XLA Ops:
  0.6 6.2 %slice-start = ((s8[6291456]{0:T(1024)(128)(4,1)}), s8[4194304]{0:T(1024)(128)(4,1)S(1)}, s32[]{:S(2)}) async-start(s8[6291456]{0:T(1024)(128)(4,1)} %bitcast.15), calls=%async_computation | async-start | bytes 8388608
  0.6 5.2 %copy-start = (f32[32,16384]{1,0:T(8,128)S(1)}, f32[32,16384]{1,0:T(8,128)}, u32[]{:S(2)}) copy-start(f32[32,16384]{1,0:T(8,128)} %param.3) | copy-start | bytes 6291460
  0.6 6.2 %slice-start.1 = ((s8[6291456]{0:T(1024)(128)(4,1)}), s8[2097152]{0:T(1024)(128)(4,1)S(1)}, s32[]{:S(2)}) async-start(s8[6291456]{0:T(1024)(128)(4,1)} %bitcast.15), calls=%async_computation.1 | async-start | bytes 4194304
  1.7 6.6 %collective-permute-start = (f32[1,128,128]{2,1,0:T(8,128)S(1)}, f32[1,128,128]{2,1,0:T(8,128)S(1)}, u32[]{:S(2)}, u32[]{:S(2)}) collective-permute-start(f32[1,128,128]{2,1,0:T(8,128)S(1)} %get-tuple-element.17.own_core), channel_id=1, source_target_pairs={{0,4},{4,0},{8,12},{12,8},{16,20},{20,16},{24,28},{28,24},{1,5},{5... | collective-permute-start | bytes 196616 | tf_op jit(solution)/shard_map/ppermute | solution.py:228
  2.3 6.1 %collective-permute-start.1 = (f32[1,128,128]{2,1,0:T(8,128)S(1)}, f32[1,128,128]{2,1,0:T(8,128)S(1)}, u32[]{:S(2)}, u32[]{:S(2)}) collective-permute-start(f32[1,128,128]{2,1,0:T(8,128)S(1)} %get-tuple-element.18.own_chip), channel_id=1, source_target_pairs={{4,8},{8,4},{12,16},{16,12},{20,24},{24,20},{0,28},{28,0},{5,9},{9... | collective-permute-start | bytes 196616 | tf_op jit(solution)/shard_map/ppermute | solution.py:228
  6.9 6.6 %copy-start.1 = (f32[3,16384]{1,0:T(4,128)S(1)}, f32[3,16384]{1,0:T(4,128)}, u32[]{:S(2)}) copy-start(f32[3,16384]{1,0:T(4,128)} %param.5) | copy-start | bytes 589828
  8.5 1.4 %collective-permute-start.2 = (f32[4,64,128]{2,1,0:T(8,128)S(1)}, f32[4,64,128]{2,1,0:T(8,128)S(1)}, u32[]{:S(2)}, u32[]{:S(2)}) collective-permute-start(f32[4,64,128]{2,1,0:T(8,128)S(1)} %get-tuple-element.23), channel_id=1, source_target_pairs={{0,4},{4,0},{8,12},{12,8},{16,20},{20,16},{24,28},{28,24},{1,5},{5... | collective-permute-start | bytes 393224 | tf_op jit(solution)/shard_map/ppermute | solution.py:228
  10.0 7.0 %collective-permute-start.5 = (f32[4,64,128]{2,1,0:T(8,128)S(1)}, f32[4,64,128]{2,1,0:T(8,128)S(1)}, u32[]{:S(2)}, u32[]{:S(2)}) collective-permute-start(f32[4,64,128]{2,1,0:T(8,128)S(1)} %chip.1.refs_0_), channel_id=1, source_target_pairs={{24,0},{28,4},{16,8},{20,12},{8,16},{12,20},{0,24},{4,28},{25,1},{... | collective-permute-start | bytes 393224 | tf_op jit(solution)/shard_map/ppermute | solution.py:228
  12.1 7.2 %collective-permute-start.4 = (f32[4,64,128]{2,1,0:T(8,128)S(1)}, f32[4,64,128]{2,1,0:T(8,128)S(1)}, u32[]{:S(2)}, u32[]{:S(2)}) collective-permute-start(f32[4,64,128]{2,1,0:T(8,128)S(1)} %chip.1.refs_0_), channel_id=1, source_target_pairs={{16,0},{20,4},{24,8},{28,12},{0,16},{4,20},{8,24},{12,28},{17,1},{... | collective-permute-start | bytes 393224 | tf_op jit(solution)/shard_map/ppermute | solution.py:228
  12.8 6.5 %collective-permute-start.3 = (f32[4,64,128]{2,1,0:T(8,128)S(1)}, f32[4,64,128]{2,1,0:T(8,128)S(1)}, u32[]{:S(2)}, u32[]{:S(2)}) collective-permute-start(f32[4,64,128]{2,1,0:T(8,128)S(1)} %chip.1.refs_0_), channel_id=1, source_target_pairs={{8,0},{12,4},{0,8},{4,12},{24,16},{28,20},{16,24},{20,28},{9,1},{1... | collective-permute-start | bytes 393224 | tf_op jit(solution)/shard_map/ppermute | solution.py:228
  19.6 1.4 %collective-permute-start.6 = (f32[4,64,128]{2,1,0:T(8,128)S(1)}, f32[4,64,128]{2,1,0:T(8,128)S(1)}, u32[]{:S(2)}, u32[]{:S(2)}) collective-permute-start(f32[4,64,128]{2,1,0:T(8,128)S(1)} %get-tuple-element.25), channel_id=1, source_target_pairs={{0,4},{4,0},{8,12},{12,8},{16,20},{20,16},{24,28},{28,24},{1,5},{5... | collective-permute-start | bytes 393224 | tf_op jit(solution)/shard_map/ppermute | solution.py:228
  21.1 12.9 %collective-permute-start.7 = (f32[1,128,128]{2,1,0:T(8,128)S(1)}, f32[1,128,128]{2,1,0:T(8,128)S(1)}, u32[]{:S(2)}, u32[]{:S(2)}) collective-permute-start(f32[1,128,128]{2,1,0:T(8,128)S(1)} %get-tuple-element.29.refs_2_), channel_id=1, source_target_pairs={{0,4},{4,0},{8,12},{12,8},{16,20},{20,16},{24,28},{28,24},{1,5},{5... | collective-permute-start | bytes 196616 | tf_op jit(solution)/shard_map/ppermute | solution.py:228
  21.3 12.7 %collective-permute-start.8 = (f32[1,128,128]{2,1,0:T(8,128)S(1)}, f32[1,128,128]{2,1,0:T(8,128)S(1)}, u32[]{:S(2)}, u32[]{:S(2)}) collective-permute-start(f32[1,128,128]{2,1,0:T(8,128)S(1)} %get-tuple-element.30.refs_3_), channel_id=1, source_target_pairs={{4,8},{8,4},{12,16},{16,12},{20,24},{24,20},{0,28},{28,0},{5,9},{9... | collective-permute-start | bytes 196616 | tf_op jit(solution)/shard_map/ppermute | solution.py:228
  23.0 3.6 %collective-permute-start.9 = (f32[8,128]{1,0:T(8,128)S(1)}, f32[8,128]{1,0:T(8,128)S(1)}, u32[]{:S(2)}, u32[]{:S(2)}) collective-permute-start(f32[8,128]{1,0:T(8,128)S(1)} %get-tuple-element.31), channel_id=1, source_target_pairs={{0,1},{1,0},{2,3},{3,2},{4,5},{5,4},{6,7},{7,6},{8,9},{9,8},{10,11... | collective-permute-start | bytes 12296 | tf_op jit(solution)/shard_map/ppermute | solution.py:228
  26.6 1.2 %collective-permute-start.10 = (f32[8,128]{1,0:T(8,128)S(1)}, f32[8,128]{1,0:T(8,128)S(1)}, u32[]{:S(2)}, u32[]{:S(2)}) collective-permute-start(f32[8,128]{1,0:T(8,128)S(1)} %add.6), channel_id=1, source_target_pairs={{0,4},{4,0},{8,12},{12,8},{16,20},{20,16},{24,28},{28,24},{1,5},{5... | collective-permute-start | bytes 12296 | tf_op jit(solution)/shard_map/ppermute | solution.py:228
  27.8 4.5 %collective-permute-start.11 = (f32[8,128]{1,0:T(8,128)S(1)}, f32[8,128]{1,0:T(8,128)S(1)}, u32[]{:S(2)}, u32[]{:S(2)}) collective-permute-start(f32[8,128]{1,0:T(8,128)S(1)} %add.7.refs_0_), channel_id=1, source_target_pairs={{0,2},{1,3},{2,0},{3,1},{4,6},{5,7},{6,4},{7,5},{8,10},{9,11},{10,... | collective-permute-start | bytes 12296 | tf_op jit(solution)/shard_map/ppermute | solution.py:228

commit v7 on v6

--- a/solution.py
+++ b/solution.py
@@ -355,8 +355,15 @@
     states = jax.ShapeDtypeStruct((4, blocks, LANES), f32)
     whole = pl.BlockSpec(memory_space=pltpu.VMEM)
     stays = pl.BlockSpec(memory_space=pl.ANY)
-    chain = [p for d in range(1, devices - 1, 2) for p in ((d, d + 1), (d + 1, d))]
-    chain += [(0, devices - 1), (devices - 1, 0)]
+    tiles_of_rays = lax.axis_size("rays")
+    swaps = [p for d in range(1, devices - 1, 2) for p in ((d, d + 1), (d + 1, d))]
+    chain = [
+        (a * tiles_of_rays + z, b * tiles_of_rays + z) for a, b in swaps for z in range(tiles_of_rays)
+    ]
+    for end, far in ((0, devices - 1), (devices - 1, 0)):
+        for z in range(tiles_of_rays):
+            to, tile = (end, z ^ 1) if tiles_of_rays % 2 == 0 else (far, z)
+            chain.append((end * tiles_of_rays + z, to * tiles_of_rays + tile))
     core_cell, chip_cell = pl.pallas_call(
         edge_kernel,
         out_shape=(row, row),
@@ -366,7 +373,7 @@
         compiler_params=pltpu.CompilerParams(vmem_limit_bytes=EDGES),
         name="edge",
     )(density, radiance)
-    rim_chip = sent(chip_cell, "depth", chain)
+    rim_chip = sent(chip_cell, ("depth", "rays"), chain)
     rim_core = sent(core_cell, "depth", swap)
 
     step = BLOCKS
@@ -475,7 +482,7 @@
         compiler_params=small,
         name="ends",
     )(scale_mine, theirs, state, opacity, core_colors, chip_colors)
-    rim_end_chip = sent(chip_end, "depth", chain)
+    rim_end_chip = sent(chip_end, ("depth", "rays"), chain)
     rim_end_core = sent(core_end, "depth", swap)
 
     def grad_part(chosen_tiles, *extra):

time: 35.3 us -> 35.2 us (level)
  starting transfers between devices: 13.9 us -> 11.9 us
  waiting for transfers between devices: 13.5 us -> 15.4 us
    ppermute x12, starting transfers between devices: 13.9 us -> 11.9 us  [sent(): return lax.ppermute(value, axis, pairs)]
    ppermute x12, waiting for transfers between devices: 13.5 us -> 15.4 us  [sent(): return lax.ppermute(value, axis, pairs)]
  transfers between devices with their start and end apart: 12 -> 12, of which waited for: 7 -> 8; matrix products, arithmetic and copies ran while one was open for 0% -> 0% of each run, Pallas kernels for 12% -> 12%
where the time goes in v7:
time: 35.2 us; the launch traced here: 35 us
  waiting for transfers between devices  15.4 us (44%)
  starting transfers between devices  11.9 us (34%)
  Pallas kernels  6.87 us (20%)
  between operations  0.79 us (2%)
    ppermute x12, waiting for transfers between devices, sent(): return lax.ppermute(value, axis, pairs)  15.4 us
    ppermute x12, starting transfers between devices, sent(): return lax.ppermute(value, axis, pairs)  11.9 us
    pallas_call x2, Pallas kernels, grad_part(): pl.pallas_call(functools.partial(grad_kernel, chosen_tiles), out_shape=ja...  2.32 us
    pallas_call x1, Pallas kernels, on_device(): pl.pallas_call(slab_kernel, out_shape=(jax.ShapeDtypeStruct((grid, 3, sam...  1.45 us
    pallas_call x1, Pallas kernels, on_device(): pl.pallas_call(edge_kernel, out_shape=(row, row), in_specs=[stays, stays]...  1.07 us
    pallas_call x1, Pallas kernels, on_device(): pl.pallas_call(opacity_kernel, out_shape=jax.ShapeDtypeStruct((grid, samp...  1.01 us
  transfers between devices with their start and end apart: 12, of which 8 were waited for; matrix products, arithmetic and copies ran while one was open for 0% of the time, Pallas kernels for 12%

profile of v7, /device:TPU:0, one launch (start us, length us, event | category | flops | bytes accessed | tf_op | source)
XLA Modules:
  0.0 35.0 jit_solution(6463704411068545231)
XLA Ops:
  0.7 1.1 %edge.1 = (f32[1,128,128]{2,1,0:T(8,128)S(1)}, f32[1,128,128]{2,1,0:T(8,128)S(1)}) custom-call(f32[4,128,8,128]{3,2,1,0:T(8,128)} %bitcast.18, f32[3,4,128,8,128]{4,3,2,1,0:T(8,128)} %bitcast.14), custom_call_target="tpu_custom_call" | custom-call | tf_op jit(solution)/shard_map/edge/pallas_call | solution.py:367
  1.7 0.6 %collective-permute-start = (f32[1,128,128]{2,1,0:T(8,128)S(1)}, f32[1,128,128]{2,1,0:T(8,128)S(1)}, u32[]{:S(2)}, u32[]{:S(2)}) collective-permute-start(f32[1,128,128]{2,1,0:T(8,128)S(1)} %get-tuple-element.17.own_core), channel_id=1, source_target_pairs={{0,4},{4,0},{8,12},{12,8},{16,20},{20,16},{24,28},{28,24},{1,5},{5... | collective-permute-start | bytes 196616 | tf_op jit(solution)/shard_map/ppermute | solution.py:228
  2.3 2.6 %collective-permute-start.1 = (f32[1,128,128]{2,1,0:T(8,128)S(1)}, f32[1,128,128]{2,1,0:T(8,128)S(1)}, u32[]{:S(2)}, u32[]{:S(2)}) collective-permute-start(f32[1,128,128]{2,1,0:T(8,128)S(1)} %get-tuple-element.18.own_chip), channel_id=1, source_target_pairs={{4,8},{5,9},{6,10},{7,11},{8,4},{9,5},{10,6},{11,7},{12,16},{13,17... | collective-permute-start | bytes 196616 | tf_op jit(solution)/shard_map/ppermute | solution.py:228
  4.9 1.0 %opacity.1.opacities = f32[8,31,16,128]{3,2,1,0:T(8,128)S(1)} custom-call(f32[4,128,8,128]{3,2,1,0:T(8,128)S(1)} %bitcast.19), custom_call_target="tpu_custom_call" | custom-call | flops 6291456 | bytes 4194304 | tf_op jit(solution)/shard_map/opacity/pallas_call | solution.py:381
  6.0 1.4 %slab.1 = (f32[8,3,31,16,128]{4,3,2,1,0:T(8,128)S(1)}, f32[4,128,128]{2,1,0:T(8,128)S(1)}, f32[3,128,128]{2,1,0:T(8,128)S(1)}, f32[3,128,128]{2,1,0:T(8,128)S(1)}) custom-call(f32[8,31,16,128]{3,2,1,0:T(8,128)S(1)} %opacity.1.opacities, f32[3,4,128,8,128]{4,3,2,1,0:T(8,128)S(1)} %bitcast.17), custom_call_target="tpu_custom_call" | custom-call | flops 14680064 | bytes 14680064 | tf_op jit(solution)/shard_map/slab/pallas_call | solution.py:394
  7.5 0.1 boundary.1
  7.6 0.1 collective-permute-start.2
  7.7 1.3 %collective-permute-done.2.theirs = f32[4,64,128]{2,1,0:T(8,128)S(1)} collective-permute-done((f32[4,64,128]{2,1,0:T(8,128)S(1)}, f32[4,64,128]{2,1,0:T(8,128)S(1)}, u32[]{:S(2)}, u32[]{:S(2)}) %collective-permute-start.2) | collective-permute-done | bytes 131104 | tf_op jit(solution)/shard_map/ppermute | solution.py:228
  9.1 2.3 %collective-permute-start.5 = (f32[4,64,128]{2,1,0:T(8,128)S(1)}, f32[4,64,128]{2,1,0:T(8,128)S(1)}, u32[]{:S(2)}, u32[]{:S(2)}) collective-permute-start(f32[4,64,128]{2,1,0:T(8,128)S(1)} %chip.1.refs_0_), channel_id=1, source_target_pairs={{24,0},{28,4},{16,8},{20,12},{8,16},{12,20},{0,24},{4,28},{25,1},{... | collective-permute-start | bytes 393224 | tf_op jit(solution)/shard_map/ppermute | solution.py:228
  11.4 1.4 %collective-permute-start.4 = (f32[4,64,128]{2,1,0:T(8,128)S(1)}, f32[4,64,128]{2,1,0:T(8,128)S(1)}, u32[]{:S(2)}, u32[]{:S(2)}) collective-permute-start(f32[4,64,128]{2,1,0:T(8,128)S(1)} %chip.1.refs_0_), channel_id=1, source_target_pairs={{16,0},{20,4},{24,8},{28,12},{0,16},{4,20},{8,24},{12,28},{17,1},{... | collective-permute-start | bytes 393224 | tf_op jit(solution)/shard_map/ppermute | solution.py:228
  12.8 3.1 %collective-permute-done.5.refs_3_ = f32[4,64,128]{2,1,0:T(8,128)S(1)} collective-permute-done((f32[4,64,128]{2,1,0:T(8,128)S(1)}, f32[4,64,128]{2,1,0:T(8,128)S(1)}, u32[]{:S(2)}, u32[]{:S(2)}) %collective-permute-start.5) | collective-permute-done | bytes 131104 | tf_op jit(solution)/shard_map/ppermute | solution.py:228
  15.9 2.5 %collective-permute-done.4.refs_2_ = f32[4,64,128]{2,1,0:T(8,128)S(1)} collective-permute-done((f32[4,64,128]{2,1,0:T(8,128)S(1)}, f32[4,64,128]{2,1,0:T(8,128)S(1)}, u32[]{:S(2)}, u32[]{:S(2)}) %collective-permute-start.4) | collective-permute-done | bytes 131104 | tf_op jit(solution)/shard_map/ppermute | solution.py:228
  18.4 0.5 %collective-permute-done.3.refs_1_ = f32[4,64,128]{2,1,0:T(8,128)S(1)} collective-permute-done((f32[4,64,128]{2,1,0:T(8,128)S(1)}, f32[4,64,128]{2,1,0:T(8,128)S(1)}, u32[]{:S(2)}, u32[]{:S(2)}) %collective-permute-start.3) | collective-permute-done | bytes 131104 | tf_op jit(solution)/shard_map/ppermute | solution.py:228
  18.9 0.3 scale.1
  19.3 1.3 %collective-permute-done.6.theirs = f32[4,64,128]{2,1,0:T(8,128)S(1)} collective-permute-done((f32[4,64,128]{2,1,0:T(8,128)S(1)}, f32[4,64,128]{2,1,0:T(8,128)S(1)}, u32[]{:S(2)}, u32[]{:S(2)}) %collective-permute-start.6) | collective-permute-done | bytes 131104 | tf_op jit(solution)/shard_map/ppermute | solution.py:228
  20.7 0.2 collective-permute-start.7
  20.9 2.0 %collective-permute-start.8 = (f32[1,128,128]{2,1,0:T(8,128)S(1)}, f32[1,128,128]{2,1,0:T(8,128)S(1)}, u32[]{:S(2)}, u32[]{:S(2)}) collective-permute-start(f32[1,128,128]{2,1,0:T(8,128)S(1)} %get-tuple-element.30.refs_3_), channel_id=1, source_target_pairs={{4,8},{5,9},{6,10},{7,11},{8,4},{9,5},{10,6},{11,7},{12,16},{13,17... | collective-permute-start | bytes 196616 | tf_op jit(solution)/shard_map/ppermute | solution.py:228
  22.9 3.5 %collective-permute-done.9 = f32[8,128]{1,0:T(8,128)S(1)} collective-permute-done((f32[8,128]{1,0:T(8,128)S(1)}, f32[8,128]{1,0:T(8,128)S(1)}, u32[]{:S(2)}, u32[]{:S(2)}) %collective-permute-start.9) | collective-permute-done | bytes 4128 | tf_op jit(solution)/shard_map/ppermute | solution.py:228
  26.5 1.2 %collective-permute-done.10 = f32[8,128]{1,0:T(8,128)S(1)} collective-permute-done((f32[8,128]{1,0:T(8,128)S(1)}, f32[8,128]{1,0:T(8,128)S(1)}, u32[]{:S(2)}, u32[]{:S(2)}) %collective-permute-start.10) | collective-permute-done | bytes 4128 | tf_op jit(solution)/shard_map/ppermute | solution.py:228
  27.6 2.6 %collective-permute-start.11 = (f32[8,128]{1,0:T(8,128)S(1)}, f32[8,128]{1,0:T(8,128)S(1)}, u32[]{:S(2)}, u32[]{:S(2)}) collective-permute-start(f32[8,128]{1,0:T(8,128)S(1)} %add.7.refs_0_), channel_id=1, source_target_pairs={{0,2},{1,3},{2,0},{3,1},{4,6},{5,7},{6,4},{7,5},{8,10},{9,11},{10,... | collective-permute-start | bytes 12296 | tf_op jit(solution)/shard_map/ppermute | solution.py:228
  30.2 1.9 %collective-permute-done.11.refs_1_ = f32[8,128]{1,0:T(8,128)S(1)} collective-permute-done((f32[8,128]{1,0:T(8,128)S(1)}, f32[8,128]{1,0:T(8,128)S(1)}, u32[]{:S(2)}, u32[]{:S(2)}) %collective-permute-start.11) | collective-permute-done | bytes 4128 | tf_op jit(solution)/shard_map/ppermute | solution.py:228
  32.1 0.5 %mean.1 = f32[1,1]{1,0:T(1,128)} custom-call(f32[8,128]{1,0:T(8,128)S(1)} %add.7.refs_0_, f32[8,128]{1,0:T(8,128)S(1)} %collective-permute-done.11.refs_1_), custom_call_target="tpu_custom_call" | custom-call | tf_op jit(solution)/shard_map/mean/pallas_call | solution.py:524
  32.7 1.1 %grad.2.refs_6_ = f32[4,128,8,128]{3,2,1,0:T(8,128)} custom-call(f32[4,128,128]{2,1,0:T(8,128)S(1)} %get-tuple-element.27.gains, f32[8,3,31,16,128]{4,3,2,1,0:T(8,128)S(1)} %get-tuple-element.28.values), custom_call_target="tpu_custom_call" | custom-call | flops 2097152 | bytes 4194304 | tf_op jit(solution)/shard_map/grad/pallas_call | solution.py:494
  33.8 1.2 %grad.3 = f32[4,128,8,128]{3,2,1,0:T(8,128)} custom-call(f32[4,128,128]{2,1,0:T(8,128)S(1)} %get-tuple-element.27.gains, f32[8,3,31,16,128]{4,3,2,1,0:T(8,128)S(1)} %get-tuple-element.28.values, f32[4,128,128]{2,1,0:T(8,128)S(1)} %get-tuple-element.21.state.refs_0_, ...), custom_call_target="tpu_custom_call", output_to_operand_aliasing={{}: (8, {})} | custom-call | flops 2097152 | bytes 4194304 | tf_op jit(solution)/shard_map/grad/pallas_call | solution.py:494
  (22 shorter events, 0.3 us)
Async XLA Ops:
  0.6 5.3 %slice-start = ((s8[6291456]{0:T(1024)(128)(4,1)}), s8[4194304]{0:T(1024)(128)(4,1)S(1)}, s32[]{:S(2)}) async-start(s8[6291456]{0:T(1024)(128)(4,1)} %bitcast.15), calls=%async_computation | async-start | bytes 8388608
  0.6 4.3 %copy-start = (f32[32,16384]{1,0:T(8,128)S(1)}, f32[32,16384]{1,0:T(8,128)}, u32[]{:S(2)}) copy-start(f32[32,16384]{1,0:T(8,128)} %param.3) | copy-start | bytes 6291460
  0.6 5.3 %slice-start.1 = ((s8[6291456]{0:T(1024)(128)(4,1)}), s8[2097152]{0:T(1024)(128)(4,1)S(1)}, s32[]{:S(2)}) async-start(s8[6291456]{0:T(1024)(128)(4,1)} %bitcast.15), calls=%async_computation.1 | async-start | bytes 4194304
  1.7 5.7 %collective-permute-start = (f32[1,128,128]{2,1,0:T(8,128)S(1)}, f32[1,128,128]{2,1,0:T(8,128)S(1)}, u32[]{:S(2)}, u32[]{:S(2)}) collective-permute-start(f32[1,128,128]{2,1,0:T(8,128)S(1)} %get-tuple-element.17.own_core), channel_id=1, source_target_pairs={{0,4},{4,0},{8,12},{12,8},{16,20},{20,16},{24,28},{28,24},{1,5},{5... | collective-permute-start | bytes 196616 | tf_op jit(solution)/shard_map/ppermute | solution.py:228
  2.3 5.2 %collective-permute-start.1 = (f32[1,128,128]{2,1,0:T(8,128)S(1)}, f32[1,128,128]{2,1,0:T(8,128)S(1)}, u32[]{:S(2)}, u32[]{:S(2)}) collective-permute-start(f32[1,128,128]{2,1,0:T(8,128)S(1)} %get-tuple-element.18.own_chip), channel_id=1, source_target_pairs={{4,8},{5,9},{6,10},{7,11},{8,4},{9,5},{10,6},{11,7},{12,16},{13,17... | collective-permute-start | bytes 196616 | tf_op jit(solution)/shard_map/ppermute | solution.py:228
  6.0 6.8 %copy-start.1 = (f32[3,16384]{1,0:T(4,128)S(1)}, f32[3,16384]{1,0:T(4,128)}, u32[]{:S(2)}) copy-start(f32[3,16384]{1,0:T(4,128)} %param.5) | copy-start | bytes 589828
  7.6 1.4 %collective-permute-start.2 = (f32[4,64,128]{2,1,0:T(8,128)S(1)}, f32[4,64,128]{2,1,0:T(8,128)S(1)}, u32[]{:S(2)}, u32[]{:S(2)}) collective-permute-start(f32[4,64,128]{2,1,0:T(8,128)S(1)} %get-tuple-element.23), channel_id=1, source_target_pairs={{0,4},{4,0},{8,12},{12,8},{16,20},{20,16},{24,28},{28,24},{1,5},{5... | collective-permute-start | bytes 393224 | tf_op jit(solution)/shard_map/ppermute | solution.py:228
  9.1 6.9 %collective-permute-start.5 = (f32[4,64,128]{2,1,0:T(8,128)S(1)}, f32[4,64,128]{2,1,0:T(8,128)S(1)}, u32[]{:S(2)}, u32[]{:S(2)}) collective-permute-start(f32[4,64,128]{2,1,0:T(8,128)S(1)} %chip.1.refs_0_), channel_id=1, source_target_pairs={{24,0},{28,4},{16,8},{20,12},{8,16},{12,20},{0,24},{4,28},{25,1},{... | collective-permute-start | bytes 393224 | tf_op jit(solution)/shard_map/ppermute | solution.py:228
  11.4 7.0 %collective-permute-start.4 = (f32[4,64,128]{2,1,0:T(8,128)S(1)}, f32[4,64,128]{2,1,0:T(8,128)S(1)}, u32[]{:S(2)}, u32[]{:S(2)}) collective-permute-start(f32[4,64,128]{2,1,0:T(8,128)S(1)} %chip.1.refs_0_), channel_id=1, source_target_pairs={{16,0},{20,4},{24,8},{28,12},{0,16},{4,20},{8,24},{12,28},{17,1},{... | collective-permute-start | bytes 393224 | tf_op jit(solution)/shard_map/ppermute | solution.py:228
  12.8 6.1 %collective-permute-start.3 = (f32[4,64,128]{2,1,0:T(8,128)S(1)}, f32[4,64,128]{2,1,0:T(8,128)S(1)}, u32[]{:S(2)}, u32[]{:S(2)}) collective-permute-start(f32[4,64,128]{2,1,0:T(8,128)S(1)} %chip.1.refs_0_), channel_id=1, source_target_pairs={{8,0},{12,4},{0,8},{4,12},{24,16},{28,20},{16,24},{20,28},{9,1},{1... | collective-permute-start | bytes 393224 | tf_op jit(solution)/shard_map/ppermute | solution.py:228
  19.2 1.4 %collective-permute-start.6 = (f32[4,64,128]{2,1,0:T(8,128)S(1)}, f32[4,64,128]{2,1,0:T(8,128)S(1)}, u32[]{:S(2)}, u32[]{:S(2)}) collective-permute-start(f32[4,64,128]{2,1,0:T(8,128)S(1)} %get-tuple-element.25), channel_id=1, source_target_pairs={{0,4},{4,0},{8,12},{12,8},{16,20},{20,16},{24,28},{28,24},{1,5},{5... | collective-permute-start | bytes 393224 | tf_op jit(solution)/shard_map/ppermute | solution.py:228
  20.7 13.1 %collective-permute-start.7 = (f32[1,128,128]{2,1,0:T(8,128)S(1)}, f32[1,128,128]{2,1,0:T(8,128)S(1)}, u32[]{:S(2)}, u32[]{:S(2)}) collective-permute-start(f32[1,128,128]{2,1,0:T(8,128)S(1)} %get-tuple-element.29.refs_2_), channel_id=1, source_target_pairs={{0,4},{4,0},{8,12},{12,8},{16,20},{20,16},{24,28},{28,24},{1,5},{5... | collective-permute-start | bytes 196616 | tf_op jit(solution)/shard_map/ppermute | solution.py:228
  20.9 12.9 %collective-permute-start.8 = (f32[1,128,128]{2,1,0:T(8,128)S(1)}, f32[1,128,128]{2,1,0:T(8,128)S(1)}, u32[]{:S(2)}, u32[]{:S(2)}) collective-permute-start(f32[1,128,128]{2,1,0:T(8,128)S(1)} %get-tuple-element.30.refs_3_), channel_id=1, source_target_pairs={{4,8},{5,9},{6,10},{7,11},{8,4},{9,5},{10,6},{11,7},{12,16},{13,17... | collective-permute-start | bytes 196616 | tf_op jit(solution)/shard_map/ppermute | solution.py:228
  22.9 3.6 %collective-permute-start.9 = (f32[8,128]{1,0:T(8,128)S(1)}, f32[8,128]{1,0:T(8,128)S(1)}, u32[]{:S(2)}, u32[]{:S(2)}) collective-permute-start(f32[8,128]{1,0:T(8,128)S(1)} %get-tuple-element.31), channel_id=1, source_target_pairs={{0,1},{1,0},{2,3},{3,2},{4,5},{5,4},{6,7},{7,6},{8,9},{9,8},{10,11... | collective-permute-start | bytes 12296 | tf_op jit(solution)/shard_map/ppermute | solution.py:228
  26.5 1.2 %collective-permute-start.10 = (f32[8,128]{1,0:T(8,128)S(1)}, f32[8,128]{1,0:T(8,128)S(1)}, u32[]{:S(2)}, u32[]{:S(2)}) collective-permute-start(f32[8,128]{1,0:T(8,128)S(1)} %add.6), channel_id=1, source_target_pairs={{0,4},{4,0},{8,12},{12,8},{16,20},{20,16},{24,28},{28,24},{1,5},{5... | collective-permute-start | bytes 12296 | tf_op jit(solution)/shard_map/ppermute | solution.py:228
  27.6 4.5 %collective-permute-start.11 = (f32[8,128]{1,0:T(8,128)S(1)}, f32[8,128]{1,0:T(8,128)S(1)}, u32[]{:S(2)}, u32[]{:S(2)}) collective-permute-start(f32[8,128]{1,0:T(8,128)S(1)} %add.7.refs_0_), channel_id=1, source_target_pairs={{0,2},{1,3},{2,0},{3,1},{4,6},{5,7},{6,4},{7,5},{8,10},{9,11},{10,... | collective-permute-start | bytes 12296 | tf_op jit(solution)/shard_map/ppermute | solution.py:228
